TPU v7x, 256 devices: a whole 4x4x8 slice. The times are simulated.
256 devices in a mesh: ba: 64 (over z_hi, x, y, core), wa: 4 (over z_lo).
Axes of the slice: x: 4, y: 4, z: 8 (z_hi: 2, z_lo: 4; z = z_hi * 4 + z_lo), core: 2. Of those that a mesh axis runs over, the one named last changes fastest.
Arguments:
- sky_model: float32 [2, 2048, 2048], P(None, None, 'wa'), may hold values from -6 to 6
- plane_w: float32 [64], P('ba'), may hold values from -60 to 60
- kernel: float32 [16, 8], replicated, may hold values from -2 to 2
- tile_ids: int32 [4096], P(('ba', 'wa')), may hold values from 0 to 255, as said below
- plane_ids: int32 [4096, 1], P(('ba', 'wa')), may hold values from 0 to 63; in each aligned block of 16 rows (0 to 15, 16 to 31, ...) at most 2 rows name the same one
- positions: int32 [4096, 2, 512], P(('ba', 'wa')), may hold values from 0 to 1935
- observed: float32 [4096, 2, 512], P(('ba', 'wa')), may hold values from -6 to 6
Outputs:
- residual_vis: float32 [4096, 2, 512], P(('ba', 'wa'))
Inputs may be any that keep to these rules, and one draw needn't show every extreme that they name: `plane_ids`: among the 16 blocks of one device at most 2 name the same w-plane, and in every draw some device has a w-plane named by exactly 2 of its blocks. `tile_ids`: A tile id is row_tile * 16 + column_tile; the blocks held at index a of wa name column tiles a * 4 to (a + 1) * 4 - 1.
All inputs are finite; a program needn't handle non-finite values.
Results may differ from a plain program's by a relative error of at most 0.0003.
Values sent between devices are 32-bit elements; how exact they have to be, the bound alone decides.
No kernel may reach another device: no remote copies, remote signals or barrier semaphores. Data moves between devices by JAX's collectives and lax.ppermute only.
A program may use at most 128 MiB of HBM per device.

v0:
```python
import math

import jax
import jax.numpy as jnp
from jax import lax
from jax.sharding import PartitionSpec as P

TILE = 128


PRECISE = lax.Precision.HIGHEST
FIELD_WIDTH = 0.7


def cut_along(value, dim, size):
    before, after = (value.shape[:dim], value.shape[dim + 1 :])
    return jnp.moveaxis(value.reshape(*before, size, -1, *after), dim, 0)


def edges_of(length, count):
    turn = length // count
    if turn >= 8:
        turn -= turn % 8
    return [turn * k for k in range(1, count)]


def laid_out(blocks, dim):
    dims = list(blocks.shape[1:])
    dims[dim] *= blocks.shape[0]
    return jnp.moveaxis(blocks, 0, dim).reshape(dims)


def cut_exchange(value, axis, pieces, split_dim, concat_dim):
    blocks = cut_along(value, split_dim, lax.axis_size(axis))
    split_at = max(range(1, max(2, blocks.ndim - 1)), key=lambda d: blocks.shape[d])
    done = []
    for piece in jnp.split(blocks, edges_of(blocks.shape[split_at], pieces), axis=split_at):
        if piece.size:
            done.append(lax.all_to_all(piece, axis, split_axis=0, concat_axis=0, tiled=True))
    return laid_out(jnp.concatenate(done, axis=split_at), concat_dim)


def product(pattern, operand_a, operand_b):
    return jnp.einsum(pattern, operand_a, operand_b, precision=PRECISE)


def complex_product(pattern, table_pair, values):
    return (
        product(pattern, table_pair[0], values[0]) - product(pattern, table_pair[1], values[1]),
        product(pattern, table_pair[0], values[1]) + product(pattern, table_pair[1], values[0]),
    )


def phase_table(rows_count, cols_count, modulus):
    first_index = jnp.arange(rows_count, dtype=jnp.int32)[:, None]
    second_index = jnp.arange(cols_count, dtype=jnp.int32)[None, :]
    angle_rad = (first_index * second_index % modulus).astype(jnp.float32) * (
        -2.0 * math.pi / modulus
    )
    return (jnp.cos(angle_rad), jnp.sin(angle_rad))


def transform(values, pattern):
    length = values[0].shape[0]
    columns = values[0].shape[1]
    long_side = min(length, 128)
    short_side = length // long_side
    shaped = (
        values[0].reshape(long_side, short_side, columns),
        values[1].reshape(long_side, short_side, columns),
    )
    section_one = complex_product(
        "ab,anl->bnl", phase_table(long_side, long_side, long_side), shaped
    )
    twiddle = phase_table(long_side, short_side, length)
    twist_real = twiddle[0][:, :, None]
    twist_imag = twiddle[1][:, :, None]
    turned = (
        section_one[0] * twist_real - section_one[1] * twist_imag,
        section_one[0] * twist_imag + section_one[1] * twist_real,
    )
    return complex_product(
        "nk,bnl->" + pattern, phase_table(short_side, short_side, short_side), turned
    )


def kernel_rows(fine_position, kernel, tile_side):
    oversample, support = kernel.shape
    cell_index = fine_position // oversample
    offset_index = fine_position % oversample
    picker = (offset_index[..., None] == jnp.arange(oversample, dtype=jnp.int32)).astype(
        jnp.float32
    )
    kernel_taps = product("gso,ok->gsk", picker, kernel)
    tile_cells = jnp.arange(tile_side, dtype=jnp.int32)
    weights = jnp.zeros(fine_position.shape + (tile_side,), jnp.float32)
    for tap_step in range(support):
        weights = weights + jnp.where(
            tile_cells == cell_index[..., None] + tap_step,
            kernel_taps[..., tap_step : tap_step + 1],
            0.0,
        )
    return weights


def degrid(tiles, fine_position, kernel):
    tile_side = tiles.shape[-1]
    row_weights = kernel_rows(fine_position[:, 0], kernel, tile_side)
    col_weights = kernel_rows(fine_position[:, 1], kernel, tile_side)
    partial_value = product("gsu,gcuv->gcsv", row_weights, tiles)
    return jnp.sum(partial_value * col_weights[:, None], axis=-1)


def grouped(function, count, operands):
    group_size = math.gcd(count, 8)
    reshaped = tuple(
        (
            operand.reshape((count // group_size, group_size) + operand.shape[1:])
            for operand in operands
        )
    )

    def apply_group(group_items):
        return function(*group_items)

    result = lax.map(apply_group, reshaped)
    return result.reshape((count,) + result.shape[2:])


def shards(sky_model, plane_w, kernel, tile_ids, plane_ids, positions, observed):
    extent = sky_model.shape[1]
    column_count = sky_model.shape[2]
    slab_index = lax.axis_index("wa")
    spacing = FIELD_WIDTH / extent
    column_coord = (
        (slab_index * column_count + jnp.arange(column_count, dtype=jnp.int32)).astype(jnp.float32)
        - extent / 2
    ) * spacing
    row_coord = (jnp.arange(extent, dtype=jnp.int32).astype(jnp.float32) - extent / 2) * spacing
    radius_sq = row_coord[:, None] ** 2 + column_coord[None, :] ** 2
    lowered = -radius_sq / (1.0 + jnp.sqrt(1.0 - radius_sq))
    phase_angle = -2.0 * math.pi * plane_w[0] * lowered
    cosine = jnp.cos(phase_angle)
    sine_part = jnp.sin(phase_angle)
    image_real = sky_model[0] * cosine - sky_model[1] * sine_part
    image_imag = sky_model[0] * sine_part + sky_model[1] * cosine
    half_done = transform((image_real, image_imag), "lkb")
    stacked = jnp.stack(
        [half_done[0].reshape(column_count, extent), half_done[1].reshape(column_count, extent)]
    )
    exchanged = cut_exchange(stacked, "wa", 2, 2, 1)
    finished = transform((exchanged[0], exchanged[1]), "kbl")
    norm_factor = 1.0 / extent
    uv_grid = jnp.stack(
        [
            finished[0].reshape(extent, column_count) * norm_factor,
            finished[1].reshape(extent, column_count) * norm_factor,
        ]
    )
    plane_count = lax.axis_size("ba")
    block_count = tile_ids.shape[0]
    sample_count = positions.shape[2]
    capacity = max(2, block_count // plane_count)
    target = plane_ids[:, 0]
    onehot = (target[:, None] == jnp.arange(plane_count, dtype=jnp.int32)[None, :]).astype(
        jnp.int32
    )
    earlier = jnp.cumsum(onehot, axis=0) - onehot
    rank_in = jnp.sum(earlier * onehot, axis=1)
    slot_index = target * capacity + rank_in
    slot_tiles = jnp.zeros((plane_count * capacity,), jnp.int32).at[slot_index].set(tile_ids)
    slot_tiles = slot_tiles.reshape(plane_count, capacity)
    tile_side = TILE
    tiles_across = extent // tile_side
    local_across = column_count // tile_side

    def cut_tile(tile_number):
        row_tile = tile_number // tiles_across
        col_tile = tile_number % tiles_across - slab_index * local_across
        return lax.dynamic_slice(
            uv_grid,
            (jnp.int32(0), row_tile * tile_side, col_tile * tile_side),
            (2, tile_side, tile_side),
        )

    slot_fine = (
        jnp.zeros((plane_count * capacity, 2, sample_count), jnp.int32)
        .at[slot_index]
        .set(positions)
    )
    slot_fine = slot_fine.reshape(plane_count, capacity, 2, sample_count)
    asked_tiles = lax.all_to_all(slot_tiles, "ba", split_axis=0, concat_axis=0, tiled=True)
    asked_fine = lax.all_to_all(slot_fine, "ba", split_axis=0, concat_axis=0, tiled=True)
    count = asked_tiles.shape[0] * asked_tiles.shape[1]

    def slot_group(tile_group, fine_group):
        return degrid(jax.vmap(cut_tile)(tile_group), fine_group, kernel)

    values = grouped(
        slot_group, count, (asked_tiles.reshape(count), asked_fine.reshape(count, 2, sample_count))
    )
    values = values.reshape(asked_tiles.shape[0], asked_tiles.shape[1], 2, sample_count)
    answers = lax.all_to_all(values, "ba", split_axis=0, concat_axis=0, tiled=True)
    predicted = answers.reshape(plane_count * capacity, 2, sample_count)[slot_index]
    return observed - predicted


def solution(mesh):
    return jax.shard_map(
        shards,
        mesh=mesh,
        in_specs=(
            P(None, None, "wa"),
            P("ba"),
            P(),
            P(("ba", "wa")),
            P(("ba", "wa"), None),
            P(("ba", "wa"), None, None),
            P(("ba", "wa"), None, None),
        ),
        out_specs=P(("ba", "wa"), None, None),
        check_vma=False,
    )
```

profile of v0, /device:TPU:1, one launch (start us, length us, event | category | flops | bytes accessed | tf_op | source)
XLA Modules:
  0.0 1336.8 jit_solution(8696440338484649406)
XLA Ops:
  3.8 15.6 %all-to-all-start = ((s32[64,1,2]{2,1,0:T(1,128)}), s32[64,1,2]{2,1,0:T(1,128)S(1)}, u32[]{:S(2)}, u32[]{:S(2)}) async-start(s32[64,1,2]{2,1,0:T(1,128)} %bitcast.12), calls=%async_computation | async-start | bytes 65536 | tf_op jit(solution)/shard_map/all_to_all | solution.py:192
  19.5 7.7 fusion.227
  27.8 26.3 %fusion.105 = f32[128,16,512]{2,0,1:T(8,128)S(1)} fusion(f32[128,16,512]{2,1,0:T(8,128)} %bitcast.269, f32[128,16,512]{2,1,0:T(8,128)} %bitcast.265, f32[512]{0:T(512)S(1)} %multiply_multiply_fusion.1, f32[128,16]{0,1:T(8,128)S(1)} %get-tuple-element.232, f32[]{:T(128)} %bitcast.16), kind=kOutput, calls=%fused_computation.194 | convolution fusion | flops 1620279296 | bytes 12593156 | tf_op jit(solution)/shard_map/ab,anl->bnl/dot_general | solution.py:44
  54.1 23.4 %fusion.103 = f32[128,16,512]{2,0,1:T(8,128)S(1)} fusion(f32[128,16,512]{2,1,0:T(8,128)S(1)} %bitcast.270, f32[128,16,512]{2,1,0:T(8,128)S(1)} %bitcast.266, f32[512]{0:T(512)S(1)} %multiply_multiply_fusion.1, f32[128,16]{0,1:T(8,128)S(1)} %get-tuple-element.232, f32[]{:T(128)} %bitcast.16), kind=kOutput, calls=%fused_computation.192 | convolution fusion | flops 1620279296 | bytes 12593156 | tf_op jit(solution)/shard_map/ab,anl->bnl/dot_general | solution.py:44
  77.6 24.7 %convolution_subtract_fusion = f32[128,16,512]{2,0,1:T(8,128)} fusion(f32[128,16,512]{2,0,1:T(8,128)S(1)} %fusion.105, f32[128,16,512]{2,1,0:T(8,128)S(1)} %bitcast.271, f32[128,16,512]{2,1,0:T(8,128)S(1)} %bitcast.267, f32[512]{0:T(512)S(1)} %multiply_multiply_fusion.1, f32[128,16]{0,1:T(8,128)S(1)} %get-tuple-element.232, f32[]{:T(128)} %bitcast.16), kind=kOutput, calls=%fused_computation.177 | convolution fusion | flops 1621327872 | bytes 16787460 | tf_op jit(solution)/shard_map/ab,anl->bnl/dot_general | solution.py:44
  102.3 25.9 %multiply_subtract_fusion.1 = (f32[128,16,512]{2,0,1:T(8,128)S(1)}, f32[128,16,512]{2,0,1:T(8,128)S(1)}) fusion(f32[128,16,512]{2,0,1:T(8,128)} %convolution_subtract_fusion, f32[128,16]{0,1:T(8,128)S(1)} %get-tuple-element.233, f32[128,16]{0,1:T(8,128)S(1)} %fusion.142, f32[128,16,512]{2,0,1:T(8,128)S(1)} %fusion.103, f32[128,16,512]{2,1,0:T(8,128)S(1)} %bitcast.272, ...), kind=kOutput, calls=%fused_computation.147 | convolution fusion | flops 1627619328 | bytes 25192452 | tf_op jit(solution)/shard_map/ab,anl->bnl/dot_general | solution.py:44
  134.8 7.0 fusion.70
  141.9 7.1 subtract_bitcast_fusion
  151.4 7.2 add_bitcast_fusion
  176.0 88.4 %all-to-all-done.1 = f32[4,2,256,512]{2,3,1,0:T(8,128)} async-done(((f32[4,2,256,512]{2,3,1,0:T(8,128)}), f32[4,2,256,512]{2,3,1,0:T(8,128)}, u32[]{:S(2)}, u32[]{:S(2)}) %all-to-all-start.1) | async-done | bytes 4194336 | tf_op jit(solution)/shard_map/all_to_all | solution.py:39
  278.9 83.2 %all-to-all-done.2 = f32[4,2,256,512]{2,3,1,0:T(8,128)} async-done(((f32[4,2,256,512]{2,3,1,0:T(8,128)}), f32[4,2,256,512]{2,3,1,0:T(8,128)}, u32[]{:S(2)}, u32[]{:S(2)}) %all-to-all-start.2) | async-done | bytes 4194336 | tf_op jit(solution)/shard_map/all_to_all | solution.py:39
  362.1 13.9 %all-to-all-start.3 = ((s32[64,2,2,512]{3,2,1,0:T(2,128)}), s32[64,2,2,512]{3,2,1,0:T(2,128)S(1)}, u32[]{:S(2)}, u32[]{:S(2)}) async-start(s32[64,2,2,512]{3,2,1,0:T(2,128)} %bitcast.30), calls=%async_computation.3 | async-start | bytes 1048576 | tf_op jit(solution)/shard_map/all_to_all | solution.py:193
  406.1 7.5 multiply_subtract_fusion
  446.3 857.3 %while.16 = (s32[]{:T(128)}, f32[16,8,2,512]{3,2,1,0:T(2,128)}, s32[16,8]{1,0:T(8,128)S(1)}, s32[]{:T(128)}, f32[2,2048,512]{2,1,0:T(8,128)}, /*index=5*/s32[16,...) while((s32[]{:T(128)}, f32[16,8,2,512]{3,2,1,0:T(2,128)}, ...), condition=%wide.region_6.7_spmd, body=%wide.region_4.6_spmd.sunk | while | flops 1649795328 | bytes 12208282 | solution.py:126
  447.0 8.9 select_add_fusion.2
  458.3 23.7 %while.17 = (s32[]{:T(128)}, f32[2,2048,512]{2,1,0:T(8,128)}, s32[8,3]{0,1:T(4,128)S(1)}, f32[8,2,128,128]{3,2,1,0:T(8,128)S(1)}, s32[]{:T(128)}) while((s32[]{:T(128)}, f32[2,2048,512]{2,1,0:T(8,128)}, s32[8,3]{0,1:T(4,128)S(1)}, f32[8,2,128,128]{3,2,1,0:T(8,128)S(1)}, s32[]{:T(128)}) %tuple.108), condition=%wide.while_cond, body=%wide.while_body.sunk | while | flops 2 | bytes 262261 | solution.py:180
  482.0 17.5 %fusion.250 = f32[8,2,512]{2,1,0:T(2,128)S(1)} fusion(f32[8,2,128,128]{3,2,1,0:T(8,128)S(1)} %get-tuple-element.349, f32[8,512,128]{1,2,0:T(8,128)} %copy.215, f32[8,512]{1,0:T(8,128)S(1)} %bitcast.283, s32[8,512]{1,0:T(8,128)S(1)} %get-tuple-element.372, f32[8,512]{1,0:T(8,128)S(1)} %bitcast.284, s32[8,512]{1,0:T(8,128)S(1)} %get-tuple-element.374, ...), kind=kOutput, calls=%fused_computation.6.clone.2 | convolution fusion | flops 1624760320 | bytes 3440640 | tf_op jit(solution)/shard_map/while/body/eval_jaxpr/gsu,gcuv->gcsv/dot_general | solution.py:44
  500.6 8.9 select_add_fusion.2
  511.9 23.7 %while.17 = (s32[]{:T(128)}, f32[2,2048,512]{2,1,0:T(8,128)}, s32[8,3]{0,1:T(4,128)S(1)}, f32[8,2,128,128]{3,2,1,0:T(8,128)S(1)}, s32[]{:T(128)}) while((s32[]{:T(128)}, f32[2,2048,512]{2,1,0:T(8,128)}, s32[8,3]{0,1:T(4,128)S(1)}, f32[8,2,128,128]{3,2,1,0:T(8,128)S(1)}, s32[]{:T(128)}) %tuple.108), condition=%wide.while_cond, body=%wide.while_body.sunk | while | flops 2 | bytes 262261 | solution.py:180
  535.5 17.5 %fusion.250 = f32[8,2,512]{2,1,0:T(2,128)S(1)} fusion(f32[8,2,128,128]{3,2,1,0:T(8,128)S(1)} %get-tuple-element.349, f32[8,512,128]{1,2,0:T(8,128)} %copy.215, f32[8,512]{1,0:T(8,128)S(1)} %bitcast.283, s32[8,512]{1,0:T(8,128)S(1)} %get-tuple-element.372, f32[8,512]{1,0:T(8,128)S(1)} %bitcast.284, s32[8,512]{1,0:T(8,128)S(1)} %get-tuple-element.374, ...), kind=kOutput, calls=%fused_computation.6.clone.2 | convolution fusion | flops 1624760320 | bytes 3440640 | tf_op jit(solution)/shard_map/while/body/eval_jaxpr/gsu,gcuv->gcsv/dot_general | solution.py:44
  554.1 8.9 select_add_fusion.2
  565.5 23.6 %while.17 = (s32[]{:T(128)}, f32[2,2048,512]{2,1,0:T(8,128)}, s32[8,3]{0,1:T(4,128)S(1)}, f32[8,2,128,128]{3,2,1,0:T(8,128)S(1)}, s32[]{:T(128)}) while((s32[]{:T(128)}, f32[2,2048,512]{2,1,0:T(8,128)}, s32[8,3]{0,1:T(4,128)S(1)}, f32[8,2,128,128]{3,2,1,0:T(8,128)S(1)}, s32[]{:T(128)}) %tuple.108), condition=%wide.while_cond, body=%wide.while_body.sunk | while | flops 2 | bytes 262261 | solution.py:180
  589.1 17.5 %fusion.250 = f32[8,2,512]{2,1,0:T(2,128)S(1)} fusion(f32[8,2,128,128]{3,2,1,0:T(8,128)S(1)} %get-tuple-element.349, f32[8,512,128]{1,2,0:T(8,128)} %copy.215, f32[8,512]{1,0:T(8,128)S(1)} %bitcast.283, s32[8,512]{1,0:T(8,128)S(1)} %get-tuple-element.372, f32[8,512]{1,0:T(8,128)S(1)} %bitcast.284, s32[8,512]{1,0:T(8,128)S(1)} %get-tuple-element.374, ...), kind=kOutput, calls=%fused_computation.6.clone.2 | convolution fusion | flops 1624760320 | bytes 3440640 | tf_op jit(solution)/shard_map/while/body/eval_jaxpr/gsu,gcuv->gcsv/dot_general | solution.py:44
  607.7 8.9 select_add_fusion.2
  619.0 23.7 %while.17 = (s32[]{:T(128)}, f32[2,2048,512]{2,1,0:T(8,128)}, s32[8,3]{0,1:T(4,128)S(1)}, f32[8,2,128,128]{3,2,1,0:T(8,128)S(1)}, s32[]{:T(128)}) while((s32[]{:T(128)}, f32[2,2048,512]{2,1,0:T(8,128)}, s32[8,3]{0,1:T(4,128)S(1)}, f32[8,2,128,128]{3,2,1,0:T(8,128)S(1)}, s32[]{:T(128)}) %tuple.108), condition=%wide.while_cond, body=%wide.while_body.sunk | while | flops 2 | bytes 262261 | solution.py:180
  642.7 17.5 %fusion.250 = f32[8,2,512]{2,1,0:T(2,128)S(1)} fusion(f32[8,2,128,128]{3,2,1,0:T(8,128)S(1)} %get-tuple-element.349, f32[8,512,128]{1,2,0:T(8,128)} %copy.215, f32[8,512]{1,0:T(8,128)S(1)} %bitcast.283, s32[8,512]{1,0:T(8,128)S(1)} %get-tuple-element.372, f32[8,512]{1,0:T(8,128)S(1)} %bitcast.284, s32[8,512]{1,0:T(8,128)S(1)} %get-tuple-element.374, ...), kind=kOutput, calls=%fused_computation.6.clone.2 | convolution fusion | flops 1624760320 | bytes 3440640 | tf_op jit(solution)/shard_map/while/body/eval_jaxpr/gsu,gcuv->gcsv/dot_general | solution.py:44
  661.2 8.9 select_add_fusion.2
  672.6 23.6 %while.17 = (s32[]{:T(128)}, f32[2,2048,512]{2,1,0:T(8,128)}, s32[8,3]{0,1:T(4,128)S(1)}, f32[8,2,128,128]{3,2,1,0:T(8,128)S(1)}, s32[]{:T(128)}) while((s32[]{:T(128)}, f32[2,2048,512]{2,1,0:T(8,128)}, s32[8,3]{0,1:T(4,128)S(1)}, f32[8,2,128,128]{3,2,1,0:T(8,128)S(1)}, s32[]{:T(128)}) %tuple.108), condition=%wide.while_cond, body=%wide.while_body.sunk | while | flops 2 | bytes 262261 | solution.py:180
  696.2 17.5 %fusion.250 = f32[8,2,512]{2,1,0:T(2,128)S(1)} fusion(f32[8,2,128,128]{3,2,1,0:T(8,128)S(1)} %get-tuple-element.349, f32[8,512,128]{1,2,0:T(8,128)} %copy.215, f32[8,512]{1,0:T(8,128)S(1)} %bitcast.283, s32[8,512]{1,0:T(8,128)S(1)} %get-tuple-element.372, f32[8,512]{1,0:T(8,128)S(1)} %bitcast.284, s32[8,512]{1,0:T(8,128)S(1)} %get-tuple-element.374, ...), kind=kOutput, calls=%fused_computation.6.clone.2 | convolution fusion | flops 1624760320 | bytes 3440640 | tf_op jit(solution)/shard_map/while/body/eval_jaxpr/gsu,gcuv->gcsv/dot_general | solution.py:44
  714.8 8.9 select_add_fusion.2
  726.1 23.7 %while.17 = (s32[]{:T(128)}, f32[2,2048,512]{2,1,0:T(8,128)}, s32[8,3]{0,1:T(4,128)S(1)}, f32[8,2,128,128]{3,2,1,0:T(8,128)S(1)}, s32[]{:T(128)}) while((s32[]{:T(128)}, f32[2,2048,512]{2,1,0:T(8,128)}, s32[8,3]{0,1:T(4,128)S(1)}, f32[8,2,128,128]{3,2,1,0:T(8,128)S(1)}, s32[]{:T(128)}) %tuple.108), condition=%wide.while_cond, body=%wide.while_body.sunk | while | flops 2 | bytes 262261 | solution.py:180
  749.8 17.5 %fusion.250 = f32[8,2,512]{2,1,0:T(2,128)S(1)} fusion(f32[8,2,128,128]{3,2,1,0:T(8,128)S(1)} %get-tuple-element.349, f32[8,512,128]{1,2,0:T(8,128)} %copy.215, f32[8,512]{1,0:T(8,128)S(1)} %bitcast.283, s32[8,512]{1,0:T(8,128)S(1)} %get-tuple-element.372, f32[8,512]{1,0:T(8,128)S(1)} %bitcast.284, s32[8,512]{1,0:T(8,128)S(1)} %get-tuple-element.374, ...), kind=kOutput, calls=%fused_computation.6.clone.2 | convolution fusion | flops 1624760320 | bytes 3440640 | tf_op jit(solution)/shard_map/while/body/eval_jaxpr/gsu,gcuv->gcsv/dot_general | solution.py:44
  768.3 8.9 select_add_fusion.2
  779.7 23.6 %while.17 = (s32[]{:T(128)}, f32[2,2048,512]{2,1,0:T(8,128)}, s32[8,3]{0,1:T(4,128)S(1)}, f32[8,2,128,128]{3,2,1,0:T(8,128)S(1)}, s32[]{:T(128)}) while((s32[]{:T(128)}, f32[2,2048,512]{2,1,0:T(8,128)}, s32[8,3]{0,1:T(4,128)S(1)}, f32[8,2,128,128]{3,2,1,0:T(8,128)S(1)}, s32[]{:T(128)}) %tuple.108), condition=%wide.while_cond, body=%wide.while_body.sunk | while | flops 2 | bytes 262261 | solution.py:180
  803.3 17.5 %fusion.250 = f32[8,2,512]{2,1,0:T(2,128)S(1)} fusion(f32[8,2,128,128]{3,2,1,0:T(8,128)S(1)} %get-tuple-element.349, f32[8,512,128]{1,2,0:T(8,128)} %copy.215, f32[8,512]{1,0:T(8,128)S(1)} %bitcast.283, s32[8,512]{1,0:T(8,128)S(1)} %get-tuple-element.372, f32[8,512]{1,0:T(8,128)S(1)} %bitcast.284, s32[8,512]{1,0:T(8,128)S(1)} %get-tuple-element.374, ...), kind=kOutput, calls=%fused_computation.6.clone.2 | convolution fusion | flops 1624760320 | bytes 3440640 | tf_op jit(solution)/shard_map/while/body/eval_jaxpr/gsu,gcuv->gcsv/dot_general | solution.py:44
  821.9 8.9 select_add_fusion.2
  833.2 23.7 %while.17 = (s32[]{:T(128)}, f32[2,2048,512]{2,1,0:T(8,128)}, s32[8,3]{0,1:T(4,128)S(1)}, f32[8,2,128,128]{3,2,1,0:T(8,128)S(1)}, s32[]{:T(128)}) while((s32[]{:T(128)}, f32[2,2048,512]{2,1,0:T(8,128)}, s32[8,3]{0,1:T(4,128)S(1)}, f32[8,2,128,128]{3,2,1,0:T(8,128)S(1)}, s32[]{:T(128)}) %tuple.108), condition=%wide.while_cond, body=%wide.while_body.sunk | while | flops 2 | bytes 262261 | solution.py:180
  856.9 17.5 %fusion.250 = f32[8,2,512]{2,1,0:T(2,128)S(1)} fusion(f32[8,2,128,128]{3,2,1,0:T(8,128)S(1)} %get-tuple-element.349, f32[8,512,128]{1,2,0:T(8,128)} %copy.215, f32[8,512]{1,0:T(8,128)S(1)} %bitcast.283, s32[8,512]{1,0:T(8,128)S(1)} %get-tuple-element.372, f32[8,512]{1,0:T(8,128)S(1)} %bitcast.284, s32[8,512]{1,0:T(8,128)S(1)} %get-tuple-element.374, ...), kind=kOutput, calls=%fused_computation.6.clone.2 | convolution fusion | flops 1624760320 | bytes 3440640 | tf_op jit(solution)/shard_map/while/body/eval_jaxpr/gsu,gcuv->gcsv/dot_general | solution.py:44
  875.4 8.9 select_add_fusion.2
  886.8 23.7 %while.17 = (s32[]{:T(128)}, f32[2,2048,512]{2,1,0:T(8,128)}, s32[8,3]{0,1:T(4,128)S(1)}, f32[8,2,128,128]{3,2,1,0:T(8,128)S(1)}, s32[]{:T(128)}) while((s32[]{:T(128)}, f32[2,2048,512]{2,1,0:T(8,128)}, s32[8,3]{0,1:T(4,128)S(1)}, f32[8,2,128,128]{3,2,1,0:T(8,128)S(1)}, s32[]{:T(128)}) %tuple.108), condition=%wide.while_cond, body=%wide.while_body.sunk | while | flops 2 | bytes 262261 | solution.py:180
  910.4 17.5 %fusion.250 = f32[8,2,512]{2,1,0:T(2,128)S(1)} fusion(f32[8,2,128,128]{3,2,1,0:T(8,128)S(1)} %get-tuple-element.349, f32[8,512,128]{1,2,0:T(8,128)} %copy.215, f32[8,512]{1,0:T(8,128)S(1)} %bitcast.283, s32[8,512]{1,0:T(8,128)S(1)} %get-tuple-element.372, f32[8,512]{1,0:T(8,128)S(1)} %bitcast.284, s32[8,512]{1,0:T(8,128)S(1)} %get-tuple-element.374, ...), kind=kOutput, calls=%fused_computation.6.clone.2 | convolution fusion | flops 1624760320 | bytes 3440640 | tf_op jit(solution)/shard_map/while/body/eval_jaxpr/gsu,gcuv->gcsv/dot_general | solution.py:44
  929.0 8.9 select_add_fusion.2
  940.3 23.7 %while.17 = (s32[]{:T(128)}, f32[2,2048,512]{2,1,0:T(8,128)}, s32[8,3]{0,1:T(4,128)S(1)}, f32[8,2,128,128]{3,2,1,0:T(8,128)S(1)}, s32[]{:T(128)}) while((s32[]{:T(128)}, f32[2,2048,512]{2,1,0:T(8,128)}, s32[8,3]{0,1:T(4,128)S(1)}, f32[8,2,128,128]{3,2,1,0:T(8,128)S(1)}, s32[]{:T(128)}) %tuple.108), condition=%wide.while_cond, body=%wide.while_body.sunk | while | flops 2 | bytes 262261 | solution.py:180
  964.0 17.5 %fusion.250 = f32[8,2,512]{2,1,0:T(2,128)S(1)} fusion(f32[8,2,128,128]{3,2,1,0:T(8,128)S(1)} %get-tuple-element.349, f32[8,512,128]{1,2,0:T(8,128)} %copy.215, f32[8,512]{1,0:T(8,128)S(1)} %bitcast.283, s32[8,512]{1,0:T(8,128)S(1)} %get-tuple-element.372, f32[8,512]{1,0:T(8,128)S(1)} %bitcast.284, s32[8,512]{1,0:T(8,128)S(1)} %get-tuple-element.374, ...), kind=kOutput, calls=%fused_computation.6.clone.2 | convolution fusion | flops 1624760320 | bytes 3440640 | tf_op jit(solution)/shard_map/while/body/eval_jaxpr/gsu,gcuv->gcsv/dot_general | solution.py:44
  982.6 8.9 select_add_fusion.2
  993.9 23.7 %while.17 = (s32[]{:T(128)}, f32[2,2048,512]{2,1,0:T(8,128)}, s32[8,3]{0,1:T(4,128)S(1)}, f32[8,2,128,128]{3,2,1,0:T(8,128)S(1)}, s32[]{:T(128)}) while((s32[]{:T(128)}, f32[2,2048,512]{2,1,0:T(8,128)}, s32[8,3]{0,1:T(4,128)S(1)}, f32[8,2,128,128]{3,2,1,0:T(8,128)S(1)}, s32[]{:T(128)}) %tuple.108), condition=%wide.while_cond, body=%wide.while_body.sunk | while | flops 2 | bytes 262261 | solution.py:180
  1017.6 17.5 %fusion.250 = f32[8,2,512]{2,1,0:T(2,128)S(1)} fusion(f32[8,2,128,128]{3,2,1,0:T(8,128)S(1)} %get-tuple-element.349, f32[8,512,128]{1,2,0:T(8,128)} %copy.215, f32[8,512]{1,0:T(8,128)S(1)} %bitcast.283, s32[8,512]{1,0:T(8,128)S(1)} %get-tuple-element.372, f32[8,512]{1,0:T(8,128)S(1)} %bitcast.284, s32[8,512]{1,0:T(8,128)S(1)} %get-tuple-element.374, ...), kind=kOutput, calls=%fused_computation.6.clone.2 | convolution fusion | flops 1624760320 | bytes 3440640 | tf_op jit(solution)/shard_map/while/body/eval_jaxpr/gsu,gcuv->gcsv/dot_general | solution.py:44
  1036.2 8.9 select_add_fusion.2
  1047.5 23.7 %while.17 = (s32[]{:T(128)}, f32[2,2048,512]{2,1,0:T(8,128)}, s32[8,3]{0,1:T(4,128)S(1)}, f32[8,2,128,128]{3,2,1,0:T(8,128)S(1)}, s32[]{:T(128)}) while((s32[]{:T(128)}, f32[2,2048,512]{2,1,0:T(8,128)}, s32[8,3]{0,1:T(4,128)S(1)}, f32[8,2,128,128]{3,2,1,0:T(8,128)S(1)}, s32[]{:T(128)}) %tuple.108), condition=%wide.while_cond, body=%wide.while_body.sunk | while | flops 2 | bytes 262261 | solution.py:180
  1071.2 17.5 %fusion.250 = f32[8,2,512]{2,1,0:T(2,128)S(1)} fusion(f32[8,2,128,128]{3,2,1,0:T(8,128)S(1)} %get-tuple-element.349, f32[8,512,128]{1,2,0:T(8,128)} %copy.215, f32[8,512]{1,0:T(8,128)S(1)} %bitcast.283, s32[8,512]{1,0:T(8,128)S(1)} %get-tuple-element.372, f32[8,512]{1,0:T(8,128)S(1)} %bitcast.284, s32[8,512]{1,0:T(8,128)S(1)} %get-tuple-element.374, ...), kind=kOutput, calls=%fused_computation.6.clone.2 | convolution fusion | flops 1624760320 | bytes 3440640 | tf_op jit(solution)/shard_map/while/body/eval_jaxpr/gsu,gcuv->gcsv/dot_general | solution.py:44
  1089.8 8.9 select_add_fusion.2
  1101.1 23.7 %while.17 = (s32[]{:T(128)}, f32[2,2048,512]{2,1,0:T(8,128)}, s32[8,3]{0,1:T(4,128)S(1)}, f32[8,2,128,128]{3,2,1,0:T(8,128)S(1)}, s32[]{:T(128)}) while((s32[]{:T(128)}, f32[2,2048,512]{2,1,0:T(8,128)}, s32[8,3]{0,1:T(4,128)S(1)}, f32[8,2,128,128]{3,2,1,0:T(8,128)S(1)}, s32[]{:T(128)}) %tuple.108), condition=%wide.while_cond, body=%wide.while_body.sunk | while | flops 2 | bytes 262261 | solution.py:180
  1124.7 17.5 %fusion.250 = f32[8,2,512]{2,1,0:T(2,128)S(1)} fusion(f32[8,2,128,128]{3,2,1,0:T(8,128)S(1)} %get-tuple-element.349, f32[8,512,128]{1,2,0:T(8,128)} %copy.215, f32[8,512]{1,0:T(8,128)S(1)} %bitcast.283, s32[8,512]{1,0:T(8,128)S(1)} %get-tuple-element.372, f32[8,512]{1,0:T(8,128)S(1)} %bitcast.284, s32[8,512]{1,0:T(8,128)S(1)} %get-tuple-element.374, ...), kind=kOutput, calls=%fused_computation.6.clone.2 | convolution fusion | flops 1624760320 | bytes 3440640 | tf_op jit(solution)/shard_map/while/body/eval_jaxpr/gsu,gcuv->gcsv/dot_general | solution.py:44
  1143.3 8.9 select_add_fusion.2
  1154.7 23.7 %while.17 = (s32[]{:T(128)}, f32[2,2048,512]{2,1,0:T(8,128)}, s32[8,3]{0,1:T(4,128)S(1)}, f32[8,2,128,128]{3,2,1,0:T(8,128)S(1)}, s32[]{:T(128)}) while((s32[]{:T(128)}, f32[2,2048,512]{2,1,0:T(8,128)}, s32[8,3]{0,1:T(4,128)S(1)}, f32[8,2,128,128]{3,2,1,0:T(8,128)S(1)}, s32[]{:T(128)}) %tuple.108), condition=%wide.while_cond, body=%wide.while_body.sunk | while | flops 2 | bytes 262261 | solution.py:180
  1178.3 17.5 %fusion.250 = f32[8,2,512]{2,1,0:T(2,128)S(1)} fusion(f32[8,2,128,128]{3,2,1,0:T(8,128)S(1)} %get-tuple-element.349, f32[8,512,128]{1,2,0:T(8,128)} %copy.215, f32[8,512]{1,0:T(8,128)S(1)} %bitcast.283, s32[8,512]{1,0:T(8,128)S(1)} %get-tuple-element.372, f32[8,512]{1,0:T(8,128)S(1)} %bitcast.284, s32[8,512]{1,0:T(8,128)S(1)} %get-tuple-element.374, ...), kind=kOutput, calls=%fused_computation.6.clone.2 | convolution fusion | flops 1624760320 | bytes 3440640 | tf_op jit(solution)/shard_map/while/body/eval_jaxpr/gsu,gcuv->gcsv/dot_general | solution.py:44
  1196.9 8.9 select_add_fusion.2
  1208.2 23.7 %while.17 = (s32[]{:T(128)}, f32[2,2048,512]{2,1,0:T(8,128)}, s32[8,3]{0,1:T(4,128)S(1)}, f32[8,2,128,128]{3,2,1,0:T(8,128)S(1)}, s32[]{:T(128)}) while((s32[]{:T(128)}, f32[2,2048,512]{2,1,0:T(8,128)}, s32[8,3]{0,1:T(4,128)S(1)}, f32[8,2,128,128]{3,2,1,0:T(8,128)S(1)}, s32[]{:T(128)}) %tuple.108), condition=%wide.while_cond, body=%wide.while_body.sunk | while | flops 2 | bytes 262261 | solution.py:180
  1231.9 17.5 %fusion.250 = f32[8,2,512]{2,1,0:T(2,128)S(1)} fusion(f32[8,2,128,128]{3,2,1,0:T(8,128)S(1)} %get-tuple-element.349, f32[8,512,128]{1,2,0:T(8,128)} %copy.215, f32[8,512]{1,0:T(8,128)S(1)} %bitcast.283, s32[8,512]{1,0:T(8,128)S(1)} %get-tuple-element.372, f32[8,512]{1,0:T(8,128)S(1)} %bitcast.284, s32[8,512]{1,0:T(8,128)S(1)} %get-tuple-element.374, ...), kind=kOutput, calls=%fused_computation.6.clone.2 | convolution fusion | flops 1624760320 | bytes 3440640 | tf_op jit(solution)/shard_map/while/body/eval_jaxpr/gsu,gcuv->gcsv/dot_general | solution.py:44
  1250.5 8.9 select_add_fusion.2
  1261.8 23.7 %while.17 = (s32[]{:T(128)}, f32[2,2048,512]{2,1,0:T(8,128)}, s32[8,3]{0,1:T(4,128)S(1)}, f32[8,2,128,128]{3,2,1,0:T(8,128)S(1)}, s32[]{:T(128)}) while((s32[]{:T(128)}, f32[2,2048,512]{2,1,0:T(8,128)}, s32[8,3]{0,1:T(4,128)S(1)}, f32[8,2,128,128]{3,2,1,0:T(8,128)S(1)}, s32[]{:T(128)}) %tuple.108), condition=%wide.while_cond, body=%wide.while_body.sunk | while | flops 2 | bytes 262261 | solution.py:180
  1285.5 17.5 %fusion.250 = f32[8,2,512]{2,1,0:T(2,128)S(1)} fusion(f32[8,2,128,128]{3,2,1,0:T(8,128)S(1)} %get-tuple-element.349, f32[8,512,128]{1,2,0:T(8,128)} %copy.215, f32[8,512]{1,0:T(8,128)S(1)} %bitcast.283, s32[8,512]{1,0:T(8,128)S(1)} %get-tuple-element.372, f32[8,512]{1,0:T(8,128)S(1)} %bitcast.284, s32[8,512]{1,0:T(8,128)S(1)} %get-tuple-element.374, ...), kind=kOutput, calls=%fused_computation.6.clone.2 | convolution fusion | flops 1624760320 | bytes 3440640 | tf_op jit(solution)/shard_map/while/body/eval_jaxpr/gsu,gcuv->gcsv/dot_general | solution.py:44
  1303.6 12.9 all-to-all-start.4
  1316.5 18.7 %all-to-all-done.4 = f32[64,2,2,512]{3,2,1,0:T(2,128)S(1)} async-done(((f32[64,2,2,512]{3,2,1,0:T(2,128)}), f32[64,2,2,512]{3,2,1,0:T(2,128)S(1)}, u32[]{:S(2)}, u32[]{:S(2)}) %all-to-all-start.4) | async-done | bytes 524320 | tf_op jit(solution)/shard_map/all_to_all | solution.py:203
  (949 shorter events, 536.7 us)
Async XLA Ops:
  3.8 162.9 %all-to-all-start = ((s32[64,1,2]{2,1,0:T(1,128)}), s32[64,1,2]{2,1,0:T(1,128)S(1)}, u32[]{:S(2)}, u32[]{:S(2)}) async-start(s32[64,1,2]{2,1,0:T(1,128)} %bitcast.12), calls=%async_computation | async-start | bytes 65536 | tf_op jit(solution)/shard_map/all_to_all | solution.py:192
  27.8 26.3 %copy-start = (f32[1,2048,512]{2,1,0:T(8,128)S(1)}, f32[1,2048,512]{2,1,0:T(8,128)}, u32[]{:S(2)}) copy-start(f32[1,2048,512]{2,1,0:T(8,128)} %get-tuple-element.230) | copy-start | bytes 12582916
  27.8 26.3 %copy-start.1 = (f32[1,2048,512]{2,1,0:T(8,128)S(1)}, f32[1,2048,512]{2,1,0:T(8,128)}, u32[]{:S(2)}) copy-start(f32[1,2048,512]{2,1,0:T(8,128)} %get-tuple-element.231) | copy-start | bytes 12582916
  166.7 97.7 %all-to-all-start.1 = ((f32[4,2,256,512]{2,3,1,0:T(8,128)}), f32[4,2,256,512]{2,3,1,0:T(8,128)}, u32[]{:S(2)}, u32[]{:S(2)}) async-start(f32[4,2,256,512]{2,3,1,0:T(8,128)} %copy.60), calls=%async_computation.1 | async-start | bytes 8388608 | tf_op jit(solution)/shard_map/all_to_all | solution.py:39
  176.0 94.3 %copy-start.3 = (s32[16,2,512]{2,1,0:T(2,128)S(1)}, s32[16,2,512]{2,1,0:T(2,128)}, u32[]{:S(2)}) copy-start(s32[16,2,512]{2,1,0:T(2,128)} %param.14) | copy-start | bytes 196612
  264.4 97.7 %all-to-all-start.2 = ((f32[4,2,256,512]{2,3,1,0:T(8,128)}), f32[4,2,256,512]{2,3,1,0:T(8,128)}, u32[]{:S(2)}, u32[]{:S(2)}) async-start(f32[4,2,256,512]{2,3,1,0:T(8,128)} %copy.61), calls=%async_computation.2 | async-start | bytes 8388608 | tf_op jit(solution)/shard_map/all_to_all | solution.py:39
  362.1 84.2 %all-to-all-start.3 = ((s32[64,2,2,512]{3,2,1,0:T(2,128)}), s32[64,2,2,512]{3,2,1,0:T(2,128)S(1)}, u32[]{:S(2)}, u32[]{:S(2)}) async-start(s32[64,2,2,512]{3,2,1,0:T(2,128)} %bitcast.30), calls=%async_computation.3 | async-start | bytes 1048576 | tf_op jit(solution)/shard_map/all_to_all | solution.py:193
  442.1 4.2 copy-start.2
  446.3 889.6 %copy-start.4 = (f32[16,2,512]{2,1,0:T(2,128)S(1)}, f32[16,2,512]{2,1,0:T(2,128)}, u32[]{:S(2)}) copy-start(f32[16,2,512]{2,1,0:T(2,128)} %param.15) | copy-start | bytes 196612
  1303.6 31.7 %all-to-all-start.4 = ((f32[64,2,2,512]{3,2,1,0:T(2,128)}), f32[64,2,2,512]{3,2,1,0:T(2,128)S(1)}, u32[]{:S(2)}, u32[]{:S(2)}) async-start(f32[64,2,2,512]{3,2,1,0:T(2,128)} %bitcast.32), calls=%async_computation.4 | async-start | bytes 1048576 | tf_op jit(solution)/shard_map/all_to_all | solution.py:203
where the time goes:
time: 1350 us; the launch traced here: 1340 us
  local copies, waits for them, and re-layouts  464 us (34%)
  matrix products  464 us (34%)
  waiting for transfers between devices  190 us (14%)
  other arithmetic  158 us (12%)
  starting transfers between devices  52.2 us (4%)
    dot_general x64, matrix products, product(): return jnp.einsum(pattern, operand_a, operand_b, precision=PRECISE)  464 us
    gather x384, local copies, waits for them, and re-layouts  376 us
    all_to_all x2, waiting for transfers between devices, cut_exchange(): lax.all_to_all(piece, axis, split_axis=0, concat_axis=0, tiled=True)  172 us
    add x16, other arithmetic, kernel_rows(): weights + jnp.where(tile_cells == cell_index[..., None] + tap_step, kerne...  143 us
    add x16, local copies, waits for them, and re-layouts, kernel_rows(): weights + jnp.where(tile_cells == cell_index[..., None] + tap_step, kerne...  30 us
  transfers between devices with their start and end apart: 5, of which 3 were waited for; matrix products, arithmetic and copies ran while one was open for 17% of the time, Pallas kernels for 0%

commit v1 on v0

v1 whole, which is shorter than its diff:
```python
import functools

import jax
import jax.numpy as jnp
from jax import lax
from jax.experimental import pallas as pl
from jax.experimental.pallas import tpu as pltpu
from jax.sharding import Mesh
from jax.sharding import PartitionSpec as P


N = 2048
SP = 0.7 / N
R = 16
CR = 128
SMEM = pl.BlockSpec(memory_space=pltpu.SMEM)
VMEM = pl.BlockSpec(memory_space=pltpu.VMEM)
HBM = pl.BlockSpec(memory_space=pltpu.HBM)
F32 = jnp.float32
BF16 = jnp.bfloat16

SIN_C = (3.14159264, -5.16771009, 2.55007766, -0.59829216, 0.07765941)
COS_C = (1.0, -4.93480214, 4.05870916, -1.33521206, 0.23493756, -0.02439672)
G_C = (0.5, 0.12500105, 0.0624521, 0.03985648, 0.0215331, 0.03890036)
MAGIC = 12582912.0


def horner(z, coefs):
    acc = jnp.full_like(z, coefs[-1])
    for c in coefs[-2::-1]:
        acc = acc * z + c
    return acc


def cis_turns(t):
    r = t - ((t + MAGIC) - MAGIC)
    z = r * r
    s = r * horner(z, SIN_C)
    c = horner(z, COS_C)
    s2 = s + s
    return 1.0 - s2 * s, s2 * c


def split(x):
    hi = x.astype(BF16)
    return hi, (x - hi.astype(F32)).astype(BF16)


def bdot(a, b):
    return jnp.dot(a, b, preferred_element_type=F32)


def tables_kernel(ids, e1h, e1l, e2h, e2l, tw1, tw2):
    row = lax.broadcasted_iota(jnp.int32, (128, 128), 0)
    col = lax.broadcasted_iota(jnp.int32, (128, 128), 1)
    lane = lax.broadcasted_iota(jnp.int32, (8, 128), 1)

    def cs(k):
        return cis_turns((k & (N - 1)).astype(F32) * (1.0 / N))

    def put(h, l, i, r, c, v):
        a, b = v
        h[i, 128 * r : 128 * r + 128, 128 * c : 128 * c + 128] = a
        l[i, 128 * r : 128 * r + 128, 128 * c : 128 * c + 128] = b

    for p in range(4):
        y = 16 * (127 - row if p > 1 else row) + 4 * p
        c, s = cs(col * y)
        ch, sh = split(c), split(s)
        put(e1h, e1l, p, 0, 0, ch)
        put(e1h, e1l, p, 1, 1, ch)
        put(e1h, e1l, p, 0, 1, (-sh[0], -sh[1]))
        put(e1h, e1l, p, 1, 0, sh)
        c, s = cs(row * (16 * col + 4 * p))
        ch, sh = split(c * (1.0 / N)), split(s * (1.0 / N))
        put(e2h, e2l, p, 0, 0, ch)
        put(e2h, e2l, p, 1, 1, ch)
        put(e2h, e2l, p, 0, 1, sh)
        put(e2h, e2l, p, 1, 0, (-sh[0], -sh[1]))
    for q in range(1, 4):
        for j in range(4):
            k = 4 * (q - 1) + j
            c, s = cs((512 * ids[1] + 128 * j + lane) * q)
            tw1[2 * k] = c
            tw1[2 * k + 1] = -s
            c, s = cs((128 * j + row) * q)
            tw2[0, k] = c
            tw2[1, k] = -s


def tables(ids):
    sds = jax.ShapeDtypeStruct
    shapes = [sds((4, 256, 256), BF16)] * 4 + [sds((24, 8, 128), F32), sds((2, 12, 128, 128), F32)]
    return pl.pallas_call(
        tables_kernel,
        out_shape=shapes,
        in_specs=[SMEM],
        out_specs=[VMEM] * 6,
        cost_estimate=pl.CostEstimate(flops=60 * 16 * 2 * 16384, bytes_accessed=4 << 20, transcendentals=0),
        name="tables",
    )(ids)


def turn_kernel(b, ids, sky, own, *rest):
    outs, (xin, t, tmp, sem_in, sem_out) = rest[:-5], rest[-5:]
    core, xc, yc = ids[0], ids[2], ids[3]
    loads = []
    for c in range(2):
        col = pl.multiple_of(256 * core + 128 * b, 128)
        loads.append(pltpu.make_async_copy(sky.at[c, :, pl.ds(col, 128)], xin.at[c], sem_in.at[c]))
        loads[c].start()
    moves = []

    def move(src, dst):
        moves.append(pltpu.make_async_copy(src, dst, sem_out.at[len(moves)]))
        moves[-1].start()

    rev = 127 - lax.broadcasted_iota(jnp.int32, (128, 128), 1)
    for y0 in range(16):
        for c in range(2):
            if y0 == 0:
                loads[c].wait()
            v = xin[c, pl.ds(y0, 128, stride=16), :].T
            if y0 > 7:
                v = jnp.take_along_axis(v, rev, axis=1)
            z = 2 * (y0 % 2) + c
            tmp[z] = v
            for j0 in range(16):
                t[y0, 8 * j0 : 8 * j0 + 8, 128 * c : 128 * c + 128] = tmp[z, pl.ds(j0, 8, stride=16), :]
        if y0 % 4 == 3 and y0 < 15:
            move(t.at[pl.ds(y0 - 3, 4)], own.at[pl.ds(y0 - 3, 4)])
    if outs:
        a_src = t.at[pl.ds(4 * xc, 4), pl.ds(pl.multiple_of(R * yc, 8), R), :]
        b_src = t.at[pl.ds(4 * yc, 4), pl.ds(pl.multiple_of(4 * R + R * xc, 8), R), :]
        ab, pa, pb = outs
        move(a_src, ab.at[0])
        move(b_src, ab.at[1])
        move(a_src, pa)
        move(b_src, pb)
    move(t.at[pl.ds(12, 4)], own.at[pl.ds(12, 4)])
    for m in moves:
        m.wait()


def turn(b, ids, sky):
    sds = lambda *d: jax.ShapeDtypeStruct(d, F32)
    outs = [sds(16, 128, 256)] + [sds(2, 4, R, 256), sds(4, R, 256), sds(4, R, 256)] * (1 - b)
    return pl.pallas_call(
        functools.partial(turn_kernel, b),
        in_specs=[SMEM, HBM],
        out_specs=[HBM] * len(outs),
        out_shape=outs,
        scratch_shapes=[
            pltpu.VMEM((2, N, 128), F32),
            pltpu.VMEM((16, 128, 256), F32),
            pltpu.VMEM((4, 128, 128), F32),
            pltpu.SemaphoreType.DMA((2,)),
            pltpu.SemaphoreType.DMA((8,)),
        ],
        cost_estimate=pl.CostEstimate(flops=1 << 22, bytes_accessed=4 << 20, transcendentals=0),
    )(ids, sky)


def gather3_kernel(zl, zr, za, zb, oa, ob):
    for k, (o, far) in enumerate(((oa, za), (ob, zb))):
        o[:, 0:R, :] = zl[k]
        o[:, R : 2 * R, :] = zr[k]
        o[:, 2 * R : 3 * R, :] = far[...]


def gather3(*z):
    return pl.pallas_call(
        gather3_kernel,
        out_shape=[jax.ShapeDtypeStruct((4, 3 * R, 256), F32)] * 2,
        in_specs=[VMEM] * 4,
        out_specs=[VMEM] * 2,
        compiler_params=pltpu.CompilerParams(vmem_limit_bytes=8 << 20),
        cost_estimate=pl.CostEstimate(flops=1 << 20, bytes_accessed=1 << 20, transcendentals=0),
        name="gather3",
    )(*z)


def join_kernel(ids, *refs):
    for k in range(4):
        for base, ref, o in ((ids[2], refs[k], refs[8]), (ids[3], refs[4 + k], refs[9])):
            o[pl.ds(4 * ((base + k) & 3), 4)] = ref[...]


def join(ids, a, b):
    return pl.pallas_call(
        join_kernel,
        out_shape=[jax.ShapeDtypeStruct((16, 3 * R, 256), F32)] * 2,
        in_specs=[SMEM] + [VMEM] * 8,
        out_specs=[VMEM] * 2,
        compiler_params=pltpu.CompilerParams(vmem_limit_bytes=16 << 20),
        cost_estimate=pl.CostEstimate(flops=1 << 20, bytes_accessed=3 << 20, transcendentals=0),
        name="join",
    )(ids, *a, *b)


def slab_of(kind, k, ids):
    a = ids[1]
    return (a + (0 if kind == "own" else (3, 1, 2)[k])) & 3


def block_rows(blk, ids):
    kind, d, n = blk["kind"], blk["d"], blk["rows"]
    if kind == "own":
        return [(slab_of(kind, 0, ids), d, n // 8)]
    if kind == "c":
        return [(slab_of(kind, d, ids), 128, n // 8)]
    first = R * ((ids[3] + d) & 3) if kind == "a" else 4 * R + R * ((ids[2] + d) & 3)
    return [(slab_of(kind, k, ids), first, R // 8) for k in range(3)]


def along_y_kernel(plan, n_src, ids, ws, e1h, e1l, tw1, *rest):
    srcs = rest[:n_src]
    keep, send = rest[n_src : n_src + 2]
    eh, el, tw, xin, xh0, xl0, yb0, xh1, xl1, yb1, gb, cs, tab, where, sem_e, sem_in, sem_out = rest[n_src + 2 :]
    core = ids[0]
    lane = lax.broadcasted_iota(jnp.int32, (8, 128), 1)
    sub = lax.broadcasted_iota(jnp.int32, (8, 128), 0)
    w = [ws[0], ws[1]]
    n_pairs = sum(blk["rows"] for blk in plan) // 16
    steps = n_pairs // 2

    e_copies = [
        pltpu.make_async_copy(src, dst, sem_e.at[i]) for i, (src, dst) in enumerate(((e1h, eh), (e1l, el), (tw1, tw)))
    ]
    for c in e_copies:
        c.start()
    kinds, k = [], 0
    for blk in plan:
        if blk["src"] not in kinds:
            kinds.append(blk["src"])
        for i in range(blk["rows"] // 16):
            where[2 * k] = kinds.index(blk["src"])
            where[2 * k + 1] = blk["row"] + 16 * i
            k += 1
    k = 0
    for blk in plan:
        for slab, first, n in block_rows(blk, ids):
            for i in range(n):
                row = first + 8 * i
                tab[k] = 512 * slab + 256 * core + 128 * (row >> 7) + ((row >> 3) & 15)
                k += 1

    def load(pair, slot, a):
        kind, row = where[2 * pair], pl.ds(pl.multiple_of(where[2 * pair + 1], 16), 16)
        for i, src in enumerate(kinds):
            @pl.when(kind == i)
            def _(src=src):
                h = 16 // len(src)
                for j, s in enumerate(src):
                    pltpu.make_async_copy(
                        srcs[s].at[:, row, :], xin.at[slot, a, pl.ds(h * j, h)], sem_in.at[slot, a]
                    ).start()

    def stores(k, slot):
        out = []
        for a in range(2):
            dst = pl.ds(pl.multiple_of(32 * k + 16 * a, 16), 16)
            out.append(pltpu.make_async_copy(gb.at[slot, a, core], keep.at[:, :, dst, :], sem_out.at[slot, a, 0]))
            out.append(pltpu.make_async_copy(gb.at[slot, a, 1 - core], send.at[:, :, dst, :], sem_out.at[slot, a, 1]))
        return out

    for k in range(min(2, steps)):
        for a in range(2):
            load(2 * k + a, k, a)
    for c in e_copies:
        c.wait()

    def image(pair, slot, s, xh, xl):
        for a in range(2):
            cx = ((tab[2 * pair + a] + 16 * sub).astype(F32) - N / 2) * SP
            cx2 = cx * cx
            for y0 in range(16):
                p, q = y0 // 4, y0 % 4
                kap = min(y0, 16 - y0)
                if y0 <= 8:
                    cy = ((16 * lane + kap).astype(F32) - N / 2) * SP
                    r2 = cx2 + cy * cy
                    t = r2 * horner(r2, G_C)
                    pairs = [cis_turns(t * w[pi]) for pi in range(2)]
                    if 0 < y0 < 8:
                        for pi in range(2):
                            cs[s, a, kap, pi, 0] = pairs[pi][0]
                            cs[s, a, kap, pi, 1] = pairs[pi][1]
                else:
                    pairs = [(cs[s, a, kap, pi, 0], cs[s, a, kap, pi, 1]) for pi in range(2)]
                sr = xin[slot, s, y0, 8 * a : 8 * a + 8, 0:128]
                si = xin[slot, s, y0, 8 * a : 8 * a + 8, 128:256]
                dst = slice(64 * a + 16 * q, 64 * a + 16 * q + 16)
                h, l = split(jnp.concatenate([sr * c - si * n for c, n in pairs], axis=0))
                xh[p, dst, 0:128] = h
                xl[p, dst, 0:128] = l
                h, l = split(jnp.concatenate([sr * n + si * c for c, n in pairs], axis=0))
                xh[p, dst, 128:256] = h
                xl[p, dst, 128:256] = l

    def long_part(xh, xl, yb):
        for p in range(4):
            x = xh[p]
            yb[p] = bdot(x, eh[p]) + bdot(xl[p], eh[p]) + bdot(x, el[p])

    def short_part(slot, s, yb):
        for a in range(2):
            for pi in range(2):
                sums = None
                for q in range(4):
                    r0 = 64 * a + 16 * q + 8 * pi
                    v = butterfly4([(yb[p, r0 : r0 + 8, 0:128], yb[p, r0 : r0 + 8, 128:256]) for p in range(4)])
                    if q:
                        out = []
                        for j, (r, i) in enumerate(v):
                            k = 8 * (q - 1) + 2 * j
                            out.append((r * tw[k] - i * tw[k + 1], r * tw[k + 1] + i * tw[k]))
                        v = out
                    sums = v if sums is None else [(x + u, y + z) for (x, y), (u, z) in zip(sums, v)]
                for j, (vr, vi) in enumerate(sums):
                    cc = slice(128 * (j % 2), 128 * (j % 2) + 128)
                    gb[slot, s, j // 2, pi, 0, 8 * a : 8 * a + 8, cc] = vr
                    gb[slot, s, j // 2, pi, 1, 8 * a : 8 * a + 8, cc] = vi

    def step(k, slot3):
        @pl.when(k >= 2)
        def _():
            for c in stores(k - 2, k & 1):
                c.start()

        @pl.when(k >= 3)
        def _():
            for c in stores(k - 3, 1 - (k & 1)):
                c.wait()

        ahead = jnp.where(slot3 == 0, 2, slot3 - 1)

        @pl.when(k + 2 < steps)
        def _():
            for a in range(2):
                load(2 * k + 4 + a, ahead, a)

        for a in range(2):
            pltpu.make_async_copy(xin.at[slot3, a], xin.at[slot3, a], sem_in.at[slot3, a]).wait()
        done = 1 - (k & 1)
        long_part(xh1, xl1, yb1)
        short_part(done, 0, yb0)
        image(2 * k, slot3, 0, xh0, xl0)
        long_part(xh0, xl0, yb0)
        short_part(done, 1, yb1)
        image(2 * k + 1, slot3, 1, xh1, xl1)
        return jnp.where(slot3 == 2, 0, slot3 + 1)

    lax.fori_loop(0, steps, step, jnp.int32(0))
    last = (steps - 1) % 2
    if steps >= 2:
        for c in stores(steps - 2, steps % 2):
            c.start()
    if steps >= 3:
        for c in stores(steps - 3, last):
            c.wait()
    long_part(xh1, xl1, yb1)
    short_part(last, 0, yb0)
    short_part(last, 1, yb1)
    for c in stores(steps - 1, last):
        c.start()
    if steps >= 2:
        for c in stores(steps - 2, steps % 2):
            c.wait()
    for c in stores(steps - 1, last):
        c.wait()


def along_y(plan, ids, ws, e1, srcs):
    total = sum(blk["rows"] for blk in plan)
    out = jax.ShapeDtypeStruct((2, 2, total, 256), F32)
    stage = [pltpu.VMEM((4, 128, 256), BF16), pltpu.VMEM((4, 128, 256), BF16), pltpu.VMEM((4, 128, 256), F32)]
    return pl.pallas_call(
        functools.partial(along_y_kernel, plan, len(srcs)),
        out_shape=[out, out],
        in_specs=[SMEM, SMEM] + [HBM] * (3 + len(srcs)),
        out_specs=[HBM, HBM],
        scratch_shapes=[
            pltpu.VMEM((4, 256, 256), BF16),
            pltpu.VMEM((4, 256, 256), BF16),
            pltpu.VMEM((24, 8, 128), F32),
            pltpu.VMEM((3, 2, 16, 16, 256), F32),
            *stage,
            *stage,
            pltpu.VMEM((2, 2, 2, 2, 2, 16, 256), F32),
            pltpu.VMEM((2, 2, 8, 2, 2, 8, 128), F32),
            pltpu.SMEM((total // 8,), jnp.int32),
            pltpu.SMEM((total // 8,), jnp.int32),
            pltpu.SemaphoreType.DMA((3,)),
            pltpu.SemaphoreType.DMA((3, 2)),
            pltpu.SemaphoreType.DMA((2, 2, 2)),
        ],
        cost_estimate=pl.CostEstimate(
            flops=total * 2 * 16 * 3 * 256 * 256 * 2, bytes_accessed=total * 24 * 1024, transcendentals=0
        ),
    )(ids, ws, *e1, *srcs)


def butterfly4(v):
    (r0, i0), (r1, i1), (r2, i2), (r3, i3) = v
    ar, ai, br, bi = r0 + r2, i0 + i2, r0 - r2, i0 - i2
    cr, ci, dr, di = r1 + r3, i1 + i3, r1 - r3, i1 - i3
    return [(ar + cr, ai + ci), (br + di, bi - dr), (ar - cr, ai - ci), (br - di, bi + dr)]


def dft16(v, tw):
    out = [None] * 16
    inner = [butterfly4([v[4 * p + q] for p in range(4)]) for q in range(4)]
    for t0 in range(4):
        cols = [inner[0][t0]]
        for q in range(1, 4):
            (r, i), (c, s) = inner[q][t0], tw(4 * (q - 1) + t0)
            cols.append((r * c - i * s, r * s + i * c))
        for t1, val in enumerate(butterfly4(cols)):
            out[t0 + 4 * t1] = val
    return out


def along_x_kernel(plans, ids, tiles, eh, el, tw, k2, pos_a, pos_b, *rest):
    n = len(plans)
    parts = rest[: 2 * n]
    out_a, out_b = rest[2 * n : 2 * n + 2]
    d, f, grid, ww, wl, ru, hu, res, lst, sem, sem_o = rest[2 * n + 2 :]
    core = ids[0]
    for i, plan in enumerate(plans):
        off = 0
        for blk in plan:
            for slab, first, cnt in block_rows(blk, ids):
                def issue(k, carry, i=i, slab=slab, first=first, off=off):
                    row = first + 8 * k
                    base = 128 * ((row >> 3) & 15) + 32 * slab + 8 * (row >> 7)
                    src = pl.ds(pl.multiple_of(off + 8 * k, 8), 8)
                    for ref, dst in ((parts[2 * i], base + 16 * core), (parts[2 * i + 1], base + 16 * (1 - core))):
                        pltpu.make_async_copy(
                            ref.at[:, :, src, :], d.at[:, :, pl.ds(pl.multiple_of(dst, 8), 8), :], sem
                        ).start()
                    return carry

                lax.fori_loop(0, cnt, issue, 0)
                off += 8 * cnt

    def scan(s, cnt):
        t = tiles[s]
        lst[cnt] = s
        mine = jnp.logical_and(t > 0, (((t - 1) >> 1) & 1) == core)
        return cnt + mine.astype(jnp.int32)

    lst[0] = 0
    count = lax.fori_loop(0, 256, scan, jnp.int32(0))
    last = jnp.where(count > 0, lst[jnp.maximum(count - 1, 0)], 0)
    for k in range(4):
        lst[count + k] = last
    pltpu.make_async_copy(d, d, sem).wait()

    for pi in range(2):
        def first(k, carry, pi=pi):
            for q in range(4):
                x0 = 4 * k + q
                rows = pl.ds(pl.multiple_of(128 * x0, 128), 128)
                h, l = split(jnp.concatenate([d[pi, 0, rows, :], d[pi, 1, rows, :]], axis=0))
                f[x0] = bdot(eh[k], h) + bdot(el[k], h) + bdot(eh[k], l)
            return carry

        lax.fori_loop(0, 4, first, 0)

        def second(m, carry, pi=pi):
            rr = pl.ds(pl.multiple_of(8 * m, 8), 8)
            ri = pl.ds(pl.multiple_of(128 + 8 * m, 8), 8)
            for jj in range(2):
                cc = slice(128 * jj, 128 * jj + 128)
                v = dft16([(f[x0, rr, cc], f[x0, ri, cc]) for x0 in range(16)], lambda k: (tw[0, k, rr, :], tw[1, k, rr, :]))
                for t in range(16):
                    grid[(pi * 2 + jj) * 16 + t, rr, :] = v[t][0]
                    grid[(pi * 2 + jj) * 16 + t, ri, :] = v[t][1]
            return carry

        lax.fori_loop(0, 16, second, 0)

    sub = lax.broadcasted_iota(jnp.int32, (8, 128), 0)
    table = k2[...]

    def taps(row):
        off = row & 15
        cell = row >> 4
        cl = cell & 7
        idx = off * 8 + ((sub - cl) & 7)
        return jnp.take_along_axis(table, idx, axis=1), (cell >> 3) + (sub < cl).astype(jnp.int32)

    def build(sid, z):
        who, rr = (sid & 127) >> 2, pl.ds(pl.multiple_of(8 * (sid & 3), 8), 8)
        pos = jnp.where(sid < 128, pos_a[who, rr, :], pos_b[who, rr, :])
        for j in range(4):
            r, h = taps(jnp.broadcast_to(pos[4 + j : 5 + j, :], (8, 128)))
            rh = r.astype(BF16).astype(F32)
            rl = r - rh
            cc = slice(128 * j, 128 * j + 128)
            for k in range(8):
                m0, m1 = h == 2 * k, h == 2 * k + 1
                wh = jnp.concatenate([jnp.where(m0, rh, 0.0), jnp.where(m1, rh, 0.0)], axis=0).astype(BF16)
                ww[z, 16 * k : 16 * k + 16, cc] = wh
                ww[z, 128 + 16 * k : 144 + 16 * k, cc] = wh
                wl[z, 16 * k : 16 * k + 16, cc] = jnp.concatenate(
                    [jnp.where(m0, rl, 0.0), jnp.where(m1, rl, 0.0)], axis=0
                ).astype(BF16)
            r, h = taps(jnp.broadcast_to(pos[j : j + 1, :], (8, 128)))
            ru[z, j] = r
            hu[z, j] = h

    def finish(sid, z):
        t = jnp.maximum(tiles[sid] - 1, 0)
        gi = (((sid >> 1) & 1) * 2 + (t & 1)) * 16 + (t >> 4)
        th, tl = split(grid[gi])
        part = bdot(jnp.concatenate([th, tl], axis=1), ww[z]) + bdot(th, wl[z])
        rows = []
        for j in range(4):
            r, h = ru[z, j], hu[z, j]
            for c in range(2):
                acc = jnp.zeros((8, 128), F32)
                for i in range(16):
                    acc = jnp.where(h == i, part[128 * c + 8 * i : 128 * c + 8 * i + 8, 128 * j : 128 * j + 128], acc)
                rows.append(jnp.sum(r * acc, axis=0, keepdims=True))
        res[sid] = jnp.concatenate(rows[0::2] + rows[1::2], axis=0)

    build(lst[0], 0)
    build(lst[1], 1)

    def pair(i, carry):
        z = 2 * (i & 1)
        for k in range(2):
            finish(lst[2 * i + k], z + k)
            build(lst[2 * i + 2 + k], 2 - z + k)
        return carry

    lax.fori_loop(0, (count + 1) >> 1, pair, 0)
    moves = [
        pltpu.make_async_copy(res.at[pl.ds(0, 128)], out_a, sem_o.at[0]),
        pltpu.make_async_copy(res.at[pl.ds(128, 128)], out_b, sem_o.at[1]),
    ]
    for m in moves:
        m.start()
    for m in moves:
        m.wait()


def along_x(plans, ids, tiles, e2, k2, pos_a, pos_b, parts):
    return pl.pallas_call(
        functools.partial(along_x_kernel, plans),
        out_shape=[jax.ShapeDtypeStruct((128, 8, 128), F32)] * 2,
        in_specs=[SMEM, SMEM] + [VMEM] * 6 + [HBM] * len(parts),
        out_specs=[HBM, HBM],
        scratch_shapes=[
            pltpu.VMEM((2, 2, N, 256), F32),
            pltpu.VMEM((16, 256, 256), F32),
            pltpu.VMEM((64, 256, 128), F32),
            pltpu.VMEM((4, 256, 512), BF16),
            pltpu.VMEM((4, 128, 512), BF16),
            pltpu.VMEM((4, 4, 8, 128), F32),
            pltpu.VMEM((4, 4, 8, 128), jnp.int32),
            pltpu.VMEM((256, 8, 128), F32),
            pltpu.SMEM((264,), jnp.int32),
            pltpu.SemaphoreType.DMA,
            pltpu.SemaphoreType.DMA((2,)),
        ],
        cost_estimate=pl.CostEstimate(flops=60_000_000_000, bytes_accessed=16 << 20, transcendentals=0),
        name="along_x",
    )(ids, tiles, *e2, k2, pos_a, pos_b, *parts)


def shift(x, axes, size, by):
    return lax.ppermute(x, axes, [(i, (i + by) % size) for i in range(size)])


def shards(sky, plane_w, kernel, tile_ids, plane_ids, positions, observed):
    i32 = jnp.int32
    core = lax.axis_index("core")
    ids = jnp.stack([core, lax.axis_index("wa"), lax.axis_index("x"), lax.axis_index("y")]).astype(i32)
    z_axes, c_axes = ("zh", "wa"), ("zh", "x", "y")
    swap = [(0, 1), (1, 0)]

    own0, ab, pa, pb = turn(0, ids, sky)
    zl = shift(ab, z_axes, 8, 1)
    zr = shift(ab, z_axes, 8, -1)
    za = shift(pa, z_axes, 8, 2)
    zb = shift(pb, z_axes, 8, -2)
    (own1,) = turn(1, ids, sky)
    cl = shift(own1, z_axes, 8, 1)
    cr = shift(own1, z_axes, 8, -1)
    cf_lo = shift(cl[:8], z_axes, 8, 1)
    cf_hi = shift(cr[8:], z_axes, 8, -1)

    mine_a, mine_b = gather3(zl, zr, za, zb)

    def three(x, axis):
        l = shift(x, axis, 4, 1)
        r = shift(x, axis, 4, -1)
        return r, shift(x, axis, 4, 2), l

    ax, bx = three(mine_a, "x"), three(mine_b, "y")
    a0, b0 = join(ids, (mine_a,) + ax, (mine_b,) + bx)
    ar, af, al = three(a0, "y")
    br, bf, bl = three(b0, "x")

    target = plane_ids[:, 0]
    same = (target[:, None] == target[None, :]).astype(i32)
    rank = jnp.sum(jnp.tril(same, -1), axis=1)
    slot = target * 2 + rank
    pos = positions.reshape(16, 8, 128)
    slot_pos = jnp.zeros((128, 8, 128), i32).at[slot].set(pos, unique_indices=True)
    slot_tile = jnp.zeros((128,), i32).at[slot].set(tile_ids + 1, unique_indices=True)
    tile_row = jnp.pad(slot_tile.reshape(32, 1, 4), ((0, 0), (0, 7), (0, 124)))
    payload = jnp.concatenate([slot_pos.reshape(32, 32, 128), tile_row], axis=1)
    asked = lax.all_to_all(payload, c_axes, split_axis=0, concat_axis=0, tiled=True)
    asked_b = lax.ppermute(asked, "core", swap)
    other_w = lax.ppermute(plane_w, "core", swap)
    ws = jnp.where(core == 0, jnp.concatenate([plane_w, other_w]), jnp.concatenate([other_w, plane_w]))
    tiles_a = asked[:, 32, :4].reshape(128)
    tiles_b = asked_b[:, 32, :4].reshape(128)
    tiles = jnp.concatenate([tiles_a, tiles_b])

    *e1, tw1, tw2 = tables(ids)
    e1, e2 = e1[:2] + [tw1], e1[2:] + [tw2]
    plans, parts = [], []

    def call(plan, srcs):
        keep, send = along_y(plan, ids, ws, e1, srcs)
        plans.append(plan)
        parts.extend([keep, lax.ppermute(send, "core", swap)])

    def blk(kind, d, rows, row, *src):
        return dict(kind=kind, d=d, rows=rows, row=row, src=src)

    call([blk("own", 0, 128, 0, 0)], [own0])
    call([blk("own", 128, 128, 0, 0), blk("a", 0, 3 * R, 0, 1), blk("b", 0, 3 * R, 0, 2)], [own1, a0, b0])
    call(
        [
            blk("a", 3, 3 * R, 0, 2),
            blk("a", 1, 3 * R, 0, 3),
            blk("b", 3, 3 * R, 0, 4),
            blk("b", 1, 3 * R, 0, 5),
            blk("c", 0, CR, 0, 0),
            blk("c", 1, CR, 0, 1),
        ],
        [cl, cr, al, ar, bl, br],
    )
    call([blk("a", 2, 3 * R, 0, 2), blk("b", 2, 3 * R, 0, 3), blk("c", 2, CR, 0, 0, 1)], [cf_lo, cf_hi, af, bf])

    k2 = jnp.broadcast_to(kernel.reshape(1, 128), (8, 128))
    out_a, out_b = along_x(plans, ids, tiles, e2, k2, asked, asked_b, parts)
    from_b = lax.ppermute(out_b, "core", swap)
    here = (((tiles_a - 1) >> 1) & 1) == core
    merged = jnp.where(here[:, None, None], out_a, from_b)
    answers = lax.all_to_all(merged.reshape(32, 32, 128), c_axes, split_axis=0, concat_axis=0, tiled=True)
    predicted = answers.reshape(128, 8, 128)[slot]
    return observed - predicted.reshape(16, 2, 512)


def solution(mesh):
    fine = Mesh(mesh.devices.reshape(2, 4, 4, 2, 4), ("zh", "x", "y", "core", "wa"))
    ba = ("zh", "x", "y", "core")
    rows = ba + ("wa",)
    return jax.shard_map(
        shards,
        mesh=fine,
        in_specs=(
            P(None, None, "wa"),
            P(ba),
            P(),
            P(rows),
            P(rows, None),
            P(rows, None, None),
            P(rows, None, None),
        ),
        out_specs=P(rows, None, None),
        check_vma=False,
    )
```

time: 1350 us -> 246 us (0.18)
  the two profiles are of different devices: /device:TPU:1 before, /device:TPU:32 now
where the time goes in v1:
time: 246 us
  Pallas kernels  81.8 us (33%)
  waiting for transfers between devices  77.3 us (31%)
  starting transfers between devices  71.7 us (29%)
  local copies, waits for them, and re-layouts  7.58 us (3%)
  other arithmetic  6.28 us (3%)
    ppermute x20, waiting for transfers between devices, shift(): return lax.ppermute(x, axes, [(i, (i + by) % size) for i in range(size)])  53.1 us
    pallas_call x4, Pallas kernels, along_y(): pl.pallas_call(functools.partial(along_y_kernel, plan, len(srcs)), out_sh...  50.1 us
    ppermute x20, starting transfers between devices, shift(): return lax.ppermute(x, axes, [(i, (i + by) % size) for i in range(size)])  38.5 us
    all_to_all x1, starting transfers between devices, shards(): lax.all_to_all(merged.reshape(32, 32, 128), c_axes, split_axis=0, concat_...  22.5 us
    all_to_all x1, waiting for transfers between devices, shards(): lax.all_to_all(merged.reshape(32, 32, 128), c_axes, split_axis=0, concat_...  21.6 us
    pallas_call x1, Pallas kernels, along_x(): pl.pallas_call(functools.partial(along_x_kernel, plans), out_shape=[jax.S...  18.1 us
    pallas_call x2, Pallas kernels, turn(): pl.pallas_call(functools.partial(turn_kernel, b), in_specs=[SMEM, HBM], o...  9.26 us
    all_to_all x1, starting transfers between devices, shards(): lax.all_to_all(payload, c_axes, split_axis=0, concat_axis=0, tiled=True)  8.28 us
  transfers between devices with their start and end apart: 29, of which 9 were waited for; matrix products, arithmetic and copies ran while one was open for 4% of the time, Pallas kernels for 24%

profile of v1, /device:TPU:32, one launch (start us, length us, event | category | flops | bytes accessed | tf_op | source)
XLA Modules:
  0.0 245.7 jit_solution(17113054679580114707)
XLA Ops:
  0.0 0.6 pad_add_fusion.2.ids
  0.6 4.6 %shard_map.75.rest_0_ = f32[16,128,256]{2,1,0:T(8,128)} custom-call(s32[4]{0:T(128)} %pad_add_fusion.2.ids, f32[2,2048,512]{2,1,0:T(8,128)} %sky.3), custom_call_target="tpu_custom_call" | custom-call | flops 4194304 | bytes 4194304 | tf_op jit(solution)/shard_map/pallas_call | solution.py:148
  5.3 2.0 collective-permute-start.14
  7.3 0.1 collective-permute-start.15
  7.4 4.7 %shard_map.73 = (f32[16,128,256]{2,1,0:T(8,128)}, f32[2,4,16,256]{3,2,1,0:T(8,128)}, f32[4,16,256]{2,1,0:T(8,128)}, f32[4,16,256]{2,1,0:T(8,128)}) custom-call(s32[4]{0:T(128)} %pad_add_fusion.2.ids, f32[2,2048,512]{2,1,0:T(8,128)} %sky.3), custom_call_target="tpu_custom_call" | custom-call | flops 4194304 | bytes 4194304 | tf_op jit(solution)/shard_map/pallas_call | solution.py:148
  12.1 4.5 %collective-permute-start.5 = (f32[4,16,256]{2,1,0:T(8,128)}, f32[4,16,256]{2,1,0:T(8,128)S(1)}, u32[]{:S(2)}, u32[]{:S(2)}) collective-permute-start(f32[4,16,256]{2,1,0:T(8,128)} %get-tuple-element.39), channel_id=1, source_target_pairs={{0,2},{1,3},{2,128},{3,129},{128,130},{129,131},{130,0},{131,1},{4... | collective-permute-start | bytes 196616 | tf_op jit(solution)/shard_map/ppermute | solution.py:575
  16.5 3.2 %collective-permute-start.3 = (f32[2,4,16,256]{3,2,1,0:T(8,128)}, f32[2,4,16,256]{3,2,1,0:T(8,128)S(1)}, u32[]{:S(2)}, u32[]{:S(2)}) collective-permute-start(f32[2,4,16,256]{3,2,1,0:T(8,128)} %get-tuple-element.38), channel_id=1, source_target_pairs={{0,1},{1,2},{2,3},{3,128},{128,129},{129,130},{130,131},{131,0},{4... | collective-permute-start | bytes 393224 | tf_op jit(solution)/shard_map/ppermute | solution.py:575
  19.8 39.8 %collective-permute-done.5.za = f32[4,16,256]{2,1,0:T(8,128)S(1)} collective-permute-done((f32[4,16,256]{2,1,0:T(8,128)}, f32[4,16,256]{2,1,0:T(8,128)S(1)}, u32[]{:S(2)}, u32[]{:S(2)}) %collective-permute-start.5) | collective-permute-done | bytes 65568 | tf_op jit(solution)/shard_map/ppermute | solution.py:575
  59.6 3.2 %collective-permute-start.6 = (f32[4,16,256]{2,1,0:T(8,128)}, f32[4,16,256]{2,1,0:T(8,128)S(1)}, u32[]{:S(2)}, u32[]{:S(2)}) collective-permute-start(f32[4,16,256]{2,1,0:T(8,128)} %get-tuple-element.40), channel_id=1, source_target_pairs={{0,130},{1,131},{2,0},{3,1},{128,2},{129,3},{130,128},{131,129},{4... | collective-permute-start | bytes 196616 | tf_op jit(solution)/shard_map/ppermute | solution.py:575
  62.7 2.8 %collective-permute-done.6.zb = f32[4,16,256]{2,1,0:T(8,128)S(1)} collective-permute-done((f32[4,16,256]{2,1,0:T(8,128)}, f32[4,16,256]{2,1,0:T(8,128)S(1)}, u32[]{:S(2)}, u32[]{:S(2)}) %collective-permute-start.6) | collective-permute-done | bytes 65568 | tf_op jit(solution)/shard_map/ppermute | solution.py:575
  65.6 2.8 %collective-permute-start.7 = (f32[4,48,256]{2,1,0:T(8,128)S(1)}, f32[4,48,256]{2,1,0:T(8,128)S(1)}, u32[]{:S(2)}, u32[]{:S(2)}) collective-permute-start(f32[4,48,256]{2,1,0:T(8,128)S(1)} %get-tuple-element.41.refs_0_), channel_id=1, source_target_pairs={{0,96},{32,0},{64,32},{96,64},{1,97},{33,1},{65,33},{97,65},{2,98}... | collective-permute-start | bytes 589832 | tf_op jit(solution)/shard_map/ppermute | solution.py:575
  68.5 0.8 collective-permute-start.8
  69.3 0.9 collective-permute-start.9
  70.1 3.6 %collective-permute-done.7.refs_1_ = f32[4,48,256]{2,1,0:T(8,128)S(1)} collective-permute-done((f32[4,48,256]{2,1,0:T(8,128)S(1)}, f32[4,48,256]{2,1,0:T(8,128)S(1)}, u32[]{:S(2)}, u32[]{:S(2)}) %collective-permute-start.7) | collective-permute-done | bytes 196640 | tf_op jit(solution)/shard_map/ppermute | solution.py:575
  73.8 3.0 %collective-permute-start.10 = (f32[4,48,256]{2,1,0:T(8,128)S(1)}, f32[4,48,256]{2,1,0:T(8,128)S(1)}, u32[]{:S(2)}, u32[]{:S(2)}) collective-permute-start(f32[4,48,256]{2,1,0:T(8,128)S(1)} %get-tuple-element.42.refs_4_), channel_id=1, source_target_pairs={{0,24},{8,0},{16,8},{24,16},{1,25},{9,1},{17,9},{25,17},{2,26},{10... | collective-permute-start | bytes 589832 | tf_op jit(solution)/shard_map/ppermute | solution.py:575
  76.8 2.1 collective-permute-start.11
  78.9 0.7 collective-permute-start.12
  79.6 0.4 collective-permute-done.10.refs_5_
  80.0 4.0 %collective-permute-done.11.refs_6_ = f32[4,48,256]{2,1,0:T(8,128)S(1)} collective-permute-done((f32[4,48,256]{2,1,0:T(8,128)S(1)}, f32[4,48,256]{2,1,0:T(8,128)S(1)}, u32[]{:S(2)}, u32[]{:S(2)}) %collective-permute-start.11) | collective-permute-done | bytes 196640 | tf_op jit(solution)/shard_map/ppermute | solution.py:575
  84.0 2.3 collective-permute-done.12.refs_7_
  86.4 0.6 join.1
  87.0 2.2 collective-permute-start.16
  89.3 1.1 collective-permute-start.17
  90.4 3.5 %collective-permute-start.19 = (f32[16,48,256]{2,1,0:T(8,128)S(1)}, f32[16,48,256]{2,1,0:T(8,128)}, u32[]{:S(2)}, u32[]{:S(2)}) collective-permute-start(f32[16,48,256]{2,1,0:T(8,128)S(1)} %get-tuple-element.44.rest_2_), channel_id=1, source_target_pairs={{0,96},{32,0},{64,32},{96,64},{1,97},{33,1},{65,33},{97,65},{2,98}... | collective-permute-start | bytes 2359304 | tf_op jit(solution)/shard_map/ppermute | solution.py:575
  93.8 0.2 select_reduce_fusion
  94.0 0.6 scatter_custom_fusion.1
  94.7 0.1 reshape.32
  94.8 0.1 reshape.48
  94.9 1.0 scatter_fusion
  95.9 0.9 pad_add_fusion
  96.8 8.3 %all-to-all-start = ((s32[32,40,128]{2,1,0:T(8,128)}), s32[32,40,128]{2,1,0:T(8,128)S(1)}, u32[]{:S(2)}, u32[]{:S(2)}) async-start(s32[32,40,128]{2,1,0:T(8,128)} %pad_add_fusion), calls=%async_computation | async-start | bytes 1310720 | tf_op jit(solution)/shard_map/all_to_all | solution.py:617
  105.7 3.7 %tables.1 = (bf16[4,256,256]{2,1,0:T(8,128)(2,1)}, bf16[4,256,256]{2,1,0:T(8,128)(2,1)}, bf16[4,256,256]{2,1,0:T(8,128)(2,1)}, bf16[4,256,256]{2,1,0:T(8,128)(2,...) custom-call(s32[4]{0:T(128)} %pad_add_fusion.2.ids), custom_call_target="tpu_custom_call" | custom-call | flops 31457280 | bytes 4194304 | tf_op jit(solution)/shard_map/tables/pallas_call | solution.py:94
  109.4 1.2 broadcast_select_fusion.1.ws
  110.6 1.3 slice.20
  112.0 3.4 %collective-permute-start.23 = (f32[16,48,256]{2,1,0:T(8,128)S(1)}, f32[16,48,256]{2,1,0:T(8,128)}, u32[]{:S(2)}, u32[]{:S(2)}) collective-permute-start(f32[16,48,256]{2,1,0:T(8,128)S(1)} %get-tuple-element.43.rest_1_), channel_id=1, source_target_pairs={{0,16},{8,24},{16,0},{24,8},{1,17},{9,25},{17,1},{25,9},{2,18},{10... | collective-permute-start | bytes 2359304 | tf_op jit(solution)/shard_map/ppermute | solution.py:575
  115.4 2.3 slice.21
  117.6 3.0 %collective-permute-start.24 = (f32[16,48,256]{2,1,0:T(8,128)S(1)}, f32[16,48,256]{2,1,0:T(8,128)}, u32[]{:S(2)}, u32[]{:S(2)}) collective-permute-start(f32[16,48,256]{2,1,0:T(8,128)S(1)} %get-tuple-element.44.rest_2_), channel_id=1, source_target_pairs={{0,64},{32,96},{64,0},{96,32},{1,65},{33,97},{65,1},{97,33},{2,66}... | collective-permute-start | bytes 2359304 | tf_op jit(solution)/shard_map/ppermute | solution.py:575
  120.6 2.0 collective-permute-start.22
  122.7 19.2 %shard_map.77 = (f32[2,2,448,256]{3,2,1,0:T(8,128)}, f32[2,2,448,256]{3,2,1,0:T(8,128)}) custom-call(s32[4]{0:T(128)} %pad_add_fusion.2.ids, f32[2]{0:T(128)} %broadcast_select_fusion.1.ws, bf16[4,256,256]{2,1,0:T(8,128)(2,1)} %get-tuple-element.32.e1h, bf16[4,256,256]{2,1,0:T(8,128)(2,1)} %get-tuple-element.33.e1l, f32[24,8,128]{2,1,0:T(8,128)} %get-tuple-element.34.tw1, ...), custom_call_target="tpu_custom_call" | custom-call | flops 5637144576 | bytes 11010048 | tf_op jit(solution)/shard_map/pallas_call | solution.py:378
  141.9 0.3 collective-permute-start.20
  142.2 11.4 %shard_map.76 = (f32[2,2,224,256]{3,2,1,0:T(8,128)}, f32[2,2,224,256]{3,2,1,0:T(8,128)}) custom-call(s32[4]{0:T(128)} %pad_add_fusion.2.ids, f32[2]{0:T(128)} %broadcast_select_fusion.1.ws, bf16[4,256,256]{2,1,0:T(8,128)(2,1)} %get-tuple-element.32.e1h, bf16[4,256,256]{2,1,0:T(8,128)(2,1)} %get-tuple-element.33.e1l, f32[24,8,128]{2,1,0:T(8,128)} %get-tuple-element.34.tw1, ...), custom_call_target="tpu_custom_call" | custom-call | flops 2818572288 | bytes 5505024 | tf_op jit(solution)/shard_map/pallas_call | solution.py:378
  153.6 0.6 collective-permute-start.13
  154.2 11.4 %shard_map.78 = (f32[2,2,224,256]{3,2,1,0:T(8,128)}, f32[2,2,224,256]{3,2,1,0:T(8,128)}) custom-call(s32[4]{0:T(128)} %pad_add_fusion.2.ids, f32[2]{0:T(128)} %broadcast_select_fusion.1.ws, bf16[4,256,256]{2,1,0:T(8,128)(2,1)} %get-tuple-element.32.e1h, bf16[4,256,256]{2,1,0:T(8,128)(2,1)} %get-tuple-element.33.e1l, f32[24,8,128]{2,1,0:T(8,128)} %get-tuple-element.34.tw1, ...), custom_call_target="tpu_custom_call" | custom-call | flops 2818572288 | bytes 5505024 | tf_op jit(solution)/shard_map/pallas_call | solution.py:378
  165.6 0.1 collective-permute-start.25
  165.7 0.5 collective-permute-start
  166.2 8.1 %shard_map.74 = (f32[2,2,128,256]{3,2,1,0:T(8,128)}, f32[2,2,128,256]{3,2,1,0:T(8,128)}) custom-call(s32[4]{0:T(128)} %pad_add_fusion.2.ids, f32[2]{0:T(128)} %broadcast_select_fusion.1.ws, bf16[4,256,256]{2,1,0:T(8,128)(2,1)} %get-tuple-element.32.e1h, bf16[4,256,256]{2,1,0:T(8,128)(2,1)} %get-tuple-element.33.e1l, f32[24,8,128]{2,1,0:T(8,128)} %get-tuple-element.34.tw1, ...), custom_call_target="tpu_custom_call" | custom-call | flops 1610612736 | bytes 3145728 | tf_op jit(solution)/shard_map/pallas_call | solution.py:378
  174.3 0.2 collective-permute-start.2
  174.5 0.1 copy.13
  174.6 0.1 broadcast_in_dim.33
  174.7 0.1 reshape_squeeze.6
  174.9 0.1 reshape_squeeze.7
  175.0 0.6 pad_add_fusion.1.tiles
  175.6 0.9 collective-permute-done.2.rest_1_
  176.5 0.6 broadcast_in_dim.34.k2
  177.2 0.1 copy-done.10
  177.3 0.3 copy-done.9
  177.6 18.1 %along_x.1 = (f32[128,8,128]{2,1,0:T(8,128)}, f32[128,8,128]{2,1,0:T(8,128)}) custom-call(s32[4]{0:T(128)} %pad_add_fusion.2.ids, s32[256]{0:T(256)} %pad_add_fusion.1.tiles, bf16[4,256,256]{2,1,0:T(8,128)(2,1)} %get-tuple-element.29.eh, bf16[4,256,256]{2,1,0:T(8,128)(2,1)} %get-tuple-element.30.el, f32[2,12,128,128]{3,2,1,0:T(8,128)} %get-tuple-element.31.tw, ...), custom_call_target="tpu_custom_call" | custom-call | flops 60000002048 | bytes 16777216 | tf_op jit(solution)/shard_map/along_x/pallas_call | solution.py:551
  195.8 0.7 collective-permute-start.26
  196.5 1.7 collective-permute-done.26
  198.2 2.1 broadcast_select_fusion
  200.3 22.5 %all-to-all-start.1 = ((f32[32,32,128]{2,1,0:T(8,128)}), f32[32,32,128]{2,1,0:T(8,128)S(1)}, u32[]{:S(2)}, u32[]{:S(2)}) async-start(f32[32,32,128]{2,1,0:T(8,128)} %bitcast.9), calls=%async_computation.1 | async-start | bytes 1048576 | tf_op jit(solution)/shard_map/all_to_all | solution.py:657
  222.8 21.6 %all-to-all-done.1 = f32[32,32,128]{2,1,0:T(8,128)S(1)} async-done(((f32[32,32,128]{2,1,0:T(8,128)}), f32[32,32,128]{2,1,0:T(8,128)S(1)}, u32[]{:S(2)}, u32[]{:S(2)}) %all-to-all-start.1) | async-done | bytes 524320 | tf_op jit(solution)/shard_map/all_to_all | solution.py:657
  244.4 0.6 gather_fusion
  245.0 0.7 sub.7
  (56 shorter events, 0.3 us)
Async XLA Ops:
  5.3 81.1 %copy-start = (s32[4]{0:T(128)S(1)}, s32[4]{0:T(128)}, u32[]{:S(2)}) copy-start(s32[4]{0:T(128)} %pad_add_fusion.2.ids) | copy-start | bytes 52
  5.3 88.6 %copy-start.7 = (s32[16,1]{0,1:T(1,128)S(1)}, s32[16,1]{0,1:T(1,128)}, u32[]{:S(2)}) copy-start(s32[16,1]{0,1:T(1,128)} %param.11) | copy-start | bytes 196
  5.3 88.7 %copy-start.11 = (s32[16]{0:T(128)S(1)}, s32[16]{0:T(128)}, u32[]{:S(2)}) copy-start(s32[16]{0:T(128)} %param.10) | copy-start | bytes 196
  5.3 89.5 %copy-start.5 = (s32[16,2,512]{2,1,0:T(2,128)S(1)}, s32[16,2,512]{2,1,0:T(2,128)}, u32[]{:S(2)}) copy-start(s32[16,2,512]{2,1,0:T(2,128)} %param.12) | copy-start | bytes 196612
  5.3 85.1 %collective-permute-start.14 = (f32[16,128,256]{2,1,0:T(8,128)}, f32[16,128,256]{2,1,0:T(8,128)}, u32[]{:S(2)}, u32[]{:S(2)}) collective-permute-start(f32[16,128,256]{2,1,0:T(8,128)} %shard_map.75.rest_0_), channel_id=1, source_target_pairs={{0,1},{1,2},{2,3},{3,128},{128,129},{129,130},{130,131},{131,0},{4... | collective-permute-start | bytes 6291464 | tf_op jit(solution)/shard_map/ppermute | solution.py:575
  7.3 104.7 %collective-permute-start.15 = (f32[16,128,256]{2,1,0:T(8,128)}, f32[16,128,256]{2,1,0:T(8,128)}, u32[]{:S(2)}, u32[]{:S(2)}) collective-permute-start(f32[16,128,256]{2,1,0:T(8,128)} %shard_map.75.rest_0_), channel_id=1, source_target_pairs={{0,131},{1,0},{2,1},{3,2},{128,3},{129,128},{130,129},{131,130},{4... | collective-permute-start | bytes 6291464 | tf_op jit(solution)/shard_map/ppermute | solution.py:575
  12.1 47.5 %collective-permute-start.5 = (f32[4,16,256]{2,1,0:T(8,128)}, f32[4,16,256]{2,1,0:T(8,128)S(1)}, u32[]{:S(2)}, u32[]{:S(2)}) collective-permute-start(f32[4,16,256]{2,1,0:T(8,128)} %get-tuple-element.39), channel_id=1, source_target_pairs={{0,2},{1,3},{2,128},{3,129},{128,130},{129,131},{130,0},{131,1},{4... | collective-permute-start | bytes 196616 | tf_op jit(solution)/shard_map/ppermute | solution.py:575
  16.5 49.1 %collective-permute-start.3 = (f32[2,4,16,256]{3,2,1,0:T(8,128)}, f32[2,4,16,256]{3,2,1,0:T(8,128)S(1)}, u32[]{:S(2)}, u32[]{:S(2)}) collective-permute-start(f32[2,4,16,256]{3,2,1,0:T(8,128)} %get-tuple-element.38), channel_id=1, source_target_pairs={{0,1},{1,2},{2,3},{3,128},{128,129},{129,130},{130,131},{131,0},{4... | collective-permute-start | bytes 393224 | tf_op jit(solution)/shard_map/ppermute | solution.py:575
  19.8 45.8 %collective-permute-start.4 = (f32[2,4,16,256]{3,2,1,0:T(8,128)}, f32[2,4,16,256]{3,2,1,0:T(8,128)S(1)}, u32[]{:S(2)}, u32[]{:S(2)}) collective-permute-start(f32[2,4,16,256]{3,2,1,0:T(8,128)} %get-tuple-element.38), channel_id=1, source_target_pairs={{0,131},{1,0},{2,1},{3,2},{128,3},{129,128},{130,129},{131,130},{4... | collective-permute-start | bytes 393224 | tf_op jit(solution)/shard_map/ppermute | solution.py:575
  59.6 6.0 %collective-permute-start.6 = (f32[4,16,256]{2,1,0:T(8,128)}, f32[4,16,256]{2,1,0:T(8,128)S(1)}, u32[]{:S(2)}, u32[]{:S(2)}) collective-permute-start(f32[4,16,256]{2,1,0:T(8,128)} %get-tuple-element.40), channel_id=1, source_target_pairs={{0,130},{1,131},{2,0},{3,1},{128,2},{129,3},{130,128},{131,129},{4... | collective-permute-start | bytes 196616 | tf_op jit(solution)/shard_map/ppermute | solution.py:575
  65.6 8.2 %collective-permute-start.7 = (f32[4,48,256]{2,1,0:T(8,128)S(1)}, f32[4,48,256]{2,1,0:T(8,128)S(1)}, u32[]{:S(2)}, u32[]{:S(2)}) collective-permute-start(f32[4,48,256]{2,1,0:T(8,128)S(1)} %get-tuple-element.41.refs_0_), channel_id=1, source_target_pairs={{0,96},{32,0},{64,32},{96,64},{1,97},{33,1},{65,33},{97,65},{2,98}... | collective-permute-start | bytes 589832 | tf_op jit(solution)/shard_map/ppermute | solution.py:575
  68.5 8.3 %collective-permute-start.8 = (f32[4,48,256]{2,1,0:T(8,128)S(1)}, f32[4,48,256]{2,1,0:T(8,128)S(1)}, u32[]{:S(2)}, u32[]{:S(2)}) collective-permute-start(f32[4,48,256]{2,1,0:T(8,128)S(1)} %get-tuple-element.41.refs_0_), channel_id=1, source_target_pairs={{0,64},{32,96},{64,0},{96,32},{1,65},{33,97},{65,1},{97,33},{2,66}... | collective-permute-start | bytes 589832 | tf_op jit(solution)/shard_map/ppermute | solution.py:575
  69.3 9.7 %collective-permute-start.9 = (f32[4,48,256]{2,1,0:T(8,128)S(1)}, f32[4,48,256]{2,1,0:T(8,128)S(1)}, u32[]{:S(2)}, u32[]{:S(2)}) collective-permute-start(f32[4,48,256]{2,1,0:T(8,128)S(1)} %get-tuple-element.41.refs_0_), channel_id=1, source_target_pairs={{0,32},{32,64},{64,96},{96,0},{1,33},{33,65},{65,97},{97,1},{2,34}... | collective-permute-start | bytes 589832 | tf_op jit(solution)/shard_map/ppermute | solution.py:575
  73.8 6.2 %collective-permute-start.10 = (f32[4,48,256]{2,1,0:T(8,128)S(1)}, f32[4,48,256]{2,1,0:T(8,128)S(1)}, u32[]{:S(2)}, u32[]{:S(2)}) collective-permute-start(f32[4,48,256]{2,1,0:T(8,128)S(1)} %get-tuple-element.42.refs_4_), channel_id=1, source_target_pairs={{0,24},{8,0},{16,8},{24,16},{1,25},{9,1},{17,9},{25,17},{2,26},{10... | collective-permute-start | bytes 589832 | tf_op jit(solution)/shard_map/ppermute | solution.py:575
  76.8 7.2 %collective-permute-start.11 = (f32[4,48,256]{2,1,0:T(8,128)S(1)}, f32[4,48,256]{2,1,0:T(8,128)S(1)}, u32[]{:S(2)}, u32[]{:S(2)}) collective-permute-start(f32[4,48,256]{2,1,0:T(8,128)S(1)} %get-tuple-element.42.refs_4_), channel_id=1, source_target_pairs={{0,16},{8,24},{16,0},{24,8},{1,17},{9,25},{17,1},{25,9},{2,18},{10... | collective-permute-start | bytes 589832 | tf_op jit(solution)/shard_map/ppermute | solution.py:575
  78.9 7.4 %collective-permute-start.12 = (f32[4,48,256]{2,1,0:T(8,128)S(1)}, f32[4,48,256]{2,1,0:T(8,128)S(1)}, u32[]{:S(2)}, u32[]{:S(2)}) collective-permute-start(f32[4,48,256]{2,1,0:T(8,128)S(1)} %get-tuple-element.42.refs_4_), channel_id=1, source_target_pairs={{0,8},{8,16},{16,24},{24,0},{1,9},{9,17},{17,25},{25,1},{2,10},{10... | collective-permute-start | bytes 589832 | tf_op jit(solution)/shard_map/ppermute | solution.py:575
  80.0 10.4 %collective-permute-start.1 = (f32[1]{0:T(128)}, f32[1]{0:T(128)}, u32[]{:S(2)}, u32[]{:S(2)}) collective-permute-start(f32[1]{0:T(128)} %param.8), channel_id=1, source_target_pairs={{0,4},{4,0},{1,5},{5,1},{2,6},{6,2},{3,7},{7,3},{8,12},{12,8},{9,1... | collective-permute-start | bytes 20 | tf_op jit(solution)/shard_map/ppermute | solution.py:619
  87.0 25.0 %copy-start.2 = (f32[16,48,256]{2,1,0:T(8,128)}, f32[16,48,256]{2,1,0:T(8,128)S(1)}, u32[]{:S(2)}) copy-start(f32[16,48,256]{2,1,0:T(8,128)S(1)} %get-tuple-element.43.rest_1_) | copy-start | bytes 2359300
  87.0 30.6 %copy-start.1 = (f32[16,48,256]{2,1,0:T(8,128)}, f32[16,48,256]{2,1,0:T(8,128)S(1)}, u32[]{:S(2)}) copy-start(f32[16,48,256]{2,1,0:T(8,128)S(1)} %get-tuple-element.44.rest_2_) | copy-start | bytes 2359300
  87.0 30.6 %collective-permute-start.16 = (f32[16,48,256]{2,1,0:T(8,128)S(1)}, f32[16,48,256]{2,1,0:T(8,128)}, u32[]{:S(2)}, u32[]{:S(2)}) collective-permute-start(f32[16,48,256]{2,1,0:T(8,128)S(1)} %get-tuple-element.43.rest_1_), channel_id=1, source_target_pairs={{0,8},{8,16},{16,24},{24,0},{1,9},{9,17},{17,25},{25,1},{2,10},{10... | collective-permute-start | bytes 2359304 | tf_op jit(solution)/shard_map/ppermute | solution.py:575
  89.3 31.3 %collective-permute-start.17 = (f32[16,48,256]{2,1,0:T(8,128)S(1)}, f32[16,48,256]{2,1,0:T(8,128)}, u32[]{:S(2)}, u32[]{:S(2)}) collective-permute-start(f32[16,48,256]{2,1,0:T(8,128)S(1)} %get-tuple-element.43.rest_1_), channel_id=1, source_target_pairs={{0,24},{8,0},{16,8},{24,16},{1,25},{9,1},{17,9},{25,17},{2,26},{10... | collective-permute-start | bytes 2359304 | tf_op jit(solution)/shard_map/ppermute | solution.py:575
  90.3 30.3 %collective-permute-start.18 = (f32[16,48,256]{2,1,0:T(8,128)S(1)}, f32[16,48,256]{2,1,0:T(8,128)}, u32[]{:S(2)}, u32[]{:S(2)}) collective-permute-start(f32[16,48,256]{2,1,0:T(8,128)S(1)} %get-tuple-element.44.rest_2_), channel_id=1, source_target_pairs={{0,32},{32,64},{64,96},{96,0},{1,33},{33,65},{65,97},{97,1},{2,34}... | collective-permute-start | bytes 2359304 | tf_op jit(solution)/shard_map/ppermute | solution.py:575
  90.4 32.3 %collective-permute-start.19 = (f32[16,48,256]{2,1,0:T(8,128)S(1)}, f32[16,48,256]{2,1,0:T(8,128)}, u32[]{:S(2)}, u32[]{:S(2)}) collective-permute-start(f32[16,48,256]{2,1,0:T(8,128)S(1)} %get-tuple-element.44.rest_2_), channel_id=1, source_target_pairs={{0,96},{32,0},{64,32},{96,64},{1,97},{33,1},{65,33},{97,65},{2,98}... | collective-permute-start | bytes 2359304 | tf_op jit(solution)/shard_map/ppermute | solution.py:575
  96.8 68.9 %all-to-all-start = ((s32[32,40,128]{2,1,0:T(8,128)}), s32[32,40,128]{2,1,0:T(8,128)S(1)}, u32[]{:S(2)}, u32[]{:S(2)}) async-start(s32[32,40,128]{2,1,0:T(8,128)} %pad_add_fusion), calls=%async_computation | async-start | bytes 1310720 | tf_op jit(solution)/shard_map/all_to_all | solution.py:617
  112.0 41.6 %collective-permute-start.23 = (f32[16,48,256]{2,1,0:T(8,128)S(1)}, f32[16,48,256]{2,1,0:T(8,128)}, u32[]{:S(2)}, u32[]{:S(2)}) collective-permute-start(f32[16,48,256]{2,1,0:T(8,128)S(1)} %get-tuple-element.43.rest_1_), channel_id=1, source_target_pairs={{0,16},{8,24},{16,0},{24,8},{1,17},{9,25},{17,1},{25,9},{2,18},{10... | collective-permute-start | bytes 2359304 | tf_op jit(solution)/shard_map/ppermute | solution.py:575
  117.6 36.5 %collective-permute-start.24 = (f32[16,48,256]{2,1,0:T(8,128)S(1)}, f32[16,48,256]{2,1,0:T(8,128)}, u32[]{:S(2)}, u32[]{:S(2)}) collective-permute-start(f32[16,48,256]{2,1,0:T(8,128)S(1)} %get-tuple-element.44.rest_2_), channel_id=1, source_target_pairs={{0,64},{32,96},{64,0},{96,32},{1,65},{33,97},{65,1},{97,33},{2,66}... | collective-permute-start | bytes 2359304 | tf_op jit(solution)/shard_map/ppermute | solution.py:575
  120.6 33.6 %collective-permute-start.21 = (f32[8,128,256]{2,1,0:T(8,128)S(1)}, f32[8,128,256]{2,1,0:T(8,128)}, u32[]{:S(2)}, u32[]{:S(2)}) collective-permute-start(f32[8,128,256]{2,1,0:T(8,128)S(1)} %slice.20), channel_id=1, source_target_pairs={{0,1},{1,2},{2,3},{3,128},{128,129},{129,130},{130,131},{131,0},{4... | collective-permute-start | bytes 3145736 | tf_op jit(solution)/shard_map/ppermute | solution.py:575
  120.6 33.6 %collective-permute-start.22 = (f32[8,128,256]{2,1,0:T(8,128)}, f32[8,128,256]{2,1,0:T(8,128)}, u32[]{:S(2)}, u32[]{:S(2)}) collective-permute-start(f32[8,128,256]{2,1,0:T(8,128)} %slice.21), channel_id=1, source_target_pairs={{0,131},{1,0},{2,1},{3,2},{128,3},{129,128},{130,129},{131,130},{4... | collective-permute-start | bytes 3145736 | tf_op jit(solution)/shard_map/ppermute | solution.py:575
  141.9 34.6 %collective-permute-start.20 = (f32[2,2,448,256]{3,2,1,0:T(8,128)}, f32[2,2,448,256]{3,2,1,0:T(8,128)}, u32[]{:S(2)}, u32[]{:S(2)}) collective-permute-start(f32[2,2,448,256]{3,2,1,0:T(8,128)} %get-tuple-element.48), channel_id=1, source_target_pairs={{0,4},{4,0},{1,5},{5,1},{2,6},{6,2},{3,7},{7,3},{8,12},{12,8},{9,1... | collective-permute-start | bytes 5505032 | tf_op jit(solution)/shard_map/ppermute | solution.py:632
  153.6 22.9 %collective-permute-start.13 = (f32[2,2,224,256]{3,2,1,0:T(8,128)}, f32[2,2,224,256]{3,2,1,0:T(8,128)}, u32[]{:S(2)}, u32[]{:S(2)}) collective-permute-start(f32[2,2,224,256]{3,2,1,0:T(8,128)} %get-tuple-element.46), channel_id=1, source_target_pairs={{0,4},{4,0},{1,5},{5,1},{2,6},{6,2},{3,7},{7,3},{8,12},{12,8},{9,1... | collective-permute-start | bytes 2752520 | tf_op jit(solution)/shard_map/ppermute | solution.py:632
  165.6 10.9 %collective-permute-start.25 = (f32[2,2,224,256]{3,2,1,0:T(8,128)}, f32[2,2,224,256]{3,2,1,0:T(8,128)S(1)}, u32[]{:S(2)}, u32[]{:S(2)}) collective-permute-start(f32[2,2,224,256]{3,2,1,0:T(8,128)} %get-tuple-element.50), channel_id=1, source_target_pairs={{0,4},{4,0},{1,5},{5,1},{2,6},{6,2},{3,7},{7,3},{8,12},{12,8},{9,1... | collective-permute-start | bytes 2752520 | tf_op jit(solution)/shard_map/ppermute | solution.py:632
  165.7 8.9 %copy-start.3 = (s32[32,40,128]{2,1,0:T(8,128)}, s32[32,40,128]{2,1,0:T(8,128)S(1)}, u32[]{:S(2)}) copy-start(s32[32,40,128]{2,1,0:T(8,128)S(1)} %all-to-all-done.pos_a) | copy-start | bytes 1966084
  165.7 9.1 %collective-permute-start = (s32[32,40,128]{2,1,0:T(8,128)S(1)}, s32[32,40,128]{2,1,0:T(8,128)S(1)}, u32[]{:S(2)}, u32[]{:S(2)}) collective-permute-start(s32[32,40,128]{2,1,0:T(8,128)S(1)} %all-to-all-done.pos_a), channel_id=1, source_target_pairs={{0,4},{4,0},{1,5},{5,1},{2,6},{6,2},{3,7},{7,3},{8,12},{12,8},{9,1... | collective-permute-start | bytes 1966088 | tf_op jit(solution)/shard_map/ppermute | solution.py:618
  166.2 8.3 %copy-start.6 = (f32[16,8]{0,1:T(8,128)S(1)}, f32[16,8]{0,1:T(8,128)}, u32[]{:S(2)}) copy-start(f32[16,8]{0,1:T(8,128)} %param.9) | copy-start | bytes 1540
  174.3 2.2 collective-permute-start.2
  174.8 2.4 copy-start.8
  176.5 0.8 copy-start.10
  176.5 1.1 copy-start.9
  195.7 49.3 %copy-start.4 = (f32[16,2,512]{2,1,0:T(2,128)S(1)}, f32[16,2,512]{2,1,0:T(2,128)}, u32[]{:S(2)}) copy-start(f32[16,2,512]{2,1,0:T(2,128)} %param.13) | copy-start | bytes 196612
  195.8 2.5 collective-permute-start.26
  200.3 44.1 %all-to-all-start.1 = ((f32[32,32,128]{2,1,0:T(8,128)}), f32[32,32,128]{2,1,0:T(8,128)S(1)}, u32[]{:S(2)}, u32[]{:S(2)}) async-start(f32[32,32,128]{2,1,0:T(8,128)} %bitcast.9), calls=%async_computation.1 | async-start | bytes 1048576 | tf_op jit(solution)/shard_map/all_to_all | solution.py:657

commit v2 on v1

--- a/solution.py
+++ b/solution.py
@@ -20,7 +20,7 @@
 BF16 = jnp.bfloat16
 
 SIN_C = (3.14159264, -5.16771009, 2.55007766, -0.59829216, 0.07765941)
-COS_C = (1.0, -4.93480214, 4.05870916, -1.33521206, 0.23493756, -0.02439672)
+COS_C = (0.99999995, -4.93479286, 4.05841191, -1.33188016, 0.21969679)
 G_C = (0.5, 0.12500105, 0.0624521, 0.03985648, 0.0215331, 0.03890036)
 MAGIC = 12582912.0
 
@@ -220,7 +220,7 @@
     core = ids[0]
     lane = lax.broadcasted_iota(jnp.int32, (8, 128), 1)
     sub = lax.broadcasted_iota(jnp.int32, (8, 128), 0)
-    w = [ws[0], ws[1]]
+    w = [ws[core], ws[1 - core]]
     n_pairs = sum(blk["rows"] for blk in plan) // 16
     steps = n_pairs // 2
 
@@ -259,9 +259,9 @@
     def stores(k, slot):
         out = []
         for a in range(2):
-            dst = pl.ds(pl.multiple_of(32 * k + 16 * a, 16), 16)
-            out.append(pltpu.make_async_copy(gb.at[slot, a, core], keep.at[:, :, dst, :], sem_out.at[slot, a, 0]))
-            out.append(pltpu.make_async_copy(gb.at[slot, a, 1 - core], send.at[:, :, dst, :], sem_out.at[slot, a, 1]))
+            dst = pl.ds(4 * k + 2 * a, 2)
+            out.append(pltpu.make_async_copy(gb.at[slot, a, core], keep.at[:, :, dst], sem_out.at[slot, a, 0]))
+            out.append(pltpu.make_async_copy(gb.at[slot, a, 1 - core], send.at[:, :, dst], sem_out.at[slot, a, 1]))
         return out
 
     for k in range(min(2, steps)):
@@ -290,13 +290,11 @@
                     pairs = [(cs[s, a, kap, pi, 0], cs[s, a, kap, pi, 1]) for pi in range(2)]
                 sr = xin[slot, s, y0, 8 * a : 8 * a + 8, 0:128]
                 si = xin[slot, s, y0, 8 * a : 8 * a + 8, 128:256]
-                dst = slice(64 * a + 16 * q, 64 * a + 16 * q + 16)
-                h, l = split(jnp.concatenate([sr * c - si * n for c, n in pairs], axis=0))
-                xh[p, dst, 0:128] = h
-                xl[p, dst, 0:128] = l
-                h, l = split(jnp.concatenate([sr * n + si * c for c, n in pairs], axis=0))
-                xh[p, dst, 128:256] = h
-                xl[p, dst, 128:256] = l
+                for pi, (c, n) in enumerate(pairs):
+                    r0 = 64 * a + 16 * q + 8 * pi
+                    h, l = split(jnp.concatenate([sr * c - si * n, sr * n + si * c], axis=1))
+                    xh[p, r0 : r0 + 8, :] = h
+                    xl[p, r0 : r0 + 8, :] = l
 
     def long_part(xh, xl, yb):
         for p in range(4):
@@ -319,8 +317,8 @@
                     sums = v if sums is None else [(x + u, y + z) for (x, y), (u, z) in zip(sums, v)]
                 for j, (vr, vi) in enumerate(sums):
                     cc = slice(128 * (j % 2), 128 * (j % 2) + 128)
-                    gb[slot, s, j // 2, pi, 0, 8 * a : 8 * a + 8, cc] = vr
-                    gb[slot, s, j // 2, pi, 1, 8 * a : 8 * a + 8, cc] = vi
+                    gb[slot, s, j // 2, pi, 0, a, :, cc] = vr
+                    gb[slot, s, j // 2, pi, 1, a, :, cc] = vi
 
     def step(k, slot3):
         @pl.when(k >= 2)
@@ -373,12 +371,12 @@
 
 def along_y(plan, ids, ws, e1, srcs):
     total = sum(blk["rows"] for blk in plan)
-    out = jax.ShapeDtypeStruct((2, 2, total, 256), F32)
+    out = jax.ShapeDtypeStruct((2, 2, total // 8, 8, 256), F32)
     stage = [pltpu.VMEM((4, 128, 256), BF16), pltpu.VMEM((4, 128, 256), BF16), pltpu.VMEM((4, 128, 256), F32)]
     return pl.pallas_call(
         functools.partial(along_y_kernel, plan, len(srcs)),
         out_shape=[out, out],
-        in_specs=[SMEM, SMEM] + [HBM] * (3 + len(srcs)),
+        in_specs=[SMEM] * 2 + [HBM] * (3 + len(srcs)),
         out_specs=[HBM, HBM],
         scratch_shapes=[
             pltpu.VMEM((4, 256, 256), BF16),
@@ -387,7 +385,7 @@
             pltpu.VMEM((3, 2, 16, 16, 256), F32),
             *stage,
             *stage,
-            pltpu.VMEM((2, 2, 2, 2, 2, 16, 256), F32),
+            pltpu.VMEM((2, 2, 2, 2, 2, 2, 8, 256), F32),
             pltpu.VMEM((2, 2, 8, 2, 2, 8, 128), F32),
             pltpu.SMEM((total // 8,), jnp.int32),
             pltpu.SMEM((total // 8,), jnp.int32),
@@ -421,104 +419,136 @@
     return out
 
 
-def along_x_kernel(plans, ids, tiles, eh, el, tw, k2, pos_a, pos_b, *rest):
+def along_x_kernel(plans, ids, k1, e2h, e2l, tw2, pos_a, pos_b, *rest):
     n = len(plans)
     parts = rest[: 2 * n]
     out_a, out_b = rest[2 * n : 2 * n + 2]
-    d, f, grid, ww, wl, ru, hu, res, lst, sem, sem_o = rest[2 * n + 2 :]
+    eh, el, tw, pv, d, f0, f1, grid = rest[2 * n + 2 : 2 * n + 10]
+    bufs = [rest[2 * n + 10 + 4 * k : 2 * n + 14 + 4 * k] for k in range(4)]
+    res, lst, notes, sem, sem_e, sem_o = rest[2 * n + 26 :]
+    f = (f0, f1)
     core = ids[0]
     for i, plan in enumerate(plans):
         off = 0
         for blk in plan:
             for slab, first, cnt in block_rows(blk, ids):
-                def issue(k, carry, i=i, slab=slab, first=first, off=off):
-                    row = first + 8 * k
-                    base = 128 * ((row >> 3) & 15) + 32 * slab + 8 * (row >> 7)
-                    src = pl.ds(pl.multiple_of(off + 8 * k, 8), 8)
-                    for ref, dst in ((parts[2 * i], base + 16 * core), (parts[2 * i + 1], base + 16 * (1 - core))):
-                        pltpu.make_async_copy(
-                            ref.at[:, :, src, :], d.at[:, :, pl.ds(pl.multiple_of(dst, 8), 8), :], sem
-                        ).start()
-                    return carry
-
-                lax.fori_loop(0, cnt, issue, 0)
-                off += 8 * cnt
+                base = 32 * slab + 8 * (first >> 7)
+                for ref, side in ((parts[2 * i], core), (parts[2 * i + 1], 1 - core)):
+                    at = pl.ds(pl.multiple_of(base + 16 * side, 8), 8)
+                    dst = d.at[:, :, pl.ds((first >> 3) & 15, cnt), at, :]
+                    pltpu.make_async_copy(ref.at[:, :, pl.ds(off, cnt)], dst, sem).start()
+                off += cnt
+    last8 = pl.ds(64, 8)
+    notice = [
+        pltpu.make_async_copy(src.at[:, last8, :], notes.at[i], sem_o.at[i]) for i, src in enumerate((pos_a, pos_b))
+    ]
+    for c in notice:
+        c.start()
+    small = [(e2h, eh), (e2l, el), (tw2, tw), (pos_a, pv.at[0]), (pos_b, pv.at[1])]
+    small = [pltpu.make_async_copy(s, t, sem_e.at[i]) for i, (s, t) in enumerate(small)]
+    for c in small:
+        c.start()
+    res[...] = jnp.zeros_like(res)
+    for c in notice:
+        c.wait()
+
+    def tile_of(sid):
+        return notes[sid >> 7, (sid & 127) >> 3, 0, sid & 7]
 
     def scan(s, cnt):
-        t = tiles[s]
-        lst[cnt] = s
-        mine = jnp.logical_and(t > 0, (((t - 1) >> 1) & 1) == core)
-        return cnt + mine.astype(jnp.int32)
+        for k in range(8):
+            t = notes[s >> 4, s & 15, 0, k]
+            lst[cnt] = 8 * s + k
+            mine = jnp.logical_and(t > 0, (((t - 1) >> 1) & 1) == core)
+            cnt = cnt + mine.astype(jnp.int32)
+        return cnt
 
     lst[0] = 0
-    count = lax.fori_loop(0, 256, scan, jnp.int32(0))
+    count = lax.fori_loop(0, 32, scan, jnp.int32(0))
     last = jnp.where(count > 0, lst[jnp.maximum(count - 1, 0)], 0)
-    for k in range(4):
+    for k in range(8):
         lst[count + k] = last
+    for c in small:
+        c.wait()
     pltpu.make_async_copy(d, d, sem).wait()
 
-    for pi in range(2):
-        def first(k, carry, pi=pi):
-            for q in range(4):
-                x0 = 4 * k + q
-                rows = pl.ds(pl.multiple_of(128 * x0, 128), 128)
-                h, l = split(jnp.concatenate([d[pi, 0, rows, :], d[pi, 1, rows, :]], axis=0))
-                f[x0] = bdot(eh[k], h) + bdot(el[k], h) + bdot(eh[k], l)
-            return carry
-
-        lax.fori_loop(0, 4, first, 0)
-
-        def second(m, carry, pi=pi):
-            rr = pl.ds(pl.multiple_of(8 * m, 8), 8)
-            ri = pl.ds(pl.multiple_of(128 + 8 * m, 8), 8)
-            for jj in range(2):
-                cc = slice(128 * jj, 128 * jj + 128)
-                v = dft16([(f[x0, rr, cc], f[x0, ri, cc]) for x0 in range(16)], lambda k: (tw[0, k, rr, :], tw[1, k, rr, :]))
-                for t in range(16):
-                    grid[(pi * 2 + jj) * 16 + t, rr, :] = v[t][0]
-                    grid[(pi * 2 + jj) * 16 + t, ri, :] = v[t][1]
-            return carry
-
-        lax.fori_loop(0, 16, second, 0)
+    def first(pi, k, qs=range(4)):
+        for q in qs:
+            x0 = 4 * k + q
+            h, l = split(jnp.concatenate([d[pi, 0, x0], d[pi, 1, x0]], axis=0))
+            f[pi][x0] = bdot(eh[k], h) + bdot(el[k], h) + bdot(eh[k], l)
+
+    def second(pi, m):
+        rr = pl.ds(pl.multiple_of(8 * m, 8), 8)
+        ri = pl.ds(pl.multiple_of(128 + 8 * m, 8), 8)
+        for jj in range(2):
+            cc = slice(128 * jj, 128 * jj + 128)
+            v = [(f[pi][x0, rr, cc], f[pi][x0, ri, cc]) for x0 in range(16)]
+            v = dft16(v, lambda k: (tw[0, k, rr, :], tw[1, k, rr, :]))
+            for t in range(16):
+                grid[(pi * 2 + jj) * 16 + t, rr, :] = v[t][0]
+                grid[(pi * 2 + jj) * 16 + t, ri, :] = v[t][1]
+
+    def stage0(k, carry):
+        first(0, k)
+        return carry
+
+    def stage1(k, carry):
+        for m in range(4):
+            first(1, k, (m,))
+            second(0, 4 * k + m)
+        return carry
+
+    def stage2(k, carry):
+        second(1, 2 * k)
+        second(1, 2 * k + 1)
+        return carry
+
+    lax.fori_loop(0, 4, stage0, 0)
+    lax.fori_loop(0, 4, stage1, 0)
+    lax.fori_loop(0, 8, stage2, 0)
 
     sub = lax.broadcasted_iota(jnp.int32, (8, 128), 0)
-    table = k2[...]
+    table = jnp.broadcast_to(k1[...], (8, 128))
 
     def taps(row):
+        row = jnp.broadcast_to(row, (8, 128))
         off = row & 15
         cell = row >> 4
         cl = cell & 7
         idx = off * 8 + ((sub - cl) & 7)
         return jnp.take_along_axis(table, idx, axis=1), (cell >> 3) + (sub < cl).astype(jnp.int32)
 
-    def build(sid, z):
-        who, rr = (sid & 127) >> 2, pl.ds(pl.multiple_of(8 * (sid & 3), 8), 8)
-        pos = jnp.where(sid < 128, pos_a[who, rr, :], pos_b[who, rr, :])
-        for j in range(4):
-            r, h = taps(jnp.broadcast_to(pos[4 + j : 5 + j, :], (8, 128)))
-            rh = r.astype(BF16).astype(F32)
-            rl = r - rh
-            cc = slice(128 * j, 128 * j + 128)
-            for k in range(8):
-                m0, m1 = h == 2 * k, h == 2 * k + 1
-                wh = jnp.concatenate([jnp.where(m0, rh, 0.0), jnp.where(m1, rh, 0.0)], axis=0).astype(BF16)
-                ww[z, 16 * k : 16 * k + 16, cc] = wh
-                ww[z, 128 + 16 * k : 144 + 16 * k, cc] = wh
-                wl[z, 16 * k : 16 * k + 16, cc] = jnp.concatenate(
-                    [jnp.where(m0, rl, 0.0), jnp.where(m1, rl, 0.0)], axis=0
+    def build(sid, buf):
+        ww, wl, ru, hu = buf
+        pos = pv[sid >> 7, (sid & 127) >> 3, pl.ds(pl.multiple_of(8 * (sid & 7), 8), 8), :]
+        for jp in range(2):
+            th = []
+            for j in (2 * jp, 2 * jp + 1):
+                r, h = taps(pos[4 + j : 5 + j, :])
+                rh = r.astype(BF16).astype(F32)
+                th.append((rh, r - rh, h))
+                ru[j], hu[j] = taps(pos[j : j + 1, :])
+            cc = slice(256 * jp, 256 * jp + 256)
+            for i in range(16):
+                masks = [h == i for _, _, h in th]
+                wh = jnp.concatenate([jnp.where(m, v[0], 0.0) for m, v in zip(masks, th)], axis=1).astype(BF16)
+                ww[8 * i : 8 * i + 8, cc] = wh
+                ww[128 + 8 * i : 136 + 8 * i, cc] = wh
+                wl[8 * i : 8 * i + 8, cc] = jnp.concatenate(
+                    [jnp.where(m, v[1], 0.0) for m, v in zip(masks, th)], axis=1
                 ).astype(BF16)
-            r, h = taps(jnp.broadcast_to(pos[j : j + 1, :], (8, 128)))
-            ru[z, j] = r
-            hu[z, j] = h
-
-    def finish(sid, z):
-        t = jnp.maximum(tiles[sid] - 1, 0)
-        gi = (((sid >> 1) & 1) * 2 + (t & 1)) * 16 + (t >> 4)
-        th, tl = split(grid[gi])
-        part = bdot(jnp.concatenate([th, tl], axis=1), ww[z]) + bdot(th, wl[z])
+
+    def finish(sid, buf):
+        ww, wl, ru, hu = buf
+        t = jnp.maximum(tile_of(sid) - 1, 0)
+        x = grid[(((sid >> 1) & 1) * 2 + (t & 1)) * 16 + (t >> 4)]
+        h = x.astype(BF16)
+        hf = h.astype(F32)
+        part = bdot(jnp.concatenate([hf, x - hf], axis=1).astype(BF16), ww[...]) + bdot(h, wl[...])
         rows = []
         for j in range(4):
-            r, h = ru[z, j], hu[z, j]
+            r, h = ru[j], hu[j]
             for c in range(2):
                 acc = jnp.zeros((8, 128), F32)
                 for i in range(16):
@@ -526,17 +556,16 @@
                 rows.append(jnp.sum(r * acc, axis=0, keepdims=True))
         res[sid] = jnp.concatenate(rows[0::2] + rows[1::2], axis=0)
 
-    build(lst[0], 0)
-    build(lst[1], 1)
-
-    def pair(i, carry):
-        z = 2 * (i & 1)
-        for k in range(2):
-            finish(lst[2 * i + k], z + k)
-            build(lst[2 * i + 2 + k], 2 - z + k)
+    build(lst[0], bufs[0])
+    build(lst[1], bufs[1])
+
+    def four(i, carry):
+        for k in range(4):
+            finish(lst[4 * i + k], bufs[k])
+            build(lst[4 * i + 2 + k], bufs[(k + 2) % 4])
         return carry
 
-    lax.fori_loop(0, (count + 1) >> 1, pair, 0)
+    lax.fori_loop(0, (count + 3) >> 2, four, 0)
     moves = [
         pltpu.make_async_copy(res.at[pl.ds(0, 128)], out_a, sem_o.at[0]),
         pltpu.make_async_copy(res.at[pl.ds(128, 128)], out_b, sem_o.at[1]),
@@ -547,28 +576,61 @@
         m.wait()
 
 
-def along_x(plans, ids, tiles, e2, k2, pos_a, pos_b, parts):
+def along_x(plans, ids, k1, e2, pos_a, pos_b, parts):
+    buf = [
+        pltpu.VMEM((256, 512), BF16),
+        pltpu.VMEM((128, 512), BF16),
+        pltpu.VMEM((4, 8, 128), F32),
+        pltpu.VMEM((4, 8, 128), jnp.int32),
+    ]
     return pl.pallas_call(
         functools.partial(along_x_kernel, plans),
         out_shape=[jax.ShapeDtypeStruct((128, 8, 128), F32)] * 2,
-        in_specs=[SMEM, SMEM] + [VMEM] * 6 + [HBM] * len(parts),
+        in_specs=[SMEM, VMEM] + [HBM] * (5 + len(parts)),
         out_specs=[HBM, HBM],
         scratch_shapes=[
-            pltpu.VMEM((2, 2, N, 256), F32),
+            pltpu.VMEM((4, 256, 256), BF16),
+            pltpu.VMEM((4, 256, 256), BF16),
+            pltpu.VMEM((2, 12, 128, 128), F32),
+            pltpu.VMEM((2, 16, 72, 128), jnp.int32),
+            pltpu.VMEM((2, 2, 16, 128, 256), F32),
+            pltpu.VMEM((16, 256, 256), F32),
             pltpu.VMEM((16, 256, 256), F32),
             pltpu.VMEM((64, 256, 128), F32),
-            pltpu.VMEM((4, 256, 512), BF16),
-            pltpu.VMEM((4, 128, 512), BF16),
-            pltpu.VMEM((4, 4, 8, 128), F32),
-            pltpu.VMEM((4, 4, 8, 128), jnp.int32),
+            *buf,
+            *buf,
+            *buf,
+            *buf,
             pltpu.VMEM((256, 8, 128), F32),
-            pltpu.SMEM((264,), jnp.int32),
+            pltpu.SMEM((272,), jnp.int32),
+            pltpu.SMEM((2, 16, 8, 128), jnp.int32),
             pltpu.SemaphoreType.DMA,
+            pltpu.SemaphoreType.DMA((5,)),
             pltpu.SemaphoreType.DMA((2,)),
         ],
         cost_estimate=pl.CostEstimate(flops=60_000_000_000, bytes_accessed=16 << 20, transcendentals=0),
         name="along_x",
-    )(ids, tiles, *e2, k2, pos_a, pos_b, *parts)
+    )(ids, k1, *e2, pos_a, pos_b, *parts)
+
+
+def pick_kernel(here, there, answers, observed, rest, other):
+    for b in range(16):
+        i, j = here[b], there[b]
+        v = answers[jnp.maximum(i, 0)]
+        rest[b] = observed[b] - jnp.where(i >= 0, v, 0.0)
+        v = answers[jnp.maximum(j, 0)]
+        other[b] = jnp.where(j >= 0, v, 0.0)
+
+
+def pick(here, there, answers, observed):
+    return pl.pallas_call(
+        pick_kernel,
+        out_shape=[jax.ShapeDtypeStruct((16, 8, 128), F32)] * 2,
+        in_specs=[SMEM, SMEM, VMEM, VMEM],
+        out_specs=[VMEM, VMEM],
+        compiler_params=pltpu.CompilerParams(vmem_limit_bytes=8 << 20),
+        name="pick",
+    )(here, there, answers, observed)
 
 
 def shift(x, axes, size, by):
@@ -579,8 +641,16 @@
     i32 = jnp.int32
     core = lax.axis_index("core")
     ids = jnp.stack([core, lax.axis_index("wa"), lax.axis_index("x"), lax.axis_index("y")]).astype(i32)
-    z_axes, c_axes = ("zh", "wa"), ("zh", "x", "y")
+    z_axes = ("zh", "wa")
     swap = [(0, 1), (1, 0)]
+    zh = lax.axis_index("zh")
+
+    target = plane_ids[:, 0]
+    same = (target[:, None] == target[None, :]).astype(i32)
+    slot = target * 2 + jnp.sum(jnp.tril(same, -1), axis=1)
+    notes = jnp.pad(jnp.stack([slot, tile_ids + 1]), ((0, 6), (0, 112)))
+    mine0 = jnp.concatenate([positions.reshape(16, 8, 128), notes[None]], axis=0)
+    got0 = lax.ppermute(mine0, "zh", swap)
 
     own0, ab, pa, pb = turn(0, ids, sky)
     zl = shift(ab, z_axes, 8, 1)
@@ -605,23 +675,22 @@
     ar, af, al = three(a0, "y")
     br, bf, bl = three(b0, "x")
 
-    target = plane_ids[:, 0]
-    same = (target[:, None] == target[None, :]).astype(i32)
-    rank = jnp.sum(jnp.tril(same, -1), axis=1)
-    slot = target * 2 + rank
-    pos = positions.reshape(16, 8, 128)
-    slot_pos = jnp.zeros((128, 8, 128), i32).at[slot].set(pos, unique_indices=True)
-    slot_tile = jnp.zeros((128,), i32).at[slot].set(tile_ids + 1, unique_indices=True)
-    tile_row = jnp.pad(slot_tile.reshape(32, 1, 4), ((0, 0), (0, 7), (0, 124)))
-    payload = jnp.concatenate([slot_pos.reshape(32, 32, 128), tile_row], axis=1)
-    asked = lax.all_to_all(payload, c_axes, split_axis=0, concat_axis=0, tiled=True)
+    def place(sl, home):
+        return jnp.where((sl >> 6) == zh, (((sl >> 2) & 15) * 2 + home) * 4 + (sl & 3), -1)
+
+    here, there = place(slot, zh), place(got0[16, 0, :16], 1 - zh)
+    dst = jnp.concatenate([here, there])
+    dst = jnp.where(dst < 0, 128 + jnp.arange(32, dtype=i32), dst)
+    pos = jnp.concatenate([mine0[:16], got0[:16]])
+    tile = jnp.concatenate([tile_ids + 1, got0[16, 1, :16]])
+    slot_pos = jnp.zeros((128, 8, 128), i32).at[dst].set(pos, unique_indices=True, mode="drop")
+    slot_tile = jnp.zeros((128,), i32).at[dst].set(tile, unique_indices=True, mode="drop")
+    tile_row = jnp.pad(slot_tile.reshape(16, 1, 8), ((0, 0), (0, 7), (0, 120)))
+    payload = jnp.concatenate([slot_pos.reshape(16, 64, 128), tile_row], axis=1)
+    asked = lax.all_to_all(payload, ("x", "y"), split_axis=0, concat_axis=0, tiled=True)
     asked_b = lax.ppermute(asked, "core", swap)
     other_w = lax.ppermute(plane_w, "core", swap)
-    ws = jnp.where(core == 0, jnp.concatenate([plane_w, other_w]), jnp.concatenate([other_w, plane_w]))
-    tiles_a = asked[:, 32, :4].reshape(128)
-    tiles_b = asked_b[:, 32, :4].reshape(128)
-    tiles = jnp.concatenate([tiles_a, tiles_b])
-
+    ws = jnp.concatenate([plane_w, other_w])
     *e1, tw1, tw2 = tables(ids)
     e1, e2 = e1[:2] + [tw1], e1[2:] + [tw2]
     plans, parts = [], []
@@ -649,14 +718,14 @@
     )
     call([blk("a", 2, 3 * R, 0, 2), blk("b", 2, 3 * R, 0, 3), blk("c", 2, CR, 0, 0, 1)], [cf_lo, cf_hi, af, bf])
 
-    k2 = jnp.broadcast_to(kernel.reshape(1, 128), (8, 128))
-    out_a, out_b = along_x(plans, ids, tiles, e2, k2, asked, asked_b, parts)
+    k1 = kernel.reshape(1, 128)
+    out_a, out_b = along_x(plans, ids, k1, e2, asked, asked_b, parts)
     from_b = lax.ppermute(out_b, "core", swap)
-    here = (((tiles_a - 1) >> 1) & 1) == core
-    merged = jnp.where(here[:, None, None], out_a, from_b)
-    answers = lax.all_to_all(merged.reshape(32, 32, 128), c_axes, split_axis=0, concat_axis=0, tiled=True)
-    predicted = answers.reshape(128, 8, 128)[slot]
-    return observed - predicted.reshape(16, 2, 512)
+    merged = out_a + from_b
+    answers = lax.all_to_all(merged.reshape(16, 64, 128), ("x", "y"), split_axis=0, concat_axis=0, tiled=True)
+    rest, other = pick(here, there, answers.reshape(128, 8, 128), observed.reshape(16, 8, 128))
+    got = lax.ppermute(other, "zh", swap)
+    return (rest - got).reshape(16, 2, 512)
 
 
 def solution(mesh):

time: 246 us -> 257 us (1.045)
  the two profiles are of different devices: /device:TPU:32 before, /device:TPU:1 now
where the time goes in v2:
time: 257 us; the launch traced here: 253 us
  starting transfers between devices  85.6 us (33%)
  Pallas kernels  79.5 us (31%)
  waiting for transfers between devices  72.6 us (28%)
  local copies, waits for them, and re-layouts  8.95 us (3%)
  other arithmetic  5.1 us (2%)
    ppermute x20, waiting for transfers between devices, shift(): return lax.ppermute(x, axes, [(i, (i + by) % size) for i in range(size)])  57.2 us
    pallas_call x4, Pallas kernels, along_y(): pl.pallas_call(functools.partial(along_y_kernel, plan, len(srcs)), out_sh...  48.5 us
    ppermute x20, starting transfers between devices, shift(): return lax.ppermute(x, axes, [(i, (i + by) % size) for i in range(size)])  33.5 us
    pallas_call x1, Pallas kernels, along_x(): pl.pallas_call(functools.partial(along_x_kernel, plans), out_shape=[jax.S...  16.8 us
    ppermute x4, starting transfers between devices, call(): parts.extend([keep, lax.ppermute(send, 'core', swap)])  16.2 us
    ppermute x1, starting transfers between devices, shards(): got = lax.ppermute(other, 'zh', swap)  12.4 us
    all_to_all x1, waiting for transfers between devices, shards(): lax.all_to_all(merged.reshape(16, 64, 128), ('x', 'y'), split_axis=0, con...  10.3 us
    all_to_all x1, starting transfers between devices, shards(): lax.all_to_all(merged.reshape(16, 64, 128), ('x', 'y'), split_axis=0, con...  9.27 us
  transfers between devices with their start and end apart: 31, of which 12 were waited for; matrix products, arithmetic and copies ran while one was open for 4% of the time, Pallas kernels for 23%

profile of v2, /device:TPU:1, one launch (start us, length us, event | category | flops | bytes accessed | tf_op | source)
XLA Modules:
  0.0 252.7 jit_solution(5981138678171746471)
XLA Ops:
  0.0 0.6 pad_add_fusion.4.ids
  0.6 4.6 %shard_map.75.rest_0_ = f32[16,128,256]{2,1,0:T(8,128)} custom-call(s32[4]{0:T(128)} %pad_add_fusion.4.ids, f32[2,2048,512]{2,1,0:T(8,128)} %sky.3), custom_call_target="tpu_custom_call" | custom-call | flops 4194304 | bytes 4194304 | tf_op jit(solution)/shard_map/pallas_call | solution.py:148
  5.3 2.5 %collective-permute-start.15 = (f32[16,128,256]{2,1,0:T(8,128)}, f32[16,128,256]{2,1,0:T(8,128)}, u32[]{:S(2)}, u32[]{:S(2)}) collective-permute-start(f32[16,128,256]{2,1,0:T(8,128)} %shard_map.75.rest_0_), channel_id=1, source_target_pairs={{0,1},{1,2},{2,3},{3,128},{128,129},{129,130},{130,131},{131,0},{4... | collective-permute-start | bytes 6291464 | tf_op jit(solution)/shard_map/ppermute | solution.py:637
  7.8 4.0 %collective-permute-start.16 = (f32[16,128,256]{2,1,0:T(8,128)}, f32[16,128,256]{2,1,0:T(8,128)}, u32[]{:S(2)}, u32[]{:S(2)}) collective-permute-start(f32[16,128,256]{2,1,0:T(8,128)} %shard_map.75.rest_0_), channel_id=1, source_target_pairs={{0,131},{1,0},{2,1},{3,2},{128,3},{129,128},{130,129},{131,130},{4... | collective-permute-start | bytes 6291464 | tf_op jit(solution)/shard_map/ppermute | solution.py:637
  11.8 4.7 %shard_map.73 = (f32[16,128,256]{2,1,0:T(8,128)}, f32[2,4,16,256]{3,2,1,0:T(8,128)}, f32[4,16,256]{2,1,0:T(8,128)}, f32[4,16,256]{2,1,0:T(8,128)}) custom-call(s32[4]{0:T(128)} %pad_add_fusion.4.ids, f32[2,2048,512]{2,1,0:T(8,128)} %sky.3), custom_call_target="tpu_custom_call" | custom-call | flops 4194304 | bytes 4194304 | tf_op jit(solution)/shard_map/pallas_call | solution.py:148
  16.6 2.7 %collective-permute-start.5 = (f32[2,4,16,256]{3,2,1,0:T(8,128)}, f32[2,4,16,256]{3,2,1,0:T(8,128)S(1)}, u32[]{:S(2)}, u32[]{:S(2)}) collective-permute-start(f32[2,4,16,256]{3,2,1,0:T(8,128)} %get-tuple-element.40), channel_id=1, source_target_pairs={{0,131},{1,0},{2,1},{3,2},{128,3},{129,128},{130,129},{131,130},{4... | collective-permute-start | bytes 393224 | tf_op jit(solution)/shard_map/ppermute | solution.py:637
  19.3 0.2 select_reduce_fusion
  19.5 43.1 %collective-permute-done.6.za = f32[4,16,256]{2,1,0:T(8,128)S(1)} collective-permute-done((f32[4,16,256]{2,1,0:T(8,128)}, f32[4,16,256]{2,1,0:T(8,128)S(1)}, u32[]{:S(2)}, u32[]{:S(2)}) %collective-permute-start.6) | collective-permute-done | bytes 65568 | tf_op jit(solution)/shard_map/ppermute | solution.py:637
  62.6 0.7 collective-permute-start.7
  63.3 4.2 %collective-permute-done.7.zb = f32[4,16,256]{2,1,0:T(8,128)S(1)} collective-permute-done((f32[4,16,256]{2,1,0:T(8,128)}, f32[4,16,256]{2,1,0:T(8,128)S(1)}, u32[]{:S(2)}, u32[]{:S(2)}) %collective-permute-start.7) | collective-permute-done | bytes 65568 | tf_op jit(solution)/shard_map/ppermute | solution.py:637
  67.5 2.6 %collective-permute-start.8 = (f32[4,48,256]{2,1,0:T(8,128)S(1)}, f32[4,48,256]{2,1,0:T(8,128)S(1)}, u32[]{:S(2)}, u32[]{:S(2)}) collective-permute-start(f32[4,48,256]{2,1,0:T(8,128)S(1)} %get-tuple-element.43.refs_0_), channel_id=1, source_target_pairs={{0,96},{32,0},{64,32},{96,64},{1,97},{33,1},{65,33},{97,65},{2,98}... | collective-permute-start | bytes 589832 | tf_op jit(solution)/shard_map/ppermute | solution.py:637
  70.0 0.5 collective-permute-start.9
  70.6 0.6 collective-permute-start.10
  71.2 3.9 %collective-permute-done.8.refs_1_ = f32[4,48,256]{2,1,0:T(8,128)S(1)} collective-permute-done((f32[4,48,256]{2,1,0:T(8,128)S(1)}, f32[4,48,256]{2,1,0:T(8,128)S(1)}, u32[]{:S(2)}, u32[]{:S(2)}) %collective-permute-start.8) | collective-permute-done | bytes 196640 | tf_op jit(solution)/shard_map/ppermute | solution.py:637
  75.1 2.7 %collective-permute-start.11 = (f32[4,48,256]{2,1,0:T(8,128)S(1)}, f32[4,48,256]{2,1,0:T(8,128)S(1)}, u32[]{:S(2)}, u32[]{:S(2)}) collective-permute-start(f32[4,48,256]{2,1,0:T(8,128)S(1)} %get-tuple-element.44.refs_4_), channel_id=1, source_target_pairs={{0,24},{8,0},{16,8},{24,16},{1,25},{9,1},{17,9},{25,17},{2,26},{10... | collective-permute-start | bytes 589832 | tf_op jit(solution)/shard_map/ppermute | solution.py:637
  77.9 1.2 collective-permute-start.12
  79.1 0.9 collective-permute-start.13
  80.1 2.5 collective-permute-done.11.refs_5_
  82.6 0.1 collective-permute-start
  82.7 1.3 collective-permute-done.12.refs_6_
  84.0 5.7 %collective-permute-start.2 = (f32[1]{0:T(128)}, f32[1]{0:T(128)}, u32[]{:S(2)}, u32[]{:S(2)}) collective-permute-start(f32[1]{0:T(128)} %param.8), channel_id=1, source_target_pairs={{0,4},{4,0},{1,5},{5,1},{2,6},{6,2},{3,7},{7,3},{8,12},{12,8},{9,1... | collective-permute-start | bytes 20 | tf_op jit(solution)/shard_map/ppermute | solution.py:692
  89.7 0.6 join.1
  90.4 0.3 collective-permute-done.2
  90.8 2.4 collective-permute-start.18
  93.1 4.2 %collective-permute-start.20 = (f32[16,48,256]{2,1,0:T(8,128)S(1)}, f32[16,48,256]{2,1,0:T(8,128)}, u32[]{:S(2)}, u32[]{:S(2)}) collective-permute-start(f32[16,48,256]{2,1,0:T(8,128)S(1)} %get-tuple-element.46.rest_2_), channel_id=1, source_target_pairs={{0,96},{32,0},{64,32},{96,64},{1,97},{33,1},{65,33},{97,65},{2,98}... | collective-permute-start | bytes 2359304 | tf_op jit(solution)/shard_map/ppermute | solution.py:637
  98.0 3.6 %tables.1 = (bf16[4,256,256]{2,1,0:T(8,128)(2,1)}, bf16[4,256,256]{2,1,0:T(8,128)(2,1)}, bf16[4,256,256]{2,1,0:T(8,128)(2,1)}, bf16[4,256,256]{2,1,0:T(8,128)(2,...) custom-call(s32[4]{0:T(128)} %pad_add_fusion.4.ids), custom_call_target="tpu_custom_call" | custom-call | flops 31457280 | bytes 4194304 | tf_op jit(solution)/shard_map/tables/pallas_call | solution.py:94
  101.6 1.2 pad_maximum_fusion.ws
  102.9 1.3 slice.23
  104.2 1.0 collective-permute-start.24
  105.3 2.3 slice.24
  107.5 1.2 collective-permute-done.17.rest_2_
  108.8 0.3 collective-permute-start.25
  109.1 3.3 %collective-permute-start.22 = (f32[8,128,256]{2,1,0:T(8,128)S(1)}, f32[8,128,256]{2,1,0:T(8,128)}, u32[]{:S(2)}, u32[]{:S(2)}) collective-permute-start(f32[8,128,256]{2,1,0:T(8,128)S(1)} %slice.23), channel_id=1, source_target_pairs={{0,1},{1,2},{2,3},{3,128},{128,129},{129,130},{130,131},{131,0},{4... | collective-permute-start | bytes 3145736 | tf_op jit(solution)/shard_map/ppermute | solution.py:637
  112.3 0.8 collective-permute-done.19.rest_4_
  113.2 3.7 %collective-permute-start.23 = (f32[8,128,256]{2,1,0:T(8,128)}, f32[8,128,256]{2,1,0:T(8,128)}, u32[]{:S(2)}, u32[]{:S(2)}) collective-permute-start(f32[8,128,256]{2,1,0:T(8,128)} %slice.24), channel_id=1, source_target_pairs={{0,131},{1,0},{2,1},{3,2},{128,3},{129,128},{130,129},{131,130},{4... | collective-permute-start | bytes 3145736 | tf_op jit(solution)/shard_map/ppermute | solution.py:637
  116.9 18.6 %shard_map.77 = (f32[2,2,56,8,256]{4,3,2,1,0:T(8,128)}, f32[2,2,56,8,256]{4,3,2,1,0:T(8,128)}) custom-call(s32[4]{0:T(128)} %pad_add_fusion.4.ids, f32[2]{0:T(128)} %pad_maximum_fusion.ws, bf16[4,256,256]{2,1,0:T(8,128)(2,1)} %get-tuple-element.34.e1h, bf16[4,256,256]{2,1,0:T(8,128)(2,1)} %get-tuple-element.35.e1l, f32[24,8,128]{2,1,0:T(8,128)} %get-tuple-element.36.tw1, ...), custom_call_target="tpu_custom_call" | custom-call | flops 5637144576 | bytes 11010048 | tf_op jit(solution)/shard_map/pallas_call | solution.py:376
  135.5 15.2 %collective-permute-start.21 = (f32[2,2,56,8,256]{4,3,2,1,0:T(8,128)}, f32[2,2,56,8,256]{4,3,2,1,0:T(8,128)}, u32[]{:S(2)}, u32[]{:S(2)}) collective-permute-start(f32[2,2,56,8,256]{4,3,2,1,0:T(8,128)} %get-tuple-element.50), channel_id=1, source_target_pairs={{0,4},{4,0},{1,5},{5,1},{2,6},{6,2},{3,7},{7,3},{8,12},{12,8},{9,1... | collective-permute-start | bytes 5505032 | tf_op jit(solution)/shard_map/ppermute | solution.py:701
  150.8 0.7 scatter_custom_fusion.1
  151.6 1.5 scatter_fusion
  153.2 0.9 pad_add_fusion
  154.1 7.9 %all-to-all-start = ((s32[16,72,128]{2,1,0:T(8,128)}), s32[16,72,128]{2,1,0:T(8,128)}, u32[]{:S(2)}, u32[]{:S(2)}) async-start(s32[16,72,128]{2,1,0:T(8,128)} %pad_add_fusion), calls=%async_computation | async-start | bytes 1179648 | tf_op jit(solution)/shard_map/all_to_all | solution.py:690
  162.0 11.0 %shard_map.76 = (f32[2,2,28,8,256]{4,3,2,1,0:T(8,128)}, f32[2,2,28,8,256]{4,3,2,1,0:T(8,128)}) custom-call(s32[4]{0:T(128)} %pad_add_fusion.4.ids, f32[2]{0:T(128)} %pad_maximum_fusion.ws, bf16[4,256,256]{2,1,0:T(8,128)(2,1)} %get-tuple-element.34.e1h, bf16[4,256,256]{2,1,0:T(8,128)(2,1)} %get-tuple-element.35.e1l, f32[24,8,128]{2,1,0:T(8,128)} %get-tuple-element.36.tw1, ...), custom_call_target="tpu_custom_call" | custom-call | flops 2818572288 | bytes 5505024 | tf_op jit(solution)/shard_map/pallas_call | solution.py:376
  173.0 0.4 collective-permute-start.14
  173.4 11.0 %shard_map.78 = (f32[2,2,28,8,256]{4,3,2,1,0:T(8,128)}, f32[2,2,28,8,256]{4,3,2,1,0:T(8,128)}) custom-call(s32[4]{0:T(128)} %pad_add_fusion.4.ids, f32[2]{0:T(128)} %pad_maximum_fusion.ws, bf16[4,256,256]{2,1,0:T(8,128)(2,1)} %get-tuple-element.34.e1h, bf16[4,256,256]{2,1,0:T(8,128)(2,1)} %get-tuple-element.35.e1l, f32[24,8,128]{2,1,0:T(8,128)} %get-tuple-element.36.tw1, ...), custom_call_target="tpu_custom_call" | custom-call | flops 2818572288 | bytes 5505024 | tf_op jit(solution)/shard_map/pallas_call | solution.py:376
  184.4 0.3 collective-permute-start.26
  184.7 0.3 collective-permute-start.1
  185.0 7.9 %shard_map.74 = (f32[2,2,16,8,256]{4,3,2,1,0:T(8,128)}, f32[2,2,16,8,256]{4,3,2,1,0:T(8,128)}) custom-call(s32[4]{0:T(128)} %pad_add_fusion.4.ids, f32[2]{0:T(128)} %pad_maximum_fusion.ws, bf16[4,256,256]{2,1,0:T(8,128)(2,1)} %get-tuple-element.34.e1h, bf16[4,256,256]{2,1,0:T(8,128)(2,1)} %get-tuple-element.35.e1l, f32[24,8,128]{2,1,0:T(8,128)} %get-tuple-element.36.tw1, ...), custom_call_target="tpu_custom_call" | custom-call | flops 1610612736 | bytes 3145728 | tf_op jit(solution)/shard_map/pallas_call | solution.py:376
  192.9 0.3 collective-permute-start.3
  193.3 0.6 reshape.123.k1
  193.9 1.2 collective-permute-done.3.rest_1_
  195.2 0.8 copy-done.10
  196.0 0.2 copy-done.9
  196.1 0.3 copy-done.7
  196.4 0.3 copy-done.8
  196.7 16.8 %along_x.1 = (f32[128,8,128]{2,1,0:T(8,128)}, f32[128,8,128]{2,1,0:T(8,128)}) custom-call(s32[4]{0:T(128)} %pad_add_fusion.4.ids, f32[1,128]{1,0:T(1,128)} %reshape.123.k1, bf16[4,256,256]{2,1,0:T(8,128)(2,1)} %get-tuple-element.31.e2h, bf16[4,256,256]{2,1,0:T(8,128)(2,1)} %get-tuple-element.32.e2l, f32[2,12,128,128]{3,2,1,0:T(8,128)} %get-tuple-element.33.tw2, ...), custom_call_target="tpu_custom_call" | custom-call | flops 60000002048 | bytes 16777216 | tf_op jit(solution)/shard_map/along_x/pallas_call | solution.py:586
  213.5 0.3 collective-permute-start.27
  213.8 1.9 collective-permute-done.27
  215.7 1.9 add.118
  217.7 9.3 %all-to-all-start.1 = ((f32[16,64,128]{2,1,0:T(8,128)}), f32[16,64,128]{2,1,0:T(8,128)S(1)}, u32[]{:S(2)}, u32[]{:S(2)}) async-start(f32[16,64,128]{2,1,0:T(8,128)} %bitcast.16), calls=%async_computation.1 | async-start | bytes 1048576 | tf_op jit(solution)/shard_map/all_to_all | solution.py:725
  227.0 10.3 %all-to-all-done.1 = f32[16,64,128]{2,1,0:T(8,128)S(1)} async-done(((f32[16,64,128]{2,1,0:T(8,128)}), f32[16,64,128]{2,1,0:T(8,128)S(1)}, u32[]{:S(2)}, u32[]{:S(2)}) %all-to-all-start.1) | async-done | bytes 524320 | tf_op jit(solution)/shard_map/all_to_all | solution.py:725
  237.3 0.6 pick.1
  238.0 12.4 %collective-permute-start.28 = (f32[16,8,128]{2,1,0:T(8,128)S(1)}, f32[16,8,128]{2,1,0:T(8,128)S(1)}, u32[]{:S(2)}, u32[]{:S(2)}) collective-permute-start(f32[16,8,128]{2,1,0:T(8,128)S(1)} %get-tuple-element.56), channel_id=1, source_target_pairs={{0,128},{128,0},{1,129},{129,1},{2,130},{130,2},{3,131},{131,3},{4... | collective-permute-start | bytes 196616 | tf_op jit(solution)/shard_map/ppermute | solution.py:727
  250.3 1.7 collective-permute-done.28
  252.0 0.7 reshape.129
  (63 shorter events, 0.8 us)
Async XLA Ops:
  5.2 14.0 %copy-start.5 = (s32[16,1]{0,1:T(1,128)S(1)}, s32[16,1]{0,1:T(1,128)}, u32[]{:S(2)}) copy-start(s32[16,1]{0,1:T(1,128)} %param.11) | copy-start | bytes 196
  5.2 65.9 %copy-start.11 = (s32[16]{0:T(128)S(1)}, s32[16]{0:T(128)}, u32[]{:S(2)}) copy-start(s32[16]{0:T(128)} %param.10) | copy-start | bytes 196
  5.3 74.8 %copy-start.3 = (s32[16,2,512]{2,1,0:T(2,128)S(1)}, s32[16,2,512]{2,1,0:T(2,128)}, u32[]{:S(2)}) copy-start(s32[16,2,512]{2,1,0:T(2,128)} %param.12) | copy-start | bytes 196612
  5.3 84.4 %copy-start = (s32[4]{0:T(128)S(1)}, s32[4]{0:T(128)}, u32[]{:S(2)}) copy-start(s32[4]{0:T(128)} %pad_add_fusion.4.ids) | copy-start | bytes 52
  5.3 87.8 %collective-permute-start.15 = (f32[16,128,256]{2,1,0:T(8,128)}, f32[16,128,256]{2,1,0:T(8,128)}, u32[]{:S(2)}, u32[]{:S(2)}) collective-permute-start(f32[16,128,256]{2,1,0:T(8,128)} %shard_map.75.rest_0_), channel_id=1, source_target_pairs={{0,1},{1,2},{2,3},{3,128},{128,129},{129,130},{130,131},{131,0},{4... | collective-permute-start | bytes 6291464 | tf_op jit(solution)/shard_map/ppermute | solution.py:637
  7.8 96.4 %collective-permute-start.16 = (f32[16,128,256]{2,1,0:T(8,128)}, f32[16,128,256]{2,1,0:T(8,128)}, u32[]{:S(2)}, u32[]{:S(2)}) collective-permute-start(f32[16,128,256]{2,1,0:T(8,128)} %shard_map.75.rest_0_), channel_id=1, source_target_pairs={{0,131},{1,0},{2,1},{3,2},{128,3},{129,128},{130,129},{131,130},{4... | collective-permute-start | bytes 6291464 | tf_op jit(solution)/shard_map/ppermute | solution.py:637
  16.5 50.9 %collective-permute-start.4 = (f32[2,4,16,256]{3,2,1,0:T(8,128)}, f32[2,4,16,256]{3,2,1,0:T(8,128)S(1)}, u32[]{:S(2)}, u32[]{:S(2)}) collective-permute-start(f32[2,4,16,256]{3,2,1,0:T(8,128)} %get-tuple-element.40), channel_id=1, source_target_pairs={{0,1},{1,2},{2,3},{3,128},{128,129},{129,130},{130,131},{131,0},{4... | collective-permute-start | bytes 393224 | tf_op jit(solution)/shard_map/ppermute | solution.py:637
  16.6 50.9 %collective-permute-start.5 = (f32[2,4,16,256]{3,2,1,0:T(8,128)}, f32[2,4,16,256]{3,2,1,0:T(8,128)S(1)}, u32[]{:S(2)}, u32[]{:S(2)}) collective-permute-start(f32[2,4,16,256]{3,2,1,0:T(8,128)} %get-tuple-element.40), channel_id=1, source_target_pairs={{0,131},{1,0},{2,1},{3,2},{128,3},{129,128},{130,129},{131,130},{4... | collective-permute-start | bytes 393224 | tf_op jit(solution)/shard_map/ppermute | solution.py:637
  19.3 43.3 %collective-permute-start.6 = (f32[4,16,256]{2,1,0:T(8,128)}, f32[4,16,256]{2,1,0:T(8,128)S(1)}, u32[]{:S(2)}, u32[]{:S(2)}) collective-permute-start(f32[4,16,256]{2,1,0:T(8,128)} %get-tuple-element.41), channel_id=1, source_target_pairs={{0,2},{1,3},{2,128},{3,129},{128,130},{129,131},{130,0},{131,1},{4... | collective-permute-start | bytes 196616 | tf_op jit(solution)/shard_map/ppermute | solution.py:637
  62.6 4.9 %collective-permute-start.7 = (f32[4,16,256]{2,1,0:T(8,128)}, f32[4,16,256]{2,1,0:T(8,128)S(1)}, u32[]{:S(2)}, u32[]{:S(2)}) collective-permute-start(f32[4,16,256]{2,1,0:T(8,128)} %get-tuple-element.42), channel_id=1, source_target_pairs={{0,130},{1,131},{2,0},{3,1},{128,2},{129,3},{130,128},{131,129},{4... | collective-permute-start | bytes 196616 | tf_op jit(solution)/shard_map/ppermute | solution.py:637
  67.5 7.6 %collective-permute-start.8 = (f32[4,48,256]{2,1,0:T(8,128)S(1)}, f32[4,48,256]{2,1,0:T(8,128)S(1)}, u32[]{:S(2)}, u32[]{:S(2)}) collective-permute-start(f32[4,48,256]{2,1,0:T(8,128)S(1)} %get-tuple-element.43.refs_0_), channel_id=1, source_target_pairs={{0,96},{32,0},{64,32},{96,64},{1,97},{33,1},{65,33},{97,65},{2,98}... | collective-permute-start | bytes 589832 | tf_op jit(solution)/shard_map/ppermute | solution.py:637
  70.0 7.8 %collective-permute-start.9 = (f32[4,48,256]{2,1,0:T(8,128)S(1)}, f32[4,48,256]{2,1,0:T(8,128)S(1)}, u32[]{:S(2)}, u32[]{:S(2)}) collective-permute-start(f32[4,48,256]{2,1,0:T(8,128)S(1)} %get-tuple-element.43.refs_0_), channel_id=1, source_target_pairs={{0,64},{32,96},{64,0},{96,32},{1,65},{33,97},{65,1},{97,33},{2,66}... | collective-permute-start | bytes 589832 | tf_op jit(solution)/shard_map/ppermute | solution.py:637
  70.6 8.5 %collective-permute-start.10 = (f32[4,48,256]{2,1,0:T(8,128)S(1)}, f32[4,48,256]{2,1,0:T(8,128)S(1)}, u32[]{:S(2)}, u32[]{:S(2)}) collective-permute-start(f32[4,48,256]{2,1,0:T(8,128)S(1)} %get-tuple-element.43.refs_0_), channel_id=1, source_target_pairs={{0,32},{32,64},{64,96},{96,0},{1,33},{33,65},{65,97},{97,1},{2,34}... | collective-permute-start | bytes 589832 | tf_op jit(solution)/shard_map/ppermute | solution.py:637
  75.1 7.5 %collective-permute-start.11 = (f32[4,48,256]{2,1,0:T(8,128)S(1)}, f32[4,48,256]{2,1,0:T(8,128)S(1)}, u32[]{:S(2)}, u32[]{:S(2)}) collective-permute-start(f32[4,48,256]{2,1,0:T(8,128)S(1)} %get-tuple-element.44.refs_4_), channel_id=1, source_target_pairs={{0,24},{8,0},{16,8},{24,16},{1,25},{9,1},{17,9},{25,17},{2,26},{10... | collective-permute-start | bytes 589832 | tf_op jit(solution)/shard_map/ppermute | solution.py:637
  77.9 6.1 %collective-permute-start.12 = (f32[4,48,256]{2,1,0:T(8,128)S(1)}, f32[4,48,256]{2,1,0:T(8,128)S(1)}, u32[]{:S(2)}, u32[]{:S(2)}) collective-permute-start(f32[4,48,256]{2,1,0:T(8,128)S(1)} %get-tuple-element.44.refs_4_), channel_id=1, source_target_pairs={{0,16},{8,24},{16,0},{24,8},{1,17},{9,25},{17,1},{25,9},{2,18},{10... | collective-permute-start | bytes 589832 | tf_op jit(solution)/shard_map/ppermute | solution.py:637
  79.1 10.6 %collective-permute-start.13 = (f32[4,48,256]{2,1,0:T(8,128)S(1)}, f32[4,48,256]{2,1,0:T(8,128)S(1)}, u32[]{:S(2)}, u32[]{:S(2)}) collective-permute-start(f32[4,48,256]{2,1,0:T(8,128)S(1)} %get-tuple-element.44.refs_4_), channel_id=1, source_target_pairs={{0,8},{8,16},{16,24},{24,0},{1,9},{9,17},{17,25},{25,1},{2,10},{10... | collective-permute-start | bytes 589832 | tf_op jit(solution)/shard_map/ppermute | solution.py:637
  82.6 10.5 %collective-permute-start = (s32[17,8,128]{2,1,0:T(8,128)S(1)}, s32[17,8,128]{2,1,0:T(8,128)S(1)}, u32[]{:S(2)}, u32[]{:S(2)}) collective-permute-start(s32[17,8,128]{2,1,0:T(8,128)S(1)} %pad_add_fusion.2), channel_id=1, source_target_pairs={{0,128},{128,0},{1,129},{129,1},{2,130},{130,2},{3,131},{131,3},{4... | collective-permute-start | bytes 208904 | tf_op jit(solution)/shard_map/ppermute | solution.py:653
  84.0 6.7 %collective-permute-start.2 = (f32[1]{0:T(128)}, f32[1]{0:T(128)}, u32[]{:S(2)}, u32[]{:S(2)}) collective-permute-start(f32[1]{0:T(128)} %param.8), channel_id=1, source_target_pairs={{0,4},{4,0},{1,5},{5,1},{2,6},{6,2},{3,7},{7,3},{8,12},{12,8},{9,1... | collective-permute-start | bytes 20 | tf_op jit(solution)/shard_map/ppermute | solution.py:692
  90.3 17.2 %copy-start.2 = (f32[16,48,256]{2,1,0:T(8,128)}, f32[16,48,256]{2,1,0:T(8,128)S(1)}, u32[]{:S(2)}) copy-start(f32[16,48,256]{2,1,0:T(8,128)S(1)} %get-tuple-element.45.rest_1_) | copy-start | bytes 2359300
  90.3 18.5 %copy-start.1 = (f32[16,48,256]{2,1,0:T(8,128)}, f32[16,48,256]{2,1,0:T(8,128)S(1)}, u32[]{:S(2)}) copy-start(f32[16,48,256]{2,1,0:T(8,128)S(1)} %get-tuple-element.46.rest_2_) | copy-start | bytes 2359300
  90.3 18.4 %collective-permute-start.17 = (f32[16,48,256]{2,1,0:T(8,128)S(1)}, f32[16,48,256]{2,1,0:T(8,128)}, u32[]{:S(2)}, u32[]{:S(2)}) collective-permute-start(f32[16,48,256]{2,1,0:T(8,128)S(1)} %get-tuple-element.45.rest_1_), channel_id=1, source_target_pairs={{0,8},{8,16},{16,24},{24,0},{1,9},{9,17},{17,25},{25,1},{2,10},{10... | collective-permute-start | bytes 2359304 | tf_op jit(solution)/shard_map/ppermute | solution.py:637
  90.8 18.3 %collective-permute-start.18 = (f32[16,48,256]{2,1,0:T(8,128)S(1)}, f32[16,48,256]{2,1,0:T(8,128)}, u32[]{:S(2)}, u32[]{:S(2)}) collective-permute-start(f32[16,48,256]{2,1,0:T(8,128)S(1)} %get-tuple-element.45.rest_1_), channel_id=1, source_target_pairs={{0,24},{8,0},{16,8},{24,16},{1,25},{9,1},{17,9},{25,17},{2,26},{10... | collective-permute-start | bytes 2359304 | tf_op jit(solution)/shard_map/ppermute | solution.py:637
  93.1 20.1 %collective-permute-start.19 = (f32[16,48,256]{2,1,0:T(8,128)S(1)}, f32[16,48,256]{2,1,0:T(8,128)}, u32[]{:S(2)}, u32[]{:S(2)}) collective-permute-start(f32[16,48,256]{2,1,0:T(8,128)S(1)} %get-tuple-element.46.rest_2_), channel_id=1, source_target_pairs={{0,32},{32,64},{64,96},{96,0},{1,33},{33,65},{65,97},{97,1},{2,34}... | collective-permute-start | bytes 2359304 | tf_op jit(solution)/shard_map/ppermute | solution.py:637
  93.1 23.8 %collective-permute-start.20 = (f32[16,48,256]{2,1,0:T(8,128)S(1)}, f32[16,48,256]{2,1,0:T(8,128)}, u32[]{:S(2)}, u32[]{:S(2)}) collective-permute-start(f32[16,48,256]{2,1,0:T(8,128)S(1)} %get-tuple-element.46.rest_2_), channel_id=1, source_target_pairs={{0,96},{32,0},{64,32},{96,64},{1,97},{33,1},{65,33},{97,65},{2,98}... | collective-permute-start | bytes 2359304 | tf_op jit(solution)/shard_map/ppermute | solution.py:637
  104.2 68.8 %collective-permute-start.24 = (f32[16,48,256]{2,1,0:T(8,128)S(1)}, f32[16,48,256]{2,1,0:T(8,128)}, u32[]{:S(2)}, u32[]{:S(2)}) collective-permute-start(f32[16,48,256]{2,1,0:T(8,128)S(1)} %get-tuple-element.45.rest_1_), channel_id=1, source_target_pairs={{0,16},{8,24},{16,0},{24,8},{1,17},{9,25},{17,1},{25,9},{2,18},{10... | collective-permute-start | bytes 2359304 | tf_op jit(solution)/shard_map/ppermute | solution.py:637
  108.8 64.6 %collective-permute-start.25 = (f32[16,48,256]{2,1,0:T(8,128)S(1)}, f32[16,48,256]{2,1,0:T(8,128)}, u32[]{:S(2)}, u32[]{:S(2)}) collective-permute-start(f32[16,48,256]{2,1,0:T(8,128)S(1)} %get-tuple-element.46.rest_2_), channel_id=1, source_target_pairs={{0,64},{32,96},{64,0},{96,32},{1,65},{33,97},{65,1},{97,33},{2,66}... | collective-permute-start | bytes 2359304 | tf_op jit(solution)/shard_map/ppermute | solution.py:637
  109.1 64.3 %collective-permute-start.22 = (f32[8,128,256]{2,1,0:T(8,128)S(1)}, f32[8,128,256]{2,1,0:T(8,128)}, u32[]{:S(2)}, u32[]{:S(2)}) collective-permute-start(f32[8,128,256]{2,1,0:T(8,128)S(1)} %slice.23), channel_id=1, source_target_pairs={{0,1},{1,2},{2,3},{3,128},{128,129},{129,130},{130,131},{131,0},{4... | collective-permute-start | bytes 3145736 | tf_op jit(solution)/shard_map/ppermute | solution.py:637
  113.2 60.2 %collective-permute-start.23 = (f32[8,128,256]{2,1,0:T(8,128)}, f32[8,128,256]{2,1,0:T(8,128)}, u32[]{:S(2)}, u32[]{:S(2)}) collective-permute-start(f32[8,128,256]{2,1,0:T(8,128)} %slice.24), channel_id=1, source_target_pairs={{0,131},{1,0},{2,1},{3,2},{128,3},{129,128},{130,129},{131,130},{4... | collective-permute-start | bytes 3145736 | tf_op jit(solution)/shard_map/ppermute | solution.py:637
  135.5 59.7 %collective-permute-start.21 = (f32[2,2,56,8,256]{4,3,2,1,0:T(8,128)}, f32[2,2,56,8,256]{4,3,2,1,0:T(8,128)}, u32[]{:S(2)}, u32[]{:S(2)}) collective-permute-start(f32[2,2,56,8,256]{4,3,2,1,0:T(8,128)} %get-tuple-element.50), channel_id=1, source_target_pairs={{0,4},{4,0},{1,5},{5,1},{2,6},{6,2},{3,7},{7,3},{8,12},{12,8},{9,1... | collective-permute-start | bytes 5505032 | tf_op jit(solution)/shard_map/ppermute | solution.py:701
  154.1 30.7 %all-to-all-start = ((s32[16,72,128]{2,1,0:T(8,128)}), s32[16,72,128]{2,1,0:T(8,128)}, u32[]{:S(2)}, u32[]{:S(2)}) async-start(s32[16,72,128]{2,1,0:T(8,128)} %pad_add_fusion), calls=%async_computation | async-start | bytes 1179648 | tf_op jit(solution)/shard_map/all_to_all | solution.py:690
  173.0 22.1 %collective-permute-start.14 = (f32[2,2,28,8,256]{4,3,2,1,0:T(8,128)}, f32[2,2,28,8,256]{4,3,2,1,0:T(8,128)S(1)}, u32[]{:S(2)}, u32[]{:S(2)}) collective-permute-start(f32[2,2,28,8,256]{4,3,2,1,0:T(8,128)} %get-tuple-element.48), channel_id=1, source_target_pairs={{0,4},{4,0},{1,5},{5,1},{2,6},{6,2},{3,7},{7,3},{8,12},{12,8},{9,1... | collective-permute-start | bytes 2752520 | tf_op jit(solution)/shard_map/ppermute | solution.py:701
  184.4 10.7 %collective-permute-start.26 = (f32[2,2,28,8,256]{4,3,2,1,0:T(8,128)}, f32[2,2,28,8,256]{4,3,2,1,0:T(8,128)S(1)}, u32[]{:S(2)}, u32[]{:S(2)}) collective-permute-start(f32[2,2,28,8,256]{4,3,2,1,0:T(8,128)} %get-tuple-element.52), channel_id=1, source_target_pairs={{0,4},{4,0},{1,5},{5,1},{2,6},{6,2},{3,7},{7,3},{8,12},{12,8},{9,1... | collective-permute-start | bytes 2752520 | tf_op jit(solution)/shard_map/ppermute | solution.py:701
  184.7 10.4 %collective-permute-start.1 = (s32[16,72,128]{2,1,0:T(8,128)}, s32[16,72,128]{2,1,0:T(8,128)S(1)}, u32[]{:S(2)}, u32[]{:S(2)}) collective-permute-start(s32[16,72,128]{2,1,0:T(8,128)} %all-to-all-done.pos_a), channel_id=1, source_target_pairs={{0,4},{4,0},{1,5},{5,1},{2,6},{6,2},{3,7},{7,3},{8,12},{12,8},{9,1... | collective-permute-start | bytes 1769480 | tf_op jit(solution)/shard_map/ppermute | solution.py:691
  185.0 8.2 %copy-start.6 = (f32[16,8]{0,1:T(8,128)S(1)}, f32[16,8]{0,1:T(8,128)}, u32[]{:S(2)}) copy-start(f32[16,8]{0,1:T(8,128)} %param.9) | copy-start | bytes 1540
  192.9 2.2 collective-permute-start.3
  195.1 0.8 copy-start.10
  195.1 1.0 copy-start.9
  195.1 1.3 copy-start.7
  195.2 1.5 copy-start.8
  213.5 13.4 %copy-start.4 = (f32[16,2,512]{2,1,0:T(2,128)S(1)}, f32[16,2,512]{2,1,0:T(2,128)}, u32[]{:S(2)}) copy-start(f32[16,2,512]{2,1,0:T(2,128)} %param.13) | copy-start | bytes 196612
  213.5 2.2 collective-permute-start.27
  217.7 19.7 %all-to-all-start.1 = ((f32[16,64,128]{2,1,0:T(8,128)}), f32[16,64,128]{2,1,0:T(8,128)S(1)}, u32[]{:S(2)}, u32[]{:S(2)}) async-start(f32[16,64,128]{2,1,0:T(8,128)} %bitcast.16), calls=%async_computation.1 | async-start | bytes 1048576 | tf_op jit(solution)/shard_map/all_to_all | solution.py:725
  238.0 14.0 %collective-permute-start.28 = (f32[16,8,128]{2,1,0:T(8,128)S(1)}, f32[16,8,128]{2,1,0:T(8,128)S(1)}, u32[]{:S(2)}, u32[]{:S(2)}) collective-permute-start(f32[16,8,128]{2,1,0:T(8,128)S(1)} %get-tuple-element.56), channel_id=1, source_target_pairs={{0,128},{128,0},{1,129},{129,1},{2,130},{130,2},{3,131},{131,3},{4... | collective-permute-start | bytes 196616 | tf_op jit(solution)/shard_map/ppermute | solution.py:727

commit v3 on v2

--- a/solution.py
+++ b/solution.py
@@ -25,6 +25,10 @@
 MAGIC = 12582912.0
 
 
+def place_ids():
+    return tuple(lax.axis_index(n) for n in ("core", "wa", "x", "y"))
+
+
 def horner(z, coefs):
     acc = jnp.full_like(z, coefs[-1])
     for c in coefs[-2::-1]:
@@ -50,10 +54,12 @@
     return jnp.dot(a, b, preferred_element_type=F32)
 
 
-def tables_kernel(ids, e1h, e1l, e2h, e2l, tw1, tw2):
+def tables_kernel(e1h, e1l, e2h, e2l, tw1, tw2):
     row = lax.broadcasted_iota(jnp.int32, (128, 128), 0)
     col = lax.broadcasted_iota(jnp.int32, (128, 128), 1)
     lane = lax.broadcasted_iota(jnp.int32, (8, 128), 1)
+
+    ids = place_ids()
 
     def cs(k):
         return cis_turns((k & (N - 1)).astype(F32) * (1.0 / N))
@@ -63,8 +69,8 @@
         h[i, 128 * r : 128 * r + 128, 128 * c : 128 * c + 128] = a
         l[i, 128 * r : 128 * r + 128, 128 * c : 128 * c + 128] = b
 
-    for p in range(4):
-        y = 16 * (127 - row if p > 1 else row) + 4 * p
+    def matrices(p, carry):
+        y = 16 * jnp.where(p > 1, 127 - row, row) + 4 * p
         c, s = cs(col * y)
         ch, sh = split(c), split(s)
         put(e1h, e1l, p, 0, 0, ch)
@@ -77,33 +83,38 @@
         put(e2h, e2l, p, 1, 1, ch)
         put(e2h, e2l, p, 0, 1, sh)
         put(e2h, e2l, p, 1, 0, (-sh[0], -sh[1]))
-    for q in range(1, 4):
-        for j in range(4):
-            k = 4 * (q - 1) + j
-            c, s = cs((512 * ids[1] + 128 * j + lane) * q)
-            tw1[2 * k] = c
-            tw1[2 * k + 1] = -s
-            c, s = cs((128 * j + row) * q)
-            tw2[0, k] = c
-            tw2[1, k] = -s
-
-
-def tables(ids):
+        return carry
+
+    def factors(k, carry):
+        q, j = 1 + (k >> 2), k & 3
+        c, s = cs((512 * ids[1] + 128 * j + lane) * q)
+        tw1[2 * k] = c
+        tw1[2 * k + 1] = -s
+        c, s = cs((128 * j + row) * q)
+        tw2[0, k] = c
+        tw2[1, k] = -s
+        return carry
+
+    lax.fori_loop(0, 4, matrices, 0)
+    lax.fori_loop(0, 12, factors, 0)
+
+
+def tables():
     sds = jax.ShapeDtypeStruct
     shapes = [sds((4, 256, 256), BF16)] * 4 + [sds((24, 8, 128), F32), sds((2, 12, 128, 128), F32)]
     return pl.pallas_call(
         tables_kernel,
         out_shape=shapes,
-        in_specs=[SMEM],
         out_specs=[VMEM] * 6,
         cost_estimate=pl.CostEstimate(flops=60 * 16 * 2 * 16384, bytes_accessed=4 << 20, transcendentals=0),
         name="tables",
-    )(ids)
-
-
-def turn_kernel(b, ids, sky, own, *rest):
+    )()
+
+
+def turn_kernel(b, sky, own, *rest):
+    core, _, xc, yc = place_ids()
     outs, (xin, t, tmp, sem_in, sem_out) = rest[:-5], rest[-5:]
-    core, xc, yc = ids[0], ids[2], ids[3]
+    own, outs = ((own,), outs) if b == 0 else ((own, outs[0]), ())
     loads = []
     for c in range(2):
         col = pl.multiple_of(256 * core + 128 * b, 128)
@@ -115,20 +126,29 @@
         moves.append(pltpu.make_async_copy(src, dst, sem_out.at[len(moves)]))
         moves[-1].start()
 
+    def part(y4):
+        return own[0].at[pl.ds(4 * y4, 4)] if b == 0 else own[y4 // 2].at[pl.ds(4 * (y4 % 2), 4)]
+
     rev = 127 - lax.broadcasted_iota(jnp.int32, (128, 128), 1)
-    for y0 in range(16):
-        for c in range(2):
-            if y0 == 0:
-                loads[c].wait()
-            v = xin[c, pl.ds(y0, 128, stride=16), :].T
-            if y0 > 7:
-                v = jnp.take_along_axis(v, rev, axis=1)
-            z = 2 * (y0 % 2) + c
-            tmp[z] = v
-            for j0 in range(16):
-                t[y0, 8 * j0 : 8 * j0 + 8, 128 * c : 128 * c + 128] = tmp[z, pl.ds(j0, 8, stride=16), :]
-        if y0 % 4 == 3 and y0 < 15:
-            move(t.at[pl.ds(y0 - 3, 4)], own.at[pl.ds(y0 - 3, 4)])
+    for c in range(2):
+        loads[c].wait()
+    for y4 in range(4):
+        def group(i, carry, y4=y4):
+            for e in range(2):
+                y0 = 4 * y4 + 2 * i + e
+                for c in range(2):
+                    v = xin[c, pl.ds(y0, 128, stride=16), :].T
+                    if y4 > 1:
+                        v = jnp.take_along_axis(v, rev, axis=1)
+                    z = 2 * e + c
+                    tmp[z] = v
+                    for j0 in range(16):
+                        t[y0, 8 * j0 : 8 * j0 + 8, 128 * c : 128 * c + 128] = tmp[z, pl.ds(j0, 8, stride=16), :]
+            return carry
+
+        lax.fori_loop(0, 2, group, 0)
+        if y4 < 3:
+            move(t.at[pl.ds(4 * y4, 4)], part(y4))
     if outs:
         a_src = t.at[pl.ds(4 * xc, 4), pl.ds(pl.multiple_of(R * yc, 8), R), :]
         b_src = t.at[pl.ds(4 * yc, 4), pl.ds(pl.multiple_of(4 * R + R * xc, 8), R), :]
@@ -137,17 +157,17 @@
         move(b_src, ab.at[1])
         move(a_src, pa)
         move(b_src, pb)
-    move(t.at[pl.ds(12, 4)], own.at[pl.ds(12, 4)])
+    move(t.at[pl.ds(12, 4)], part(3))
     for m in moves:
         m.wait()
 
 
-def turn(b, ids, sky):
+def turn(b, sky):
     sds = lambda *d: jax.ShapeDtypeStruct(d, F32)
-    outs = [sds(16, 128, 256)] + [sds(2, 4, R, 256), sds(4, R, 256), sds(4, R, 256)] * (1 - b)
+    outs = [sds(8, 128, 256)] * 2 if b else [sds(16, 128, 256), sds(2, 4, R, 256), sds(4, R, 256), sds(4, R, 256)]
     return pl.pallas_call(
         functools.partial(turn_kernel, b),
-        in_specs=[SMEM, HBM],
+        in_specs=[HBM],
         out_specs=[HBM] * len(outs),
         out_shape=outs,
         scratch_shapes=[
@@ -158,7 +178,7 @@
             pltpu.SemaphoreType.DMA((8,)),
         ],
         cost_estimate=pl.CostEstimate(flops=1 << 22, bytes_accessed=4 << 20, transcendentals=0),
-    )(ids, sky)
+    )(sky)
 
 
 def gather3_kernel(zl, zr, za, zb, oa, ob):
@@ -180,22 +200,23 @@
     )(*z)
 
 
-def join_kernel(ids, *refs):
+def join_kernel(*refs):
+    ids = place_ids()
     for k in range(4):
         for base, ref, o in ((ids[2], refs[k], refs[8]), (ids[3], refs[4 + k], refs[9])):
             o[pl.ds(4 * ((base + k) & 3), 4)] = ref[...]
 
 
-def join(ids, a, b):
+def join(a, b):
     return pl.pallas_call(
         join_kernel,
         out_shape=[jax.ShapeDtypeStruct((16, 3 * R, 256), F32)] * 2,
-        in_specs=[SMEM] + [VMEM] * 8,
+        in_specs=[VMEM] * 8,
         out_specs=[VMEM] * 2,
         compiler_params=pltpu.CompilerParams(vmem_limit_bytes=16 << 20),
         cost_estimate=pl.CostEstimate(flops=1 << 20, bytes_accessed=3 << 20, transcendentals=0),
         name="join",
-    )(ids, *a, *b)
+    )(*a, *b)
 
 
 def slab_of(kind, k, ids):
@@ -213,22 +234,18 @@
     return [(slab_of(kind, k, ids), first, R // 8) for k in range(3)]
 
 
-def along_y_kernel(plan, n_src, ids, ws, e1h, e1l, tw1, *rest):
+def along_y_kernel(plan, n_src, w_own, w_other, e1h, e1l, tw1, *rest):
+    ids = place_ids()
     srcs = rest[:n_src]
     keep, send = rest[n_src : n_src + 2]
     eh, el, tw, xin, xh0, xl0, yb0, xh1, xl1, yb1, gb, cs, tab, where, sem_e, sem_in, sem_out = rest[n_src + 2 :]
     core = ids[0]
     lane = lax.broadcasted_iota(jnp.int32, (8, 128), 1)
     sub = lax.broadcasted_iota(jnp.int32, (8, 128), 0)
-    w = [ws[core], ws[1 - core]]
+    w = [jnp.where(core == pi, w_own[0], w_other[0]) for pi in range(2)]
     n_pairs = sum(blk["rows"] for blk in plan) // 16
     steps = n_pairs // 2
 
-    e_copies = [
-        pltpu.make_async_copy(src, dst, sem_e.at[i]) for i, (src, dst) in enumerate(((e1h, eh), (e1l, el), (tw1, tw)))
-    ]
-    for c in e_copies:
-        c.start()
     kinds, k = [], 0
     for blk in plan:
         if blk["src"] not in kinds:
@@ -267,8 +284,12 @@
     for k in range(min(2, steps)):
         for a in range(2):
             load(2 * k + a, k, a)
+
+    e_copies = [
+        pltpu.make_async_copy(src, dst, sem_e.at[i]) for i, (src, dst) in enumerate(((e1h, eh), (e1l, el), (tw1, tw)))
+    ]
     for c in e_copies:
-        c.wait()
+        c.start()
 
     def image(pair, slot, s, xh, xl):
         for a in range(2):
@@ -301,24 +322,33 @@
             x = xh[p]
             yb[p] = bdot(x, eh[p]) + bdot(xl[p], eh[p]) + bdot(x, el[p])
 
+    def short_one(slot, s, yb, a, pi):
+        sums = None
+        for q in range(4):
+            r0 = 64 * a + 16 * q + 8 * pi
+            rows = pl.ds(r0 if isinstance(r0, int) else pl.multiple_of(r0, 8), 8)
+            v = butterfly4([(yb[p, rows, 0:128], yb[p, rows, 128:256]) for p in range(4)])
+            if q:
+                out = []
+                for j, (r, i) in enumerate(v):
+                    k = 8 * (q - 1) + 2 * j
+                    out.append((r * tw[k] - i * tw[k + 1], r * tw[k + 1] + i * tw[k]))
+                v = out
+            sums = v if sums is None else [(x + u, y + z) for (x, y), (u, z) in zip(sums, v)]
+        for j, (vr, vi) in enumerate(sums):
+            cc = slice(128 * (j % 2), 128 * (j % 2) + 128)
+            gb[slot, s, j // 2, pi, 0, a, :, cc] = vr
+            gb[slot, s, j // 2, pi, 1, a, :, cc] = vi
+
     def short_part(slot, s, yb):
         for a in range(2):
             for pi in range(2):
-                sums = None
-                for q in range(4):
-                    r0 = 64 * a + 16 * q + 8 * pi
-                    v = butterfly4([(yb[p, r0 : r0 + 8, 0:128], yb[p, r0 : r0 + 8, 128:256]) for p in range(4)])
-                    if q:
-                        out = []
-                        for j, (r, i) in enumerate(v):
-                            k = 8 * (q - 1) + 2 * j
-                            out.append((r * tw[k] - i * tw[k + 1], r * tw[k + 1] + i * tw[k]))
-                        v = out
-                    sums = v if sums is None else [(x + u, y + z) for (x, y), (u, z) in zip(sums, v)]
-                for j, (vr, vi) in enumerate(sums):
-                    cc = slice(128 * (j % 2), 128 * (j % 2) + 128)
-                    gb[slot, s, j // 2, pi, 0, a, :, cc] = vr
-                    gb[slot, s, j // 2, pi, 1, a, :, cc] = vi
+                short_one(slot, s, yb, a, pi)
+
+    def short_tail(i, carry):
+        for s, yb in enumerate((yb0, yb1)):
+            short_one((steps - 1) % 2, s, yb, i >> 1, i & 1)
+        return carry
 
     def step(k, slot3):
         @pl.when(k >= 2)
@@ -349,7 +379,20 @@
         image(2 * k + 1, slot3, 1, xh1, xl1)
         return jnp.where(slot3 == 2, 0, slot3 + 1)
 
-    lax.fori_loop(0, steps, step, jnp.int32(0))
+    def arrived(slot):
+        for a in range(2):
+            pltpu.make_async_copy(xin.at[slot, a], xin.at[slot, a], sem_in.at[slot, a]).wait()
+
+    if steps > 2:
+        for a in range(2):
+            load(4 + a, 2, a)
+    arrived(0)
+    image(0, 0, 0, xh0, xl0)
+    for c in e_copies:
+        c.wait()
+    long_part(xh0, xl0, yb0)
+    image(1, 0, 1, xh1, xl1)
+    lax.fori_loop(1, steps, step, jnp.int32(1))
     last = (steps - 1) % 2
     if steps >= 2:
         for c in stores(steps - 2, steps % 2):
@@ -358,8 +401,7 @@
         for c in stores(steps - 3, last):
             c.wait()
     long_part(xh1, xl1, yb1)
-    short_part(last, 0, yb0)
-    short_part(last, 1, yb1)
+    lax.fori_loop(0, 4, short_tail, 0)
     for c in stores(steps - 1, last):
         c.start()
     if steps >= 2:
@@ -369,7 +411,7 @@
         c.wait()
 
 
-def along_y(plan, ids, ws, e1, srcs):
+def along_y(plan, ws, e1, srcs):
     total = sum(blk["rows"] for blk in plan)
     out = jax.ShapeDtypeStruct((2, 2, total // 8, 8, 256), F32)
     stage = [pltpu.VMEM((4, 128, 256), BF16), pltpu.VMEM((4, 128, 256), BF16), pltpu.VMEM((4, 128, 256), F32)]
@@ -393,10 +435,11 @@
             pltpu.SemaphoreType.DMA((3, 2)),
             pltpu.SemaphoreType.DMA((2, 2, 2)),
         ],
+        compiler_params=pltpu.CompilerParams(vmem_limit_bytes=67043328),
         cost_estimate=pl.CostEstimate(
             flops=total * 2 * 16 * 3 * 256 * 256 * 2, bytes_accessed=total * 24 * 1024, transcendentals=0
         ),
-    )(ids, ws, *e1, *srcs)
+    )(*ws, *e1, *srcs)
 
 
 def butterfly4(v):
@@ -419,15 +462,17 @@
     return out
 
 
-def along_x_kernel(plans, ids, k1, e2h, e2l, tw2, pos_a, pos_b, *rest):
+def along_x_kernel(plans, kt, e2h, e2l, tw2, pos_a, pos_b, *rest):
+    ids = place_ids()
     n = len(plans)
     parts = rest[: 2 * n]
     out_a, out_b = rest[2 * n : 2 * n + 2]
     eh, el, tw, pv, d, f0, f1, grid = rest[2 * n + 2 : 2 * n + 10]
     bufs = [rest[2 * n + 10 + 4 * k : 2 * n + 14 + 4 * k] for k in range(4)]
-    res, lst, notes, sem, sem_e, sem_o = rest[2 * n + 26 :]
+    res, wide, lst, notes, sem, sem_e, sem_o = rest[2 * n + 26 :]
     f = (f0, f1)
     core = ids[0]
+    loads = []
     for i, plan in enumerate(plans):
         off = 0
         for blk in plan:
@@ -435,9 +480,12 @@
                 base = 32 * slab + 8 * (first >> 7)
                 for ref, side in ((parts[2 * i], core), (parts[2 * i + 1], 1 - core)):
                     at = pl.ds(pl.multiple_of(base + 16 * side, 8), 8)
-                    dst = d.at[:, :, pl.ds((first >> 3) & 15, cnt), at, :]
-                    pltpu.make_async_copy(ref.at[:, :, pl.ds(off, cnt)], dst, sem).start()
+                    loads.append((ref, off, cnt, (first >> 3) & 15, at))
                 off += cnt
+    for pi in range(2):
+        for ref, off, cnt, j0, at in loads:
+            dst = d.at[pi, :, pl.ds(j0, cnt), at, :]
+            pltpu.make_async_copy(ref.at[pi, :, pl.ds(off, cnt)], dst, sem.at[pi]).start()
     last8 = pl.ds(64, 8)
     notice = [
         pltpu.make_async_copy(src.at[:, last8, :], notes.at[i], sem_o.at[i]) for i, src in enumerate((pos_a, pos_b))
@@ -470,7 +518,7 @@
         lst[count + k] = last
     for c in small:
         c.wait()
-    pltpu.make_async_copy(d, d, sem).wait()
+    pltpu.make_async_copy(d.at[0], d.at[0], sem.at[0]).wait()
 
     def first(pi, k, qs=range(4)):
         for q in qs:
@@ -500,16 +548,20 @@
         return carry
 
     def stage2(k, carry):
-        second(1, 2 * k)
-        second(1, 2 * k + 1)
+        second(1, k)
         return carry
 
     lax.fori_loop(0, 4, stage0, 0)
+    pltpu.make_async_copy(d.at[1], d.at[1], sem.at[1]).wait()
     lax.fori_loop(0, 4, stage1, 0)
-    lax.fori_loop(0, 8, stage2, 0)
+    lax.fori_loop(0, 16, stage2, 0)
 
     sub = lax.broadcasted_iota(jnp.int32, (8, 128), 0)
-    table = jnp.broadcast_to(k1[...], (8, 128))
+    lane = lax.broadcasted_iota(jnp.int32, (8, 128), 1)
+    wide[...] = jnp.zeros_like(wide)
+    wide[:, 0:16] = kt[...]
+    spread = jnp.take_along_axis(wide[...], lane >> 3, axis=1)
+    table = jnp.broadcast_to(jnp.sum(jnp.where(sub == (lane & 7), spread, 0.0), axis=0, keepdims=True), (8, 128))
 
     def taps(row):
         row = jnp.broadcast_to(row, (8, 128))
@@ -576,7 +628,7 @@
         m.wait()
 
 
-def along_x(plans, ids, k1, e2, pos_a, pos_b, parts):
+def along_x(plans, kt, e2, pos_a, pos_b, parts):
     buf = [
         pltpu.VMEM((256, 512), BF16),
         pltpu.VMEM((128, 512), BF16),
@@ -586,7 +638,7 @@
     return pl.pallas_call(
         functools.partial(along_x_kernel, plans),
         out_shape=[jax.ShapeDtypeStruct((128, 8, 128), F32)] * 2,
-        in_specs=[SMEM, VMEM] + [HBM] * (5 + len(parts)),
+        in_specs=[VMEM] + [HBM] * (5 + len(parts)),
         out_specs=[HBM, HBM],
         scratch_shapes=[
             pltpu.VMEM((4, 256, 256), BF16),
@@ -602,15 +654,64 @@
             *buf,
             *buf,
             pltpu.VMEM((256, 8, 128), F32),
+            pltpu.VMEM((8, 128), F32),
             pltpu.SMEM((272,), jnp.int32),
             pltpu.SMEM((2, 16, 8, 128), jnp.int32),
-            pltpu.SemaphoreType.DMA,
+            pltpu.SemaphoreType.DMA((2,)),
             pltpu.SemaphoreType.DMA((5,)),
             pltpu.SemaphoreType.DMA((2,)),
         ],
+        compiler_params=pltpu.CompilerParams(vmem_limit_bytes=67043328),
         cost_estimate=pl.CostEstimate(flops=60_000_000_000, bytes_accessed=16 << 20, transcendentals=0),
         name="along_x",
-    )(ids, k1, *e2, pos_a, pos_b, *parts)
+    )(kt, *e2, pos_a, pos_b, *parts)
+
+
+def arrange_kernel(mine, got, payload, here, there, blocks, notes, sem):
+    zh = lax.axis_index("zh")
+    copies = []
+    for i, src in enumerate((mine, got)):
+        copies.append(pltpu.make_async_copy(src.at[pl.ds(0, 16)], blocks.at[i], sem.at[2 * i]))
+        copies.append(pltpu.make_async_copy(src.at[16], notes.at[i], sem.at[2 * i + 1]))
+    for c in copies:
+        c.start()
+    for c in copies:
+        c.wait()
+    payload[:, 64:72, :] = jnp.zeros((16, 8, 128), jnp.int32)
+    lane = lax.broadcasted_iota(jnp.int32, (8, 128), 1)
+    for i, (out, home) in enumerate(((here, zh), (there, 1 - zh))):
+        def one(b, carry, i=i, out=out, home=home):
+            slot, tile = notes[i, 0, b], notes[i, 1, b]
+            mine = (slot >> 6) == zh
+            chip, k = (slot >> 2) & 15, 4 * home + (slot & 3)
+            out[b] = jnp.where(mine, 8 * chip + k, -1)
+
+            @pl.when(mine)
+            def _():
+                payload[chip, pl.ds(pl.multiple_of(8 * k, 8), 8), :] = blocks[i, b]
+                payload[chip, 64:72, :] = jnp.where(lane == k, tile, payload[chip, 64:72, :])
+
+            return carry
+
+        lax.fori_loop(0, 16, one, 0)
+
+
+def arrange(mine, got):
+    i32 = jnp.int32
+    return pl.pallas_call(
+        arrange_kernel,
+        out_shape=[jax.ShapeDtypeStruct((16, 72, 128), i32)] + [jax.ShapeDtypeStruct((16,), i32)] * 2,
+        in_specs=[HBM, HBM],
+        out_specs=[VMEM, SMEM, SMEM],
+        scratch_shapes=[
+            pltpu.VMEM((2, 16, 8, 128), i32),
+            pltpu.SMEM((2, 8, 128), i32),
+            pltpu.SemaphoreType.DMA((4,)),
+        ],
+        compiler_params=pltpu.CompilerParams(vmem_limit_bytes=8 << 20),
+        cost_estimate=pl.CostEstimate(flops=1 << 20, bytes_accessed=1 << 20, transcendentals=0),
+        name="arrange",
+    )(mine, got)
 
 
 def pick_kernel(here, there, answers, observed, rest, other):
@@ -639,11 +740,8 @@
 
 def shards(sky, plane_w, kernel, tile_ids, plane_ids, positions, observed):
     i32 = jnp.int32
-    core = lax.axis_index("core")
-    ids = jnp.stack([core, lax.axis_index("wa"), lax.axis_index("x"), lax.axis_index("y")]).astype(i32)
     z_axes = ("zh", "wa")
     swap = [(0, 1), (1, 0)]
-    zh = lax.axis_index("zh")
 
     target = plane_ids[:, 0]
     same = (target[:, None] == target[None, :]).astype(i32)
@@ -652,16 +750,18 @@
     mine0 = jnp.concatenate([positions.reshape(16, 8, 128), notes[None]], axis=0)
     got0 = lax.ppermute(mine0, "zh", swap)
 
-    own0, ab, pa, pb = turn(0, ids, sky)
+    own0, ab, pa, pb = turn(0, sky)
     zl = shift(ab, z_axes, 8, 1)
     zr = shift(ab, z_axes, 8, -1)
     za = shift(pa, z_axes, 8, 2)
     zb = shift(pb, z_axes, 8, -2)
-    (own1,) = turn(1, ids, sky)
-    cl = shift(own1, z_axes, 8, 1)
-    cr = shift(own1, z_axes, 8, -1)
-    cf_lo = shift(cl[:8], z_axes, 8, 1)
-    cf_hi = shift(cr[8:], z_axes, 8, -1)
+    lo, hi = turn(1, sky)
+    cl_lo = shift(lo, z_axes, 8, 1)
+    cr_hi = shift(hi, z_axes, 8, -1)
+    cl_hi = shift(hi, z_axes, 8, 1)
+    cr_lo = shift(lo, z_axes, 8, -1)
+    cf_lo = shift(cl_lo, z_axes, 8, 1)
+    cf_hi = shift(cr_hi, z_axes, 8, -1)
 
     mine_a, mine_b = gather3(zl, zr, za, zb)
 
@@ -671,32 +771,21 @@
         return r, shift(x, axis, 4, 2), l
 
     ax, bx = three(mine_a, "x"), three(mine_b, "y")
-    a0, b0 = join(ids, (mine_a,) + ax, (mine_b,) + bx)
+    a0, b0 = join((mine_a,) + ax, (mine_b,) + bx)
     ar, af, al = three(a0, "y")
     br, bf, bl = three(b0, "x")
 
-    def place(sl, home):
-        return jnp.where((sl >> 6) == zh, (((sl >> 2) & 15) * 2 + home) * 4 + (sl & 3), -1)
-
-    here, there = place(slot, zh), place(got0[16, 0, :16], 1 - zh)
-    dst = jnp.concatenate([here, there])
-    dst = jnp.where(dst < 0, 128 + jnp.arange(32, dtype=i32), dst)
-    pos = jnp.concatenate([mine0[:16], got0[:16]])
-    tile = jnp.concatenate([tile_ids + 1, got0[16, 1, :16]])
-    slot_pos = jnp.zeros((128, 8, 128), i32).at[dst].set(pos, unique_indices=True, mode="drop")
-    slot_tile = jnp.zeros((128,), i32).at[dst].set(tile, unique_indices=True, mode="drop")
-    tile_row = jnp.pad(slot_tile.reshape(16, 1, 8), ((0, 0), (0, 7), (0, 120)))
-    payload = jnp.concatenate([slot_pos.reshape(16, 64, 128), tile_row], axis=1)
+    payload, here, there = arrange(mine0, got0)
     asked = lax.all_to_all(payload, ("x", "y"), split_axis=0, concat_axis=0, tiled=True)
     asked_b = lax.ppermute(asked, "core", swap)
     other_w = lax.ppermute(plane_w, "core", swap)
-    ws = jnp.concatenate([plane_w, other_w])
-    *e1, tw1, tw2 = tables(ids)
+    ws = plane_w, other_w
+    *e1, tw1, tw2 = tables()
     e1, e2 = e1[:2] + [tw1], e1[2:] + [tw2]
     plans, parts = [], []
 
     def call(plan, srcs):
-        keep, send = along_y(plan, ids, ws, e1, srcs)
+        keep, send = along_y(plan, ws, e1, srcs)
         plans.append(plan)
         parts.extend([keep, lax.ppermute(send, "core", swap)])
 
@@ -704,22 +793,21 @@
         return dict(kind=kind, d=d, rows=rows, row=row, src=src)
 
     call([blk("own", 0, 128, 0, 0)], [own0])
-    call([blk("own", 128, 128, 0, 0), blk("a", 0, 3 * R, 0, 1), blk("b", 0, 3 * R, 0, 2)], [own1, a0, b0])
+    call([blk("own", 128, 128, 0, 0, 1), blk("a", 0, 3 * R, 0, 2), blk("b", 0, 3 * R, 0, 3)], [lo, hi, a0, b0])
     call(
         [
-            blk("a", 3, 3 * R, 0, 2),
-            blk("a", 1, 3 * R, 0, 3),
-            blk("b", 3, 3 * R, 0, 4),
-            blk("b", 1, 3 * R, 0, 5),
-            blk("c", 0, CR, 0, 0),
-            blk("c", 1, CR, 0, 1),
+            blk("c", 0, CR, 0, 0, 1),
+            blk("c", 1, CR, 0, 2, 3),
+            blk("a", 3, 3 * R, 0, 4),
+            blk("a", 1, 3 * R, 0, 5),
+            blk("b", 3, 3 * R, 0, 6),
+            blk("b", 1, 3 * R, 0, 7),
         ],
-        [cl, cr, al, ar, bl, br],
+        [cl_lo, cl_hi, cr_lo, cr_hi, al, ar, bl, br],
     )
-    call([blk("a", 2, 3 * R, 0, 2), blk("b", 2, 3 * R, 0, 3), blk("c", 2, CR, 0, 0, 1)], [cf_lo, cf_hi, af, bf])
-
-    k1 = kernel.reshape(1, 128)
-    out_a, out_b = along_x(plans, ids, k1, e2, asked, asked_b, parts)
+    call([blk("c", 2, CR, 0, 0, 1), blk("a", 2, 3 * R, 0, 2), blk("b", 2, 3 * R, 0, 3)], [cf_lo, cf_hi, af, bf])
+
+    out_a, out_b = along_x(plans, kernel.T, e2, asked, asked_b, parts)
     from_b = lax.ppermute(out_b, "core", swap)
     merged = out_a + from_b
     answers = lax.all_to_all(merged.reshape(16, 64, 128), ("x", "y"), split_axis=0, concat_axis=0, tiled=True)

time: 257 us -> 246 us (0.957)
  starting transfers between devices: 85.6 us -> 72.3 us
  waiting for transfers between devices: 72.6 us -> 85.4 us
  local copies, waits for them, and re-layouts: 8.95 us -> 1.82 us
    ppermute x4, starting transfers between devices: 16.2 us -> 3.05 us  [call(): parts.extend([keep, lax.ppermute(send, 'core', swap)])]
    ppermute x20 -> x22, waiting for transfers between devices: 57.2 us -> 69.4 us  [shift(): return lax.ppermute(x, axes, [(i, (i + by) % size) for i in range(size)])]
    slice x3 -> x0, local copies, waits for them, and re-layouts: 3.62 us -> none  [the longest x1 2.28 us: shards(): cf_hi = shift(cr[8:], z_axes, 8, -1)]
    pallas_call x3 -> x4, Pallas kernels: 12.9 us -> 15.2 us  [the longest x2 9.21 us: turn(): pl.pallas_call(functools.partial(turn_kernel, b), in_specs=[HBM], out_spe...]
    ppermute x20 -> x22, starting transfers between devices: 33.5 us -> 34.1 us  [shift(): return lax.ppermute(x, axes, [(i, (i + by) % size) for i in range(size)])]
  transfers between devices with their start and end apart: 31 -> 33, of which waited for: 12 -> 13; matrix products, arithmetic and copies ran while one was open for 4% -> 0% of each run, Pallas kernels for 23% -> 24%
where the time goes in v3:
time: 246 us; the launch traced here: 243 us
  waiting for transfers between devices  85.4 us (35%)
  Pallas kernels  80.1 us (33%)
  starting transfers between devices  72.3 us (29%)
  other arithmetic  2.75 us (1%)
    ppermute x22, waiting for transfers between devices, shift(): return lax.ppermute(x, axes, [(i, (i + by) % size) for i in range(size)])  69.4 us
    pallas_call x4, Pallas kernels, along_y(): pl.pallas_call(functools.partial(along_y_kernel, plan, len(srcs)), out_sh...  46.3 us
    ppermute x22, starting transfers between devices, shift(): return lax.ppermute(x, axes, [(i, (i + by) % size) for i in range(size)])  34.1 us
    pallas_call x1, Pallas kernels, along_x(): pl.pallas_call(functools.partial(along_x_kernel, plans), out_shape=[jax.S...  16.7 us
    ppermute x1, starting transfers between devices, shards(): got = lax.ppermute(other, 'zh', swap)  10.4 us
    all_to_all x1, waiting for transfers between devices, shards(): lax.all_to_all(merged.reshape(16, 64, 128), ('x', 'y'), split_axis=0, con...  10.3 us
    pallas_call x2, Pallas kernels, turn(): pl.pallas_call(functools.partial(turn_kernel, b), in_specs=[HBM], out_spe...  9.21 us
    all_to_all x1, starting transfers between devices, shards(): lax.all_to_all(merged.reshape(16, 64, 128), ('x', 'y'), split_axis=0, con...  9.13 us
  transfers between devices with their start and end apart: 33, of which 13 were waited for; matrix products, arithmetic and copies ran while one was open for 0% of the time, Pallas kernels for 24%

profile of v3, /device:TPU:1, one launch (start us, length us, event | category | flops | bytes accessed | tf_op | source)
XLA Modules:
  0.0 243.2 jit_solution(15942519938525879878)
XLA Ops:
  0.0 4.6 %shard_map.75 = (f32[8,128,256]{2,1,0:T(8,128)}, f32[8,128,256]{2,1,0:T(8,128)}) custom-call(f32[2,2048,512]{2,1,0:T(8,128)} %sky.3), custom_call_target="tpu_custom_call" | custom-call | flops 4194304 | bytes 4194304 | tf_op jit(solution)/shard_map/pallas_call | solution.py:168
  4.6 2.5 %collective-permute-start.15 = (f32[8,128,256]{2,1,0:T(8,128)}, f32[8,128,256]{2,1,0:T(8,128)}, u32[]{:S(2)}, u32[]{:S(2)}) collective-permute-start(f32[8,128,256]{2,1,0:T(8,128)} %get-tuple-element.48.rest_0_), channel_id=1, source_target_pairs={{0,1},{1,2},{2,3},{3,128},{128,129},{129,130},{130,131},{131,0},{4... | collective-permute-start | bytes 3145736 | tf_op jit(solution)/shard_map/ppermute | solution.py:738
  7.1 1.6 collective-permute-start.16
  8.8 2.5 %collective-permute-start.17 = (f32[8,128,256]{2,1,0:T(8,128)}, f32[8,128,256]{2,1,0:T(8,128)}, u32[]{:S(2)}, u32[]{:S(2)}) collective-permute-start(f32[8,128,256]{2,1,0:T(8,128)} %get-tuple-element.48.rest_0_), channel_id=1, source_target_pairs={{0,131},{1,0},{2,1},{3,2},{128,3},{129,128},{130,129},{131,130},{4... | collective-permute-start | bytes 3145736 | tf_op jit(solution)/shard_map/ppermute | solution.py:738
  11.3 4.6 %shard_map.73 = (f32[16,128,256]{2,1,0:T(8,128)}, f32[2,4,16,256]{3,2,1,0:T(8,128)}, f32[4,16,256]{2,1,0:T(8,128)}, f32[4,16,256]{2,1,0:T(8,128)}) custom-call(f32[2,2048,512]{2,1,0:T(8,128)} %sky.3), custom_call_target="tpu_custom_call" | custom-call | flops 4194304 | bytes 4194304 | tf_op jit(solution)/shard_map/pallas_call | solution.py:168
  15.9 0.0 copy-start.8
  15.9 1.8 collective-permute-start.6
  17.7 1.9 collective-permute-start.7
  19.6 39.5 %collective-permute-done.6.za = f32[4,16,256]{2,1,0:T(8,128)S(1)} collective-permute-done((f32[4,16,256]{2,1,0:T(8,128)}, f32[4,16,256]{2,1,0:T(8,128)S(1)}, u32[]{:S(2)}, u32[]{:S(2)}) %collective-permute-start.6) | collective-permute-done | bytes 65568 | tf_op jit(solution)/shard_map/ppermute | solution.py:738
  59.1 0.1 collective-permute-start.4
  59.2 2.5 %collective-permute-start.5 = (f32[2,4,16,256]{3,2,1,0:T(8,128)}, f32[2,4,16,256]{3,2,1,0:T(8,128)S(1)}, u32[]{:S(2)}, u32[]{:S(2)}) collective-permute-start(f32[2,4,16,256]{3,2,1,0:T(8,128)} %get-tuple-element.50), channel_id=1, source_target_pairs={{0,131},{1,0},{2,1},{3,2},{128,3},{129,128},{130,129},{131,130},{4... | collective-permute-start | bytes 393224 | tf_op jit(solution)/shard_map/ppermute | solution.py:738
  61.8 2.6 %collective-permute-done.4.zl = f32[2,4,16,256]{3,2,1,0:T(8,128)S(1)} collective-permute-done((f32[2,4,16,256]{3,2,1,0:T(8,128)}, f32[2,4,16,256]{3,2,1,0:T(8,128)S(1)}, u32[]{:S(2)}, u32[]{:S(2)}) %collective-permute-start.4) | collective-permute-done | bytes 131104 | tf_op jit(solution)/shard_map/ppermute | solution.py:738
  64.4 2.6 %collective-permute-start.8 = (f32[4,48,256]{2,1,0:T(8,128)S(1)}, f32[4,48,256]{2,1,0:T(8,128)S(1)}, u32[]{:S(2)}, u32[]{:S(2)}) collective-permute-start(f32[4,48,256]{2,1,0:T(8,128)S(1)} %get-tuple-element.53.refs_0_), channel_id=1, source_target_pairs={{0,96},{32,0},{64,32},{96,64},{1,97},{33,1},{65,33},{97,65},{2,98}... | collective-permute-start | bytes 589832 | tf_op jit(solution)/shard_map/ppermute | solution.py:738
  66.9 0.5 collective-permute-start.9
  67.4 4.6 %collective-permute-done.8.refs_1_ = f32[4,48,256]{2,1,0:T(8,128)S(1)} collective-permute-done((f32[4,48,256]{2,1,0:T(8,128)S(1)}, f32[4,48,256]{2,1,0:T(8,128)S(1)}, u32[]{:S(2)}, u32[]{:S(2)}) %collective-permute-start.8) | collective-permute-done | bytes 196640 | tf_op jit(solution)/shard_map/ppermute | solution.py:738
  72.0 0.9 collective-permute-done.9.refs_2_
  72.9 2.7 %collective-permute-start.11 = (f32[4,48,256]{2,1,0:T(8,128)S(1)}, f32[4,48,256]{2,1,0:T(8,128)S(1)}, u32[]{:S(2)}, u32[]{:S(2)}) collective-permute-start(f32[4,48,256]{2,1,0:T(8,128)S(1)} %get-tuple-element.54.refs_4_), channel_id=1, source_target_pairs={{0,24},{8,0},{16,8},{24,16},{1,25},{9,1},{17,9},{25,17},{2,26},{10... | collective-permute-start | bytes 589832 | tf_op jit(solution)/shard_map/ppermute | solution.py:738
  75.7 3.3 %collective-permute-done.10.refs_3_ = f32[4,48,256]{2,1,0:T(8,128)S(1)} collective-permute-done((f32[4,48,256]{2,1,0:T(8,128)S(1)}, f32[4,48,256]{2,1,0:T(8,128)S(1)}, u32[]{:S(2)}, u32[]{:S(2)}) %collective-permute-start.10) | collective-permute-done | bytes 196640 | tf_op jit(solution)/shard_map/ppermute | solution.py:738
  79.0 2.9 %collective-permute-start.12 = (f32[4,48,256]{2,1,0:T(8,128)S(1)}, f32[4,48,256]{2,1,0:T(8,128)S(1)}, u32[]{:S(2)}, u32[]{:S(2)}) collective-permute-start(f32[4,48,256]{2,1,0:T(8,128)S(1)} %get-tuple-element.54.refs_4_), channel_id=1, source_target_pairs={{0,16},{8,24},{16,0},{24,8},{1,17},{9,25},{17,1},{25,9},{2,18},{10... | collective-permute-start | bytes 589832 | tf_op jit(solution)/shard_map/ppermute | solution.py:738
  81.9 3.0 %collective-permute-start.18 = (f32[8,128,256]{2,1,0:T(8,128)S(1)}, f32[8,128,256]{2,1,0:T(8,128)}, u32[]{:S(2)}, u32[]{:S(2)}) collective-permute-start(f32[8,128,256]{2,1,0:T(8,128)S(1)} %copy-done.7), channel_id=1, source_target_pairs={{0,131},{1,0},{2,1},{3,2},{128,3},{129,128},{130,129},{131,130},{4... | collective-permute-start | bytes 3145736 | tf_op jit(solution)/shard_map/ppermute | solution.py:738
  84.9 0.1 reshape.35
  85.6 3.6 %tables.1 = (bf16[4,256,256]{2,1,0:T(8,128)(2,1)}, bf16[4,256,256]{2,1,0:T(8,128)(2,1)}, bf16[4,256,256]{2,1,0:T(8,128)(2,1)}, bf16[4,256,256]{2,1,0:T(8,128)(2,...) custom-call(), custom_call_target="tpu_custom_call" | custom-call | flops 31457280 | bytes 4194304 | tf_op jit(solution)/shard_map/tables/pallas_call | solution.py:105
  89.2 0.4 collective-permute-start.13
  89.6 0.2 select_reduce_fusion
  89.8 5.1 %collective-permute-done.13.refs_7_ = f32[4,48,256]{2,1,0:T(8,128)S(1)} collective-permute-done((f32[4,48,256]{2,1,0:T(8,128)S(1)}, f32[4,48,256]{2,1,0:T(8,128)S(1)}, u32[]{:S(2)}, u32[]{:S(2)}) %collective-permute-start.13) | collective-permute-done | bytes 196640 | tf_op jit(solution)/shard_map/ppermute | solution.py:738
  94.9 6.0 %collective-permute-start.2 = (f32[1]{0:T(128)}, f32[1]{0:T(128)}, u32[]{:S(2)}, u32[]{:S(2)}) collective-permute-start(f32[1]{0:T(128)} %param.8), channel_id=1, source_target_pairs={{0,4},{4,0},{1,5},{5,1},{2,6},{6,2},{3,7},{7,3},{8,12},{12,8},{9,1... | collective-permute-start | bytes 20 | tf_op jit(solution)/shard_map/ppermute | solution.py:781
  100.9 1.3 join.1
  102.2 2.7 %collective-permute-start.20 = (f32[16,48,256]{2,1,0:T(8,128)}, f32[16,48,256]{2,1,0:T(8,128)}, u32[]{:S(2)}, u32[]{:S(2)}) collective-permute-start(f32[16,48,256]{2,1,0:T(8,128)} %get-tuple-element.55.rest_2_), channel_id=1, source_target_pairs={{0,24},{8,0},{16,8},{24,16},{1,25},{9,1},{17,9},{25,17},{2,26},{10... | collective-permute-start | bytes 2359304 | tf_op jit(solution)/shard_map/ppermute | solution.py:738
  104.9 2.2 collective-permute-start.21
  107.1 0.5 collective-permute-start.22
  107.6 0.6 pad_add_fusion.mine
  108.3 2.3 collective-permute-start
  110.6 12.3 %collective-permute-done.19.rest_4_ = f32[16,48,256]{2,1,0:T(8,128)} collective-permute-done((f32[16,48,256]{2,1,0:T(8,128)}, f32[16,48,256]{2,1,0:T(8,128)}, u32[]{:S(2)}, u32[]{:S(2)}) %collective-permute-start.19) | collective-permute-done | bytes 786464 | tf_op jit(solution)/shard_map/ppermute | solution.py:738
  122.9 1.7 collective-permute-start.27
  124.6 0.4 collective-permute-done.21.rest_6_
  125.0 0.7 collective-permute-done.22.rest_7_
  125.7 2.0 collective-permute-start.25
  127.7 17.7 %shard_map.77 = (f32[2,2,56,8,256]{4,3,2,1,0:T(8,128)}, f32[2,2,56,8,256]{4,3,2,1,0:T(8,128)}) custom-call(f32[1]{0:T(128)S(6)} %copy.8.w_own, f32[1]{0:T(128)} %collective-permute-done.2.w_other, bf16[4,256,256]{2,1,0:T(8,128)(2,1)} %get-tuple-element.42.e1h, bf16[4,256,256]{2,1,0:T(8,128)(2,1)} %get-tuple-element.43.e1l, ...), custom_call_target="tpu_custom_call" | custom-call | flops 5637144576 | bytes 11010048 | tf_op jit(solution)/shard_map/pallas_call | solution.py:418
  145.3 2.1 collective-permute-start.23
  147.4 2.4 arrange.1
  149.8 0.5 copy-done
  150.3 0.5 copy-done.2
  150.8 6.6 %all-to-all-start = ((s32[16,72,128]{2,1,0:T(8,128)}), s32[16,72,128]{2,1,0:T(8,128)}, u32[]{:S(2)}, u32[]{:S(2)}) async-start(s32[16,72,128]{2,1,0:T(8,128)} %get-tuple-element.41), calls=%async_computation | async-start | bytes 1179648 | tf_op jit(solution)/shard_map/all_to_all | solution.py:779
  157.4 10.7 %shard_map.76 = (f32[2,2,28,8,256]{4,3,2,1,0:T(8,128)}, f32[2,2,28,8,256]{4,3,2,1,0:T(8,128)}) custom-call(f32[1]{0:T(128)S(6)} %copy.8.w_own, f32[1]{0:T(128)} %collective-permute-done.2.w_other, bf16[4,256,256]{2,1,0:T(8,128)(2,1)} %get-tuple-element.42.e1h, bf16[4,256,256]{2,1,0:T(8,128)(2,1)} %get-tuple-element.43.e1l, ...), custom_call_target="tpu_custom_call" | custom-call | flops 2818572288 | bytes 5505024 | tf_op jit(solution)/shard_map/pallas_call | solution.py:418
  168.1 0.4 collective-permute-start.14
  168.5 10.7 %shard_map.78 = (f32[2,2,28,8,256]{4,3,2,1,0:T(8,128)}, f32[2,2,28,8,256]{4,3,2,1,0:T(8,128)}) custom-call(f32[1]{0:T(128)S(6)} %copy.8.w_own, f32[1]{0:T(128)} %collective-permute-done.2.w_other, bf16[4,256,256]{2,1,0:T(8,128)(2,1)} %get-tuple-element.42.e1h, bf16[4,256,256]{2,1,0:T(8,128)(2,1)} %get-tuple-element.43.e1l, ...), custom_call_target="tpu_custom_call" | custom-call | flops 2818572288 | bytes 5505024 | tf_op jit(solution)/shard_map/pallas_call | solution.py:418
  179.1 0.3 collective-permute-start.28
  179.4 0.3 collective-permute-start.1
  179.7 7.3 %shard_map.74 = (f32[2,2,16,8,256]{4,3,2,1,0:T(8,128)}, f32[2,2,16,8,256]{4,3,2,1,0:T(8,128)}) custom-call(f32[1]{0:T(128)S(6)} %copy.8.w_own, f32[1]{0:T(128)} %collective-permute-done.2.w_other, bf16[4,256,256]{2,1,0:T(8,128)(2,1)} %get-tuple-element.42.e1h, bf16[4,256,256]{2,1,0:T(8,128)(2,1)} %get-tuple-element.43.e1l, ...), custom_call_target="tpu_custom_call" | custom-call | flops 1610612736 | bytes 3145728 | tf_op jit(solution)/shard_map/pallas_call | solution.py:418
  187.0 0.3 collective-permute-start.3
  187.3 2.0 collective-permute-done.3.rest_1_
  189.4 16.7 %along_x.1 = (f32[128,8,128]{2,1,0:T(8,128)}, f32[128,8,128]{2,1,0:T(8,128)}) custom-call(f32[8,16]{1,0:T(8,128)} %bitcast.14, bf16[4,256,256]{2,1,0:T(8,128)(2,1)} %get-tuple-element.38.e2h, bf16[4,256,256]{2,1,0:T(8,128)(2,1)} %get-tuple-element.39.e2l, f32[2,12,128,128]{3,2,1,0:T(8,128)} %get-tuple-element.40.tw2, s32[16,72,128]{2,1,0:T(8,128)} %all-to-all-done.pos_a, ...), custom_call_target="tpu_custom_call" | custom-call | flops 60000002048 | bytes 16777216 | tf_op jit(solution)/shard_map/along_x/pallas_call | solution.py:638
  206.1 0.0 copy-start.5
  206.1 0.0 copy-start.1
  206.1 0.3 collective-permute-start.29
  206.4 1.9 collective-permute-done.29
  208.4 1.9 add.31
  210.3 9.1 %all-to-all-start.1 = ((f32[16,64,128]{2,1,0:T(8,128)}), f32[16,64,128]{2,1,0:T(8,128)S(1)}, u32[]{:S(2)}, u32[]{:S(2)}) async-start(f32[16,64,128]{2,1,0:T(8,128)} %bitcast.6), calls=%async_computation.1 | async-start | bytes 1048576 | tf_op jit(solution)/shard_map/all_to_all | solution.py:813
  219.4 0.1 reshape.38.observed
  219.5 10.3 %all-to-all-done.1 = f32[16,64,128]{2,1,0:T(8,128)S(1)} async-done(((f32[16,64,128]{2,1,0:T(8,128)}), f32[16,64,128]{2,1,0:T(8,128)S(1)}, u32[]{:S(2)}, u32[]{:S(2)}) %all-to-all-start.1) | async-done | bytes 524320 | tf_op jit(solution)/shard_map/all_to_all | solution.py:813
  229.8 0.6 pick.1
  230.4 10.4 %collective-permute-start.30 = (f32[16,8,128]{2,1,0:T(8,128)S(1)}, f32[16,8,128]{2,1,0:T(8,128)S(1)}, u32[]{:S(2)}, u32[]{:S(2)}) collective-permute-start(f32[16,8,128]{2,1,0:T(8,128)S(1)} %get-tuple-element.66), channel_id=1, source_target_pairs={{0,128},{128,0},{1,129},{129,1},{2,130},{130,2},{3,131},{131,3},{4... | collective-permute-start | bytes 196616 | tf_op jit(solution)/shard_map/ppermute | solution.py:815
  240.8 1.7 collective-permute-done.30
  242.5 0.7 reshape.39
  (44 shorter events, 0.2 us)
Async XLA Ops:
  4.6 97.6 %collective-permute-start.15 = (f32[8,128,256]{2,1,0:T(8,128)}, f32[8,128,256]{2,1,0:T(8,128)}, u32[]{:S(2)}, u32[]{:S(2)}) collective-permute-start(f32[8,128,256]{2,1,0:T(8,128)} %get-tuple-element.48.rest_0_), channel_id=1, source_target_pairs={{0,1},{1,2},{2,3},{3,128},{128,129},{129,130},{130,131},{131,0},{4... | collective-permute-start | bytes 3145736 | tf_op jit(solution)/shard_map/ppermute | solution.py:738
  7.1 74.8 %copy-start.7 = (f32[8,128,256]{2,1,0:T(8,128)S(1)}, f32[8,128,256]{2,1,0:T(8,128)}, u32[]{:S(2)}) copy-start(f32[8,128,256]{2,1,0:T(8,128)} %get-tuple-element.49.rest_1_) | copy-start | bytes 3145732
  7.1 77.7 %copy-start.4 = (s32[16,2,512]{2,1,0:T(2,128)S(1)}, s32[16,2,512]{2,1,0:T(2,128)}, u32[]{:S(2)}) copy-start(s32[16,2,512]{2,1,0:T(2,128)} %param.12) | copy-start | bytes 196612
  7.1 82.5 %copy-start.6 = (s32[16,1]{0,1:T(1,128)S(1)}, s32[16,1]{0,1:T(1,128)}, u32[]{:S(2)}) copy-start(s32[16,1]{0,1:T(1,128)} %param.11) | copy-start | bytes 196
  7.1 97.8 %collective-permute-start.16 = (f32[8,128,256]{2,1,0:T(8,128)}, f32[8,128,256]{2,1,0:T(8,128)}, u32[]{:S(2)}, u32[]{:S(2)}) collective-permute-start(f32[8,128,256]{2,1,0:T(8,128)} %get-tuple-element.49.rest_1_), channel_id=1, source_target_pairs={{0,1},{1,2},{2,3},{3,128},{128,129},{129,130},{130,131},{131,0},{4... | collective-permute-start | bytes 3145736 | tf_op jit(solution)/shard_map/ppermute | solution.py:738
  8.8 98.3 %collective-permute-start.17 = (f32[8,128,256]{2,1,0:T(8,128)}, f32[8,128,256]{2,1,0:T(8,128)}, u32[]{:S(2)}, u32[]{:S(2)}) collective-permute-start(f32[8,128,256]{2,1,0:T(8,128)} %get-tuple-element.48.rest_0_), channel_id=1, source_target_pairs={{0,131},{1,0},{2,1},{3,2},{128,3},{129,128},{130,129},{131,130},{4... | collective-permute-start | bytes 3145736 | tf_op jit(solution)/shard_map/ppermute | solution.py:738
  15.9 91.7 %copy-start.8 = (s32[16]{0:T(128)S(1)}, s32[16]{0:T(128)}, u32[]{:S(2)}) copy-start(s32[16]{0:T(128)} %param.10) | copy-start | bytes 196
  15.9 43.2 %collective-permute-start.6 = (f32[4,16,256]{2,1,0:T(8,128)}, f32[4,16,256]{2,1,0:T(8,128)S(1)}, u32[]{:S(2)}, u32[]{:S(2)}) collective-permute-start(f32[4,16,256]{2,1,0:T(8,128)} %get-tuple-element.51), channel_id=1, source_target_pairs={{0,2},{1,3},{2,128},{3,129},{128,130},{129,131},{130,0},{131,1},{4... | collective-permute-start | bytes 196616 | tf_op jit(solution)/shard_map/ppermute | solution.py:738
  17.7 41.5 %collective-permute-start.7 = (f32[4,16,256]{2,1,0:T(8,128)}, f32[4,16,256]{2,1,0:T(8,128)S(1)}, u32[]{:S(2)}, u32[]{:S(2)}) collective-permute-start(f32[4,16,256]{2,1,0:T(8,128)} %get-tuple-element.52), channel_id=1, source_target_pairs={{0,130},{1,131},{2,0},{3,1},{128,2},{129,3},{130,128},{131,129},{4... | collective-permute-start | bytes 196616 | tf_op jit(solution)/shard_map/ppermute | solution.py:738
  59.1 5.2 %collective-permute-start.4 = (f32[2,4,16,256]{3,2,1,0:T(8,128)}, f32[2,4,16,256]{3,2,1,0:T(8,128)S(1)}, u32[]{:S(2)}, u32[]{:S(2)}) collective-permute-start(f32[2,4,16,256]{3,2,1,0:T(8,128)} %get-tuple-element.50), channel_id=1, source_target_pairs={{0,1},{1,2},{2,3},{3,128},{128,129},{129,130},{130,131},{131,0},{4... | collective-permute-start | bytes 393224 | tf_op jit(solution)/shard_map/ppermute | solution.py:738
  59.2 5.1 %collective-permute-start.5 = (f32[2,4,16,256]{3,2,1,0:T(8,128)}, f32[2,4,16,256]{3,2,1,0:T(8,128)S(1)}, u32[]{:S(2)}, u32[]{:S(2)}) collective-permute-start(f32[2,4,16,256]{3,2,1,0:T(8,128)} %get-tuple-element.50), channel_id=1, source_target_pairs={{0,131},{1,0},{2,1},{3,2},{128,3},{129,128},{130,129},{131,130},{4... | collective-permute-start | bytes 393224 | tf_op jit(solution)/shard_map/ppermute | solution.py:738
  64.4 7.7 %collective-permute-start.8 = (f32[4,48,256]{2,1,0:T(8,128)S(1)}, f32[4,48,256]{2,1,0:T(8,128)S(1)}, u32[]{:S(2)}, u32[]{:S(2)}) collective-permute-start(f32[4,48,256]{2,1,0:T(8,128)S(1)} %get-tuple-element.53.refs_0_), channel_id=1, source_target_pairs={{0,96},{32,0},{64,32},{96,64},{1,97},{33,1},{65,33},{97,65},{2,98}... | collective-permute-start | bytes 589832 | tf_op jit(solution)/shard_map/ppermute | solution.py:738
  66.9 6.0 %collective-permute-start.9 = (f32[4,48,256]{2,1,0:T(8,128)S(1)}, f32[4,48,256]{2,1,0:T(8,128)S(1)}, u32[]{:S(2)}, u32[]{:S(2)}) collective-permute-start(f32[4,48,256]{2,1,0:T(8,128)S(1)} %get-tuple-element.53.refs_0_), channel_id=1, source_target_pairs={{0,64},{32,96},{64,0},{96,32},{1,65},{33,97},{65,1},{97,33},{2,66}... | collective-permute-start | bytes 589832 | tf_op jit(solution)/shard_map/ppermute | solution.py:738
  72.0 7.0 %collective-permute-start.10 = (f32[4,48,256]{2,1,0:T(8,128)S(1)}, f32[4,48,256]{2,1,0:T(8,128)S(1)}, u32[]{:S(2)}, u32[]{:S(2)}) collective-permute-start(f32[4,48,256]{2,1,0:T(8,128)S(1)} %get-tuple-element.53.refs_0_), channel_id=1, source_target_pairs={{0,32},{32,64},{64,96},{96,0},{1,33},{33,65},{65,97},{97,1},{2,34}... | collective-permute-start | bytes 589832 | tf_op jit(solution)/shard_map/ppermute | solution.py:738
  72.9 9.0 %collective-permute-start.11 = (f32[4,48,256]{2,1,0:T(8,128)S(1)}, f32[4,48,256]{2,1,0:T(8,128)S(1)}, u32[]{:S(2)}, u32[]{:S(2)}) collective-permute-start(f32[4,48,256]{2,1,0:T(8,128)S(1)} %get-tuple-element.54.refs_4_), channel_id=1, source_target_pairs={{0,24},{8,0},{16,8},{24,16},{1,25},{9,1},{17,9},{25,17},{2,26},{10... | collective-permute-start | bytes 589832 | tf_op jit(solution)/shard_map/ppermute | solution.py:738
  79.0 10.2 %collective-permute-start.12 = (f32[4,48,256]{2,1,0:T(8,128)S(1)}, f32[4,48,256]{2,1,0:T(8,128)S(1)}, u32[]{:S(2)}, u32[]{:S(2)}) collective-permute-start(f32[4,48,256]{2,1,0:T(8,128)S(1)} %get-tuple-element.54.refs_4_), channel_id=1, source_target_pairs={{0,16},{8,24},{16,0},{24,8},{1,17},{9,25},{17,1},{25,9},{2,18},{10... | collective-permute-start | bytes 589832 | tf_op jit(solution)/shard_map/ppermute | solution.py:738
  81.9 26.4 %collective-permute-start.18 = (f32[8,128,256]{2,1,0:T(8,128)S(1)}, f32[8,128,256]{2,1,0:T(8,128)}, u32[]{:S(2)}, u32[]{:S(2)}) collective-permute-start(f32[8,128,256]{2,1,0:T(8,128)S(1)} %copy-done.7), channel_id=1, source_target_pairs={{0,131},{1,0},{2,1},{3,2},{128,3},{129,128},{130,129},{131,130},{4... | collective-permute-start | bytes 3145736 | tf_op jit(solution)/shard_map/ppermute | solution.py:738
  89.2 5.7 %collective-permute-start.13 = (f32[4,48,256]{2,1,0:T(8,128)S(1)}, f32[4,48,256]{2,1,0:T(8,128)S(1)}, u32[]{:S(2)}, u32[]{:S(2)}) collective-permute-start(f32[4,48,256]{2,1,0:T(8,128)S(1)} %get-tuple-element.54.refs_4_), channel_id=1, source_target_pairs={{0,8},{8,16},{16,24},{24,0},{1,9},{9,17},{17,25},{25,1},{2,10},{10... | collective-permute-start | bytes 589832 | tf_op jit(solution)/shard_map/ppermute | solution.py:738
  94.9 7.3 %collective-permute-start.2 = (f32[1]{0:T(128)}, f32[1]{0:T(128)}, u32[]{:S(2)}, u32[]{:S(2)}) collective-permute-start(f32[1]{0:T(128)} %param.8), channel_id=1, source_target_pairs={{0,4},{4,0},{1,5},{5,1},{2,6},{6,2},{3,7},{7,3},{8,12},{12,8},{9,1... | collective-permute-start | bytes 20 | tf_op jit(solution)/shard_map/ppermute | solution.py:781
  102.2 20.6 %collective-permute-start.19 = (f32[16,48,256]{2,1,0:T(8,128)}, f32[16,48,256]{2,1,0:T(8,128)}, u32[]{:S(2)}, u32[]{:S(2)}) collective-permute-start(f32[16,48,256]{2,1,0:T(8,128)} %get-tuple-element.55.rest_2_), channel_id=1, source_target_pairs={{0,8},{8,16},{16,24},{24,0},{1,9},{9,17},{17,25},{25,1},{2,10},{10... | collective-permute-start | bytes 2359304 | tf_op jit(solution)/shard_map/ppermute | solution.py:738
  102.2 20.6 %collective-permute-start.20 = (f32[16,48,256]{2,1,0:T(8,128)}, f32[16,48,256]{2,1,0:T(8,128)}, u32[]{:S(2)}, u32[]{:S(2)}) collective-permute-start(f32[16,48,256]{2,1,0:T(8,128)} %get-tuple-element.55.rest_2_), channel_id=1, source_target_pairs={{0,24},{8,0},{16,8},{24,16},{1,25},{9,1},{17,9},{25,17},{2,26},{10... | collective-permute-start | bytes 2359304 | tf_op jit(solution)/shard_map/ppermute | solution.py:738
  104.9 20.1 %collective-permute-start.21 = (f32[16,48,256]{2,1,0:T(8,128)}, f32[16,48,256]{2,1,0:T(8,128)}, u32[]{:S(2)}, u32[]{:S(2)}) collective-permute-start(f32[16,48,256]{2,1,0:T(8,128)} %get-tuple-element.56.rest_3_), channel_id=1, source_target_pairs={{0,32},{32,64},{64,96},{96,0},{1,33},{33,65},{65,97},{97,1},{2,34}... | collective-permute-start | bytes 2359304 | tf_op jit(solution)/shard_map/ppermute | solution.py:738
  107.1 18.6 %collective-permute-start.22 = (f32[16,48,256]{2,1,0:T(8,128)}, f32[16,48,256]{2,1,0:T(8,128)}, u32[]{:S(2)}, u32[]{:S(2)}) collective-permute-start(f32[16,48,256]{2,1,0:T(8,128)} %get-tuple-element.56.rest_3_), channel_id=1, source_target_pairs={{0,96},{32,0},{64,32},{96,64},{1,97},{33,1},{65,33},{97,65},{2,98}... | collective-permute-start | bytes 2359304 | tf_op jit(solution)/shard_map/ppermute | solution.py:738
  108.3 37.0 %collective-permute-start = (s32[17,8,128]{2,1,0:T(8,128)}, s32[17,8,128]{2,1,0:T(8,128)}, u32[]{:S(2)}, u32[]{:S(2)}) collective-permute-start(s32[17,8,128]{2,1,0:T(8,128)} %pad_add_fusion.mine), channel_id=1, source_target_pairs={{0,128},{128,0},{1,129},{129,1},{2,130},{130,2},{3,131},{131,3},{4... | collective-permute-start | bytes 208904 | tf_op jit(solution)/shard_map/ppermute | solution.py:751
  122.8 45.2 %collective-permute-start.26 = (f32[16,48,256]{2,1,0:T(8,128)}, f32[16,48,256]{2,1,0:T(8,128)}, u32[]{:S(2)}, u32[]{:S(2)}) collective-permute-start(f32[16,48,256]{2,1,0:T(8,128)} %get-tuple-element.55.rest_2_), channel_id=1, source_target_pairs={{0,16},{8,24},{16,0},{24,8},{1,17},{9,25},{17,1},{25,9},{2,18},{10... | collective-permute-start | bytes 2359304 | tf_op jit(solution)/shard_map/ppermute | solution.py:738
  122.9 45.6 %collective-permute-start.27 = (f32[16,48,256]{2,1,0:T(8,128)}, f32[16,48,256]{2,1,0:T(8,128)}, u32[]{:S(2)}, u32[]{:S(2)}) collective-permute-start(f32[16,48,256]{2,1,0:T(8,128)} %get-tuple-element.56.rest_3_), channel_id=1, source_target_pairs={{0,64},{32,96},{64,0},{96,32},{1,65},{33,97},{65,1},{97,33},{2,66}... | collective-permute-start | bytes 2359304 | tf_op jit(solution)/shard_map/ppermute | solution.py:738
  125.0 43.5 %collective-permute-start.24 = (f32[8,128,256]{2,1,0:T(8,128)}, f32[8,128,256]{2,1,0:T(8,128)}, u32[]{:S(2)}, u32[]{:S(2)}) collective-permute-start(f32[8,128,256]{2,1,0:T(8,128)} %collective-permute-done.15.rest_0_), channel_id=1, source_target_pairs={{0,1},{1,2},{2,3},{3,128},{128,129},{129,130},{130,131},{131,0},{4... | collective-permute-start | bytes 3145736 | tf_op jit(solution)/shard_map/ppermute | solution.py:738
  125.7 42.8 %collective-permute-start.25 = (f32[8,128,256]{2,1,0:T(8,128)}, f32[8,128,256]{2,1,0:T(8,128)}, u32[]{:S(2)}, u32[]{:S(2)}) collective-permute-start(f32[8,128,256]{2,1,0:T(8,128)} %collective-permute-done.18.rest_3_), channel_id=1, source_target_pairs={{0,131},{1,0},{2,1},{3,2},{128,3},{129,128},{130,129},{131,130},{4... | collective-permute-start | bytes 3145736 | tf_op jit(solution)/shard_map/ppermute | solution.py:738
  145.3 44.1 %collective-permute-start.23 = (f32[2,2,56,8,256]{4,3,2,1,0:T(8,128)}, f32[2,2,56,8,256]{4,3,2,1,0:T(8,128)}, u32[]{:S(2)}, u32[]{:S(2)}) collective-permute-start(f32[2,2,56,8,256]{4,3,2,1,0:T(8,128)} %get-tuple-element.60), channel_id=1, source_target_pairs={{0,4},{4,0},{1,5},{5,1},{2,6},{6,2},{3,7},{7,3},{8,12},{12,8},{9,1... | collective-permute-start | bytes 5505032 | tf_op jit(solution)/shard_map/ppermute | solution.py:790
  149.8 0.5 copy-start
  150.3 0.5 copy-start.2
  150.8 28.6 %all-to-all-start = ((s32[16,72,128]{2,1,0:T(8,128)}), s32[16,72,128]{2,1,0:T(8,128)}, u32[]{:S(2)}, u32[]{:S(2)}) async-start(s32[16,72,128]{2,1,0:T(8,128)} %get-tuple-element.41), calls=%async_computation | async-start | bytes 1179648 | tf_op jit(solution)/shard_map/all_to_all | solution.py:779
  168.1 21.3 %collective-permute-start.14 = (f32[2,2,28,8,256]{4,3,2,1,0:T(8,128)}, f32[2,2,28,8,256]{4,3,2,1,0:T(8,128)}, u32[]{:S(2)}, u32[]{:S(2)}) collective-permute-start(f32[2,2,28,8,256]{4,3,2,1,0:T(8,128)} %get-tuple-element.58), channel_id=1, source_target_pairs={{0,4},{4,0},{1,5},{5,1},{2,6},{6,2},{3,7},{7,3},{8,12},{12,8},{9,1... | collective-permute-start | bytes 2752520 | tf_op jit(solution)/shard_map/ppermute | solution.py:790
  179.1 10.3 %collective-permute-start.28 = (f32[2,2,28,8,256]{4,3,2,1,0:T(8,128)}, f32[2,2,28,8,256]{4,3,2,1,0:T(8,128)}, u32[]{:S(2)}, u32[]{:S(2)}) collective-permute-start(f32[2,2,28,8,256]{4,3,2,1,0:T(8,128)} %get-tuple-element.62), channel_id=1, source_target_pairs={{0,4},{4,0},{1,5},{5,1},{2,6},{6,2},{3,7},{7,3},{8,12},{12,8},{9,1... | collective-permute-start | bytes 2752520 | tf_op jit(solution)/shard_map/ppermute | solution.py:790
  179.4 10.0 %collective-permute-start.1 = (s32[16,72,128]{2,1,0:T(8,128)}, s32[16,72,128]{2,1,0:T(8,128)}, u32[]{:S(2)}, u32[]{:S(2)}) collective-permute-start(s32[16,72,128]{2,1,0:T(8,128)} %all-to-all-done.pos_a), channel_id=1, source_target_pairs={{0,4},{4,0},{1,5},{5,1},{2,6},{6,2},{3,7},{7,3},{8,12},{12,8},{9,1... | collective-permute-start | bytes 1769480 | tf_op jit(solution)/shard_map/ppermute | solution.py:780
  187.0 2.3 collective-permute-start.3
  206.1 13.3 %copy-start.5 = (f32[16,2,512]{2,1,0:T(2,128)S(1)}, f32[16,2,512]{2,1,0:T(2,128)}, u32[]{:S(2)}) copy-start(f32[16,2,512]{2,1,0:T(2,128)} %param.13) | copy-start | bytes 196612
  206.1 23.7 %copy-start.1 = (s32[16]{0:T(128)S(1)}, s32[16]{0:T(128)}, u32[]{:S(2)}) copy-start(s32[16]{0:T(128)} %copy-done) | copy-start | bytes 196
  206.1 23.6 %copy-start.3 = (s32[16]{0:T(128)S(1)}, s32[16]{0:T(128)}, u32[]{:S(2)}) copy-start(s32[16]{0:T(128)} %copy-done.2) | copy-start | bytes 196
  206.1 2.2 collective-permute-start.29
  210.3 19.5 %all-to-all-start.1 = ((f32[16,64,128]{2,1,0:T(8,128)}), f32[16,64,128]{2,1,0:T(8,128)S(1)}, u32[]{:S(2)}, u32[]{:S(2)}) async-start(f32[16,64,128]{2,1,0:T(8,128)} %bitcast.6), calls=%async_computation.1 | async-start | bytes 1048576 | tf_op jit(solution)/shard_map/all_to_all | solution.py:813
  230.4 12.1 %collective-permute-start.30 = (f32[16,8,128]{2,1,0:T(8,128)S(1)}, f32[16,8,128]{2,1,0:T(8,128)S(1)}, u32[]{:S(2)}, u32[]{:S(2)}) collective-permute-start(f32[16,8,128]{2,1,0:T(8,128)S(1)} %get-tuple-element.66), channel_id=1, source_target_pairs={{0,128},{128,0},{1,129},{129,1},{2,130},{130,2},{3,131},{131,3},{4... | collective-permute-start | bytes 196616 | tf_op jit(solution)/shard_map/ppermute | solution.py:815

commit v4 on v3

--- a/solution.py
+++ b/solution.py
@@ -132,31 +132,27 @@
     rev = 127 - lax.broadcasted_iota(jnp.int32, (128, 128), 1)
     for c in range(2):
         loads[c].wait()
-    for y4 in range(4):
-        def group(i, carry, y4=y4):
-            for e in range(2):
-                y0 = 4 * y4 + 2 * i + e
-                for c in range(2):
+        for y4 in range(4):
+            def group(i, carry, y4=y4, c=c):
+                for e in range(2):
+                    y0 = 4 * y4 + 2 * i + e
                     v = xin[c, pl.ds(y0, 128, stride=16), :].T
                     if y4 > 1:
                         v = jnp.take_along_axis(v, rev, axis=1)
-                    z = 2 * e + c
-                    tmp[z] = v
+                    tmp[e] = v
                     for j0 in range(16):
-                        t[y0, 8 * j0 : 8 * j0 + 8, 128 * c : 128 * c + 128] = tmp[z, pl.ds(j0, 8, stride=16), :]
-            return carry
-
-        lax.fori_loop(0, 2, group, 0)
-        if y4 < 3:
-            move(t.at[pl.ds(4 * y4, 4)], part(y4))
+                        t[y0, 8 * j0 : 8 * j0 + 8, 128 * c : 128 * c + 128] = tmp[e, pl.ds(j0, 8, stride=16), :]
+                return carry
+
+            lax.fori_loop(0, 2, group, 0)
+            if c == 1 and y4 < 3:
+                move(t.at[pl.ds(4 * y4, 4)], part(y4))
     if outs:
         a_src = t.at[pl.ds(4 * xc, 4), pl.ds(pl.multiple_of(R * yc, 8), R), :]
         b_src = t.at[pl.ds(4 * yc, 4), pl.ds(pl.multiple_of(4 * R + R * xc, 8), R), :]
-        ab, pa, pb = outs
+        (ab,) = outs
         move(a_src, ab.at[0])
         move(b_src, ab.at[1])
-        move(a_src, pa)
-        move(b_src, pb)
     move(t.at[pl.ds(12, 4)], part(3))
     for m in moves:
         m.wait()
@@ -164,7 +160,7 @@
 
 def turn(b, sky):
     sds = lambda *d: jax.ShapeDtypeStruct(d, F32)
-    outs = [sds(8, 128, 256)] * 2 if b else [sds(16, 128, 256), sds(2, 4, R, 256), sds(4, R, 256), sds(4, R, 256)]
+    outs = [sds(8, 128, 256)] * 2 if b else [sds(16, 128, 256), sds(2, 4, R, 256)]
     return pl.pallas_call(
         functools.partial(turn_kernel, b),
         in_specs=[HBM],
@@ -181,18 +177,17 @@
     )(sky)
 
 
-def gather3_kernel(zl, zr, za, zb, oa, ob):
-    for k, (o, far) in enumerate(((oa, za), (ob, zb))):
-        o[:, 0:R, :] = zl[k]
-        o[:, R : 2 * R, :] = zr[k]
-        o[:, 2 * R : 3 * R, :] = far[...]
+def gather3_kernel(zl, zr, zf, oa, ob):
+    for k, o in enumerate((oa, ob)):
+        for i, z in enumerate((zl, zr, zf)):
+            o[:, R * i : R * i + R, :] = z[k]
 
 
 def gather3(*z):
     return pl.pallas_call(
         gather3_kernel,
         out_shape=[jax.ShapeDtypeStruct((4, 3 * R, 256), F32)] * 2,
-        in_specs=[VMEM] * 4,
+        in_specs=[VMEM] * 3,
         out_specs=[VMEM] * 2,
         compiler_params=pltpu.CompilerParams(vmem_limit_bytes=8 << 20),
         cost_estimate=pl.CostEstimate(flops=1 << 20, bytes_accessed=1 << 20, transcendentals=0),
@@ -486,7 +481,7 @@
         for ref, off, cnt, j0, at in loads:
             dst = d.at[pi, :, pl.ds(j0, cnt), at, :]
             pltpu.make_async_copy(ref.at[pi, :, pl.ds(off, cnt)], dst, sem.at[pi]).start()
-    last8 = pl.ds(64, 8)
+    last8 = pl.ds(64, 1)
     notice = [
         pltpu.make_async_copy(src.at[:, last8, :], notes.at[i], sem_o.at[i]) for i, src in enumerate((pos_a, pos_b))
     ]
@@ -503,13 +498,12 @@
     def tile_of(sid):
         return notes[sid >> 7, (sid & 127) >> 3, 0, sid & 7]
 
-    def scan(s, cnt):
-        for k in range(8):
-            t = notes[s >> 4, s & 15, 0, k]
-            lst[cnt] = 8 * s + k
-            mine = jnp.logical_and(t > 0, (((t - 1) >> 1) & 1) == core)
-            cnt = cnt + mine.astype(jnp.int32)
-        return cnt
+    def scan(g, cnt):
+        def one(i, cnt):
+            lst[cnt] = 8 * g + notes[g >> 4, g & 15, 0, 16 + 8 * core + i]
+            return cnt + 1
+
+        return lax.fori_loop(0, notes[g >> 4, g & 15, 0, 8 + core], one, cnt)
 
     lst[0] = 0
     count = lax.fori_loop(0, 32, scan, jnp.int32(0))
@@ -618,14 +612,14 @@
         return carry
 
     lax.fori_loop(0, (count + 3) >> 2, four, 0)
-    moves = [
-        pltpu.make_async_copy(res.at[pl.ds(0, 128)], out_a, sem_o.at[0]),
-        pltpu.make_async_copy(res.at[pl.ds(128, 128)], out_b, sem_o.at[1]),
-    ]
-    for m in moves:
-        m.start()
-    for m in moves:
-        m.wait()
+
+    def hand_over(i, carry):
+        r8 = pl.ds(pl.multiple_of(8 * i, 8), 8)
+        out_a[r8] = res[r8]
+        out_b[r8] = res[pl.ds(pl.multiple_of(128 + 8 * i, 8), 8)]
+        return carry
+
+    lax.fori_loop(0, 16, hand_over, 0)
 
 
 def along_x(plans, kt, e2, pos_a, pos_b, parts):
@@ -639,7 +633,7 @@
         functools.partial(along_x_kernel, plans),
         out_shape=[jax.ShapeDtypeStruct((128, 8, 128), F32)] * 2,
         in_specs=[VMEM] + [HBM] * (5 + len(parts)),
-        out_specs=[HBM, HBM],
+        out_specs=[VMEM, VMEM],
         scratch_shapes=[
             pltpu.VMEM((4, 256, 256), BF16),
             pltpu.VMEM((4, 256, 256), BF16),
@@ -656,7 +650,7 @@
             pltpu.VMEM((256, 8, 128), F32),
             pltpu.VMEM((8, 128), F32),
             pltpu.SMEM((272,), jnp.int32),
-            pltpu.SMEM((2, 16, 8, 128), jnp.int32),
+            pltpu.SMEM((2, 16, 1, 128), jnp.int32),
             pltpu.SemaphoreType.DMA((2,)),
             pltpu.SemaphoreType.DMA((5,)),
             pltpu.SemaphoreType.DMA((2,)),
@@ -667,7 +661,7 @@
     )(kt, *e2, pos_a, pos_b, *parts)
 
 
-def arrange_kernel(mine, got, payload, here, there, blocks, notes, sem):
+def arrange_kernel(mine, got, payload, blocks, notes, counts, sem):
     zh = lax.axis_index("zh")
     copies = []
     for i, src in enumerate((mine, got)):
@@ -678,18 +672,24 @@
     for c in copies:
         c.wait()
     payload[:, 64:72, :] = jnp.zeros((16, 8, 128), jnp.int32)
+    for i in range(32):
+        counts[i] = 0
     lane = lax.broadcasted_iota(jnp.int32, (8, 128), 1)
-    for i, (out, home) in enumerate(((here, zh), (there, 1 - zh))):
-        def one(b, carry, i=i, out=out, home=home):
+    for i, home in enumerate((zh, 1 - zh)):
+        def one(b, carry, i=i, home=home):
             slot, tile = notes[i, 0, b], notes[i, 1, b]
             mine = (slot >> 6) == zh
             chip, k = (slot >> 2) & 15, 4 * home + (slot & 3)
-            out[b] = jnp.where(mine, 8 * chip + k, -1)
 
             @pl.when(mine)
             def _():
                 payload[chip, pl.ds(pl.multiple_of(8 * k, 8), 8), :] = blocks[i, b]
-                payload[chip, 64:72, :] = jnp.where(lane == k, tile, payload[chip, 64:72, :])
+                side = ((tile - 1) >> 1) & 1
+                n = counts[2 * chip + side]
+                counts[2 * chip + side] = n + 1
+                row = jnp.where(lane == k, tile, payload[chip, 64:72, :])
+                row = jnp.where(lane == 8 + side, n + 1, row)
+                payload[chip, 64:72, :] = jnp.where(lane == 16 + 8 * side + n, k, row)
 
             return carry
 
@@ -700,12 +700,13 @@
     i32 = jnp.int32
     return pl.pallas_call(
         arrange_kernel,
-        out_shape=[jax.ShapeDtypeStruct((16, 72, 128), i32)] + [jax.ShapeDtypeStruct((16,), i32)] * 2,
+        out_shape=jax.ShapeDtypeStruct((16, 72, 128), i32),
         in_specs=[HBM, HBM],
-        out_specs=[VMEM, SMEM, SMEM],
+        out_specs=VMEM,
         scratch_shapes=[
             pltpu.VMEM((2, 16, 8, 128), i32),
             pltpu.SMEM((2, 8, 128), i32),
+            pltpu.SMEM((32,), i32),
             pltpu.SemaphoreType.DMA((4,)),
         ],
         compiler_params=pltpu.CompilerParams(vmem_limit_bytes=8 << 20),
@@ -750,11 +751,10 @@
     mine0 = jnp.concatenate([positions.reshape(16, 8, 128), notes[None]], axis=0)
     got0 = lax.ppermute(mine0, "zh", swap)
 
-    own0, ab, pa, pb = turn(0, sky)
+    own0, ab = turn(0, sky)
     zl = shift(ab, z_axes, 8, 1)
     zr = shift(ab, z_axes, 8, -1)
-    za = shift(pa, z_axes, 8, 2)
-    zb = shift(pb, z_axes, 8, -2)
+    zf = shift(ab, z_axes, 8, 2)
     lo, hi = turn(1, sky)
     cl_lo = shift(lo, z_axes, 8, 1)
     cr_hi = shift(hi, z_axes, 8, -1)
@@ -763,7 +763,7 @@
     cf_lo = shift(cl_lo, z_axes, 8, 1)
     cf_hi = shift(cr_hi, z_axes, 8, -1)
 
-    mine_a, mine_b = gather3(zl, zr, za, zb)
+    mine_a, mine_b = gather3(zl, zr, zf)
 
     def three(x, axis):
         l = shift(x, axis, 4, 1)
@@ -775,7 +775,13 @@
     ar, af, al = three(a0, "y")
     br, bf, bl = three(b0, "x")
 
-    payload, here, there = arrange(mine0, got0)
+    payload = arrange(mine0, got0)
+
+    def place(sl, home):
+        return jnp.where((sl >> 6) == zh, ((sl >> 2) & 15) * 8 + 4 * home + (sl & 3), -1)
+
+    zh = lax.axis_index("zh")
+    here, there = place(slot, zh), place(got0[16, 0, :16], 1 - zh)
     asked = lax.all_to_all(payload, ("x", "y"), split_axis=0, concat_axis=0, tiled=True)
     asked_b = lax.ppermute(asked, "core", swap)
     other_w = lax.ppermute(plane_w, "core", swap)

time: 246 us -> 248 us (level)
    ppermute x22 -> x21, starting transfers between devices: 34.1 us -> 30.6 us  [shift(): return lax.ppermute(x, axes, [(i, (i + by) % size) for i in range(size)])]
    ppermute x22 -> x21, waiting for transfers between devices: 69.4 us -> 71.9 us  [shift(): return lax.ppermute(x, axes, [(i, (i + by) % size) for i in range(size)])]
  transfers between devices with their start and end apart: 33 -> 32, of which waited for: 13 -> 13; matrix products, arithmetic and copies ran while one was open for 0% -> 1% of each run, Pallas kernels for 24% -> 24%
where the time goes in v4:
time: 248 us; the launch traced here: 244 us
  waiting for transfers between devices  87.1 us (35%)
  Pallas kernels  80.6 us (32%)
  starting transfers between devices  70.8 us (29%)
  other arithmetic  3.48 us (1%)
    ppermute x21, waiting for transfers between devices, shift(): return lax.ppermute(x, axes, [(i, (i + by) % size) for i in range(size)])  71.9 us
    pallas_call x4, Pallas kernels, along_y(): pl.pallas_call(functools.partial(along_y_kernel, plan, len(srcs)), out_sh...  46.3 us
    ppermute x21, starting transfers between devices, shift(): return lax.ppermute(x, axes, [(i, (i + by) % size) for i in range(size)])  30.6 us
    pallas_call x1, Pallas kernels, along_x(): pl.pallas_call(functools.partial(along_x_kernel, plans), out_shape=[jax.S...  16.8 us
    ppermute x1, starting transfers between devices, shards(): got = lax.ppermute(other, 'zh', swap)  10.6 us
    pallas_call x2, Pallas kernels, turn(): pl.pallas_call(functools.partial(turn_kernel, b), in_specs=[HBM], out_spe...  9.59 us
    all_to_all x1, waiting for transfers between devices, shards(): lax.all_to_all(merged.reshape(16, 64, 128), ('x', 'y'), split_axis=0, con...  9.57 us
    all_to_all x1, starting transfers between devices, shards(): lax.all_to_all(merged.reshape(16, 64, 128), ('x', 'y'), split_axis=0, con...  9.22 us
  transfers between devices with their start and end apart: 32, of which 13 were waited for; matrix products, arithmetic and copies ran while one was open for 1% of the time, Pallas kernels for 24%

profile of v4, /device:TPU:1, one launch (start us, length us, event | category | flops | bytes accessed | tf_op | source)
XLA Modules:
  0.0 243.8 jit_solution(10187989384994133873)
XLA Ops:
  0.0 4.8 %shard_map.73 = (f32[16,128,256]{2,1,0:T(8,128)}, f32[2,4,16,256]{3,2,1,0:T(8,128)}) custom-call(f32[2,2048,512]{2,1,0:T(8,128)} %sky.3), custom_call_target="tpu_custom_call" | custom-call | flops 4194304 | bytes 4194304 | tf_op jit(solution)/shard_map/pallas_call | solution.py:164
  4.8 0.0 copy-start
  4.9 0.0 copy-start.2
  4.9 2.5 %collective-permute-start.4 = (f32[2,4,16,256]{3,2,1,0:T(8,128)}, f32[2,4,16,256]{3,2,1,0:T(8,128)S(1)}, u32[]{:S(2)}, u32[]{:S(2)}) collective-permute-start(f32[2,4,16,256]{3,2,1,0:T(8,128)} %get-tuple-element.42), channel_id=1, source_target_pairs={{0,1},{1,2},{2,3},{3,128},{128,129},{129,130},{130,131},{131,0},{4... | collective-permute-start | bytes 393224 | tf_op jit(solution)/shard_map/ppermute | solution.py:739
  7.4 4.8 %shard_map.75 = (f32[8,128,256]{2,1,0:T(8,128)}, f32[8,128,256]{2,1,0:T(8,128)}) custom-call(f32[2,2048,512]{2,1,0:T(8,128)} %sky.3), custom_call_target="tpu_custom_call" | custom-call | flops 4194304 | bytes 4194304 | tf_op jit(solution)/shard_map/pallas_call | solution.py:164
  12.2 0.0 copy-start.8
  12.2 1.7 collective-permute-start.14
  13.9 1.6 collective-permute-start.15
  15.5 1.0 collective-permute-start.16
  16.6 1.3 collective-permute-start.5
  17.9 1.8 collective-permute-start.6
  19.7 23.9 %collective-permute-done.5.zr = f32[2,4,16,256]{3,2,1,0:T(8,128)S(1)} collective-permute-done((f32[2,4,16,256]{3,2,1,0:T(8,128)S(1)}, f32[2,4,16,256]{3,2,1,0:T(8,128)S(1)}, u32[]{:S(2)}, u32[]{:S(2)}) %collective-permute-start.5) | collective-permute-done | bytes 131104 | tf_op jit(solution)/shard_map/ppermute | solution.py:739
  43.5 22.9 %collective-permute-done.6.zf = f32[2,4,16,256]{3,2,1,0:T(8,128)S(1)} collective-permute-done((f32[2,4,16,256]{3,2,1,0:T(8,128)S(1)}, f32[2,4,16,256]{3,2,1,0:T(8,128)S(1)}, u32[]{:S(2)}, u32[]{:S(2)}) %collective-permute-start.6) | collective-permute-done | bytes 131104 | tf_op jit(solution)/shard_map/ppermute | solution.py:739
  66.4 2.6 %collective-permute-start.7 = (f32[4,48,256]{2,1,0:T(8,128)S(1)}, f32[4,48,256]{2,1,0:T(8,128)S(1)}, u32[]{:S(2)}, u32[]{:S(2)}) collective-permute-start(f32[4,48,256]{2,1,0:T(8,128)S(1)} %get-tuple-element.43.refs_0_), channel_id=1, source_target_pairs={{0,96},{32,0},{64,32},{96,64},{1,97},{33,1},{65,33},{97,65},{2,98}... | collective-permute-start | bytes 589832 | tf_op jit(solution)/shard_map/ppermute | solution.py:739
  69.0 0.5 collective-permute-start.8
  69.5 4.4 %collective-permute-done.7.refs_1_ = f32[4,48,256]{2,1,0:T(8,128)S(1)} collective-permute-done((f32[4,48,256]{2,1,0:T(8,128)S(1)}, f32[4,48,256]{2,1,0:T(8,128)S(1)}, u32[]{:S(2)}, u32[]{:S(2)}) %collective-permute-start.7) | collective-permute-done | bytes 196640 | tf_op jit(solution)/shard_map/ppermute | solution.py:739
  73.9 1.1 collective-permute-done.8.refs_2_
  75.0 2.7 %collective-permute-start.10 = (f32[4,48,256]{2,1,0:T(8,128)S(1)}, f32[4,48,256]{2,1,0:T(8,128)S(1)}, u32[]{:S(2)}, u32[]{:S(2)}) collective-permute-start(f32[4,48,256]{2,1,0:T(8,128)S(1)} %get-tuple-element.44.refs_4_), channel_id=1, source_target_pairs={{0,24},{8,0},{16,8},{24,16},{1,25},{9,1},{17,9},{25,17},{2,26},{10... | collective-permute-start | bytes 589832 | tf_op jit(solution)/shard_map/ppermute | solution.py:739
  77.7 3.0 %collective-permute-done.9.refs_3_ = f32[4,48,256]{2,1,0:T(8,128)S(1)} collective-permute-done((f32[4,48,256]{2,1,0:T(8,128)S(1)}, f32[4,48,256]{2,1,0:T(8,128)S(1)}, u32[]{:S(2)}, u32[]{:S(2)}) %collective-permute-start.9) | collective-permute-done | bytes 196640 | tf_op jit(solution)/shard_map/ppermute | solution.py:739
  80.8 2.9 %collective-permute-start.11 = (f32[4,48,256]{2,1,0:T(8,128)S(1)}, f32[4,48,256]{2,1,0:T(8,128)S(1)}, u32[]{:S(2)}, u32[]{:S(2)}) collective-permute-start(f32[4,48,256]{2,1,0:T(8,128)S(1)} %get-tuple-element.44.refs_4_), channel_id=1, source_target_pairs={{0,16},{8,24},{16,0},{24,8},{1,17},{9,25},{17,1},{25,9},{2,18},{10... | collective-permute-start | bytes 589832 | tf_op jit(solution)/shard_map/ppermute | solution.py:739
  83.7 1.9 collective-permute-start.17
  85.6 0.1 reshape.49
  86.3 3.6 %tables.1 = (bf16[4,256,256]{2,1,0:T(8,128)(2,1)}, bf16[4,256,256]{2,1,0:T(8,128)(2,1)}, bf16[4,256,256]{2,1,0:T(8,128)(2,1)}, bf16[4,256,256]{2,1,0:T(8,128)(2,...) custom-call(), custom_call_target="tpu_custom_call" | custom-call | flops 31457280 | bytes 4194304 | tf_op jit(solution)/shard_map/tables/pallas_call | solution.py:105
  89.9 0.4 collective-permute-start.12
  90.3 0.2 select_reduce_fusion
  90.5 5.1 %collective-permute-done.12.refs_7_ = f32[4,48,256]{2,1,0:T(8,128)S(1)} collective-permute-done((f32[4,48,256]{2,1,0:T(8,128)S(1)}, f32[4,48,256]{2,1,0:T(8,128)S(1)}, u32[]{:S(2)}, u32[]{:S(2)}) %collective-permute-start.12) | collective-permute-done | bytes 196640 | tf_op jit(solution)/shard_map/ppermute | solution.py:739
  95.7 6.4 %collective-permute-start.2 = (f32[1]{0:T(128)}, f32[1]{0:T(128)}, u32[]{:S(2)}, u32[]{:S(2)}) collective-permute-start(f32[1]{0:T(128)} %param.8), channel_id=1, source_target_pairs={{0,4},{4,0},{1,5},{5,1},{2,6},{6,2},{3,7},{7,3},{8,12},{12,8},{9,1... | collective-permute-start | bytes 20 | tf_op jit(solution)/shard_map/ppermute | solution.py:787
  102.1 1.3 join.1
  103.4 2.7 %collective-permute-start.19 = (f32[16,48,256]{2,1,0:T(8,128)}, f32[16,48,256]{2,1,0:T(8,128)}, u32[]{:S(2)}, u32[]{:S(2)}) collective-permute-start(f32[16,48,256]{2,1,0:T(8,128)} %get-tuple-element.45.rest_2_), channel_id=1, source_target_pairs={{0,24},{8,0},{16,8},{24,16},{1,25},{9,1},{17,9},{25,17},{2,26},{10... | collective-permute-start | bytes 2359304 | tf_op jit(solution)/shard_map/ppermute | solution.py:739
  106.1 2.0 collective-permute-start.20
  108.1 0.7 collective-permute-start.21
  108.8 0.6 pad_add_fusion.mine
  109.4 3.7 %collective-permute-start = (s32[17,8,128]{2,1,0:T(8,128)}, s32[17,8,128]{2,1,0:T(8,128)}, u32[]{:S(2)}, u32[]{:S(2)}) collective-permute-start(s32[17,8,128]{2,1,0:T(8,128)} %pad_add_fusion.mine), channel_id=1, source_target_pairs={{0,128},{128,0},{1,129},{129,1},{2,130},{130,2},{3,131},{131,3},{4... | collective-permute-start | bytes 208904 | tf_op jit(solution)/shard_map/ppermute | solution.py:752
  113.2 10.8 %collective-permute-done.18.rest_4_ = f32[16,48,256]{2,1,0:T(8,128)} collective-permute-done((f32[16,48,256]{2,1,0:T(8,128)}, f32[16,48,256]{2,1,0:T(8,128)}, u32[]{:S(2)}, u32[]{:S(2)}) %collective-permute-start.18) | collective-permute-done | bytes 786464 | tf_op jit(solution)/shard_map/ppermute | solution.py:739
  124.0 2.0 collective-permute-start.26
  126.0 0.1 collective-permute-done.20.rest_6_
  126.1 0.5 collective-permute-done.21.rest_7_
  126.7 2.2 collective-permute-start.24
  128.8 17.7 %shard_map.77 = (f32[2,2,56,8,256]{4,3,2,1,0:T(8,128)}, f32[2,2,56,8,256]{4,3,2,1,0:T(8,128)}) custom-call(f32[1]{0:T(128)S(6)} %copy.8.w_own, f32[1]{0:T(128)} %collective-permute-done.2.w_other, bf16[4,256,256]{2,1,0:T(8,128)(2,1)} %get-tuple-element.34.e1h, bf16[4,256,256]{2,1,0:T(8,128)(2,1)} %get-tuple-element.35.e1l, ...), custom_call_target="tpu_custom_call" | custom-call | flops 5637144576 | bytes 11010048 | tf_op jit(solution)/shard_map/pallas_call | solution.py:413
  146.5 2.1 collective-permute-start.22
  148.6 2.4 arrange.1
  151.0 6.4 %all-to-all-start = ((s32[16,72,128]{2,1,0:T(8,128)}), s32[16,72,128]{2,1,0:T(8,128)}, u32[]{:S(2)}, u32[]{:S(2)}) async-start(s32[16,72,128]{2,1,0:T(8,128)} %arrange.1), calls=%async_computation | async-start | bytes 1179648 | tf_op jit(solution)/shard_map/all_to_all | solution.py:785
  157.4 10.7 %shard_map.76 = (f32[2,2,28,8,256]{4,3,2,1,0:T(8,128)}, f32[2,2,28,8,256]{4,3,2,1,0:T(8,128)}) custom-call(f32[1]{0:T(128)S(6)} %copy.8.w_own, f32[1]{0:T(128)} %collective-permute-done.2.w_other, bf16[4,256,256]{2,1,0:T(8,128)(2,1)} %get-tuple-element.34.e1h, bf16[4,256,256]{2,1,0:T(8,128)(2,1)} %get-tuple-element.35.e1l, ...), custom_call_target="tpu_custom_call" | custom-call | flops 2818572288 | bytes 5505024 | tf_op jit(solution)/shard_map/pallas_call | solution.py:413
  168.1 0.6 collective-permute-start.13
  168.7 10.7 %shard_map.78 = (f32[2,2,28,8,256]{4,3,2,1,0:T(8,128)}, f32[2,2,28,8,256]{4,3,2,1,0:T(8,128)}) custom-call(f32[1]{0:T(128)S(6)} %copy.8.w_own, f32[1]{0:T(128)} %collective-permute-done.2.w_other, bf16[4,256,256]{2,1,0:T(8,128)(2,1)} %get-tuple-element.34.e1h, bf16[4,256,256]{2,1,0:T(8,128)(2,1)} %get-tuple-element.35.e1l, ...), custom_call_target="tpu_custom_call" | custom-call | flops 2818572288 | bytes 5505024 | tf_op jit(solution)/shard_map/pallas_call | solution.py:413
  179.3 0.3 collective-permute-start.27
  179.7 0.3 collective-permute-start.1
  179.9 7.3 %shard_map.74 = (f32[2,2,16,8,256]{4,3,2,1,0:T(8,128)}, f32[2,2,16,8,256]{4,3,2,1,0:T(8,128)}) custom-call(f32[1]{0:T(128)S(6)} %copy.8.w_own, f32[1]{0:T(128)} %collective-permute-done.2.w_other, bf16[4,256,256]{2,1,0:T(8,128)(2,1)} %get-tuple-element.34.e1h, bf16[4,256,256]{2,1,0:T(8,128)(2,1)} %get-tuple-element.35.e1l, ...), custom_call_target="tpu_custom_call" | custom-call | flops 1610612736 | bytes 3145728 | tf_op jit(solution)/shard_map/pallas_call | solution.py:413
  187.2 0.3 collective-permute-start.3
  187.6 2.0 collective-permute-done.3.rest_1_
  189.6 16.8 %along_x.1 = (f32[128,8,128]{2,1,0:T(8,128)}, f32[128,8,128]{2,1,0:T(8,128)}) custom-call(f32[8,16]{1,0:T(8,128)} %bitcast.17, bf16[4,256,256]{2,1,0:T(8,128)(2,1)} %get-tuple-element.31.e2h, bf16[4,256,256]{2,1,0:T(8,128)(2,1)} %get-tuple-element.32.e2l, f32[2,12,128,128]{3,2,1,0:T(8,128)} %get-tuple-element.33.tw2, s32[16,72,128]{2,1,0:T(8,128)} %all-to-all-done.pos_a, ...), custom_call_target="tpu_custom_call" | custom-call | flops 60000002048 | bytes 16777216 | tf_op jit(solution)/shard_map/along_x/pallas_call | solution.py:632
  206.4 0.0 copy-start.1
  206.4 0.0 copy-start.3
  206.5 0.3 collective-permute-start.28
  206.8 1.9 collective-permute-done.28
  208.7 1.9 add.62
  210.6 9.2 %all-to-all-start.1 = ((f32[16,64,128]{2,1,0:T(8,128)}), f32[16,64,128]{2,1,0:T(8,128)S(1)}, u32[]{:S(2)}, u32[]{:S(2)}) async-start(f32[16,64,128]{2,1,0:T(8,128)} %bitcast.7), calls=%async_computation.1 | async-start | bytes 1048576 | tf_op jit(solution)/shard_map/all_to_all | solution.py:819
  219.8 0.1 reshape.52.observed
  219.9 0.7 fusion.there
  220.6 9.6 %all-to-all-done.1 = f32[16,64,128]{2,1,0:T(8,128)S(1)} async-done(((f32[16,64,128]{2,1,0:T(8,128)}), f32[16,64,128]{2,1,0:T(8,128)S(1)}, u32[]{:S(2)}, u32[]{:S(2)}) %all-to-all-start.1) | async-done | bytes 524320 | tf_op jit(solution)/shard_map/all_to_all | solution.py:819
  230.2 0.6 pick.1
  230.8 10.6 %collective-permute-start.29 = (f32[16,8,128]{2,1,0:T(8,128)S(1)}, f32[16,8,128]{2,1,0:T(8,128)S(1)}, u32[]{:S(2)}, u32[]{:S(2)}) collective-permute-start(f32[16,8,128]{2,1,0:T(8,128)S(1)} %get-tuple-element.56), channel_id=1, source_target_pairs={{0,128},{128,0},{1,129},{129,1},{2,130},{130,2},{3,131},{131,3},{4... | collective-permute-start | bytes 196616 | tf_op jit(solution)/shard_map/ppermute | solution.py:821
  241.4 1.7 collective-permute-done.29
  243.1 0.7 reshape.53
  (44 shorter events, 0.2 us)
Async XLA Ops:
  4.8 11.7 %copy-start.7 = (f32[2,4,16,256]{3,2,1,0:T(8,128)S(1)}, f32[2,4,16,256]{3,2,1,0:T(8,128)}, u32[]{:S(2)}) copy-start(f32[2,4,16,256]{3,2,1,0:T(8,128)} %get-tuple-element.42) | copy-start | bytes 393220
  4.8 80.8 %copy-start = (s32[16,2,512]{2,1,0:T(2,128)S(1)}, s32[16,2,512]{2,1,0:T(2,128)}, u32[]{:S(2)}) copy-start(s32[16,2,512]{2,1,0:T(2,128)} %param.12) | copy-start | bytes 196612
  4.9 85.5 %copy-start.2 = (s32[16,1]{0,1:T(1,128)S(1)}, s32[16,1]{0,1:T(1,128)}, u32[]{:S(2)}) copy-start(s32[16,1]{0,1:T(1,128)} %param.11) | copy-start | bytes 196
  4.9 13.0 %collective-permute-start.4 = (f32[2,4,16,256]{3,2,1,0:T(8,128)}, f32[2,4,16,256]{3,2,1,0:T(8,128)S(1)}, u32[]{:S(2)}, u32[]{:S(2)}) collective-permute-start(f32[2,4,16,256]{3,2,1,0:T(8,128)} %get-tuple-element.42), channel_id=1, source_target_pairs={{0,1},{1,2},{2,3},{3,128},{128,129},{129,130},{130,131},{131,0},{4... | collective-permute-start | bytes 393224 | tf_op jit(solution)/shard_map/ppermute | solution.py:739
  12.2 96.6 %copy-start.8 = (s32[16]{0:T(128)S(1)}, s32[16]{0:T(128)}, u32[]{:S(2)}) copy-start(s32[16]{0:T(128)} %param.10) | copy-start | bytes 196
  12.2 91.2 %collective-permute-start.14 = (f32[8,128,256]{2,1,0:T(8,128)}, f32[8,128,256]{2,1,0:T(8,128)}, u32[]{:S(2)}, u32[]{:S(2)}) collective-permute-start(f32[8,128,256]{2,1,0:T(8,128)} %get-tuple-element.40.rest_0_), channel_id=1, source_target_pairs={{0,1},{1,2},{2,3},{3,128},{128,129},{129,130},{130,131},{131,0},{4... | collective-permute-start | bytes 3145736 | tf_op jit(solution)/shard_map/ppermute | solution.py:739
  13.9 92.2 %collective-permute-start.15 = (f32[8,128,256]{2,1,0:T(8,128)}, f32[8,128,256]{2,1,0:T(8,128)S(1)}, u32[]{:S(2)}, u32[]{:S(2)}) collective-permute-start(f32[8,128,256]{2,1,0:T(8,128)} %get-tuple-element.41.rest_1_), channel_id=1, source_target_pairs={{0,1},{1,2},{2,3},{3,128},{128,129},{129,130},{130,131},{131,0},{4... | collective-permute-start | bytes 3145736 | tf_op jit(solution)/shard_map/ppermute | solution.py:739
  15.5 92.5 %collective-permute-start.16 = (f32[8,128,256]{2,1,0:T(8,128)}, f32[8,128,256]{2,1,0:T(8,128)}, u32[]{:S(2)}, u32[]{:S(2)}) collective-permute-start(f32[8,128,256]{2,1,0:T(8,128)} %get-tuple-element.40.rest_0_), channel_id=1, source_target_pairs={{0,131},{1,0},{2,1},{3,2},{128,3},{129,128},{130,129},{131,130},{4... | collective-permute-start | bytes 3145736 | tf_op jit(solution)/shard_map/ppermute | solution.py:739
  16.6 26.9 %collective-permute-start.5 = (f32[2,4,16,256]{3,2,1,0:T(8,128)S(1)}, f32[2,4,16,256]{3,2,1,0:T(8,128)S(1)}, u32[]{:S(2)}, u32[]{:S(2)}) collective-permute-start(f32[2,4,16,256]{3,2,1,0:T(8,128)S(1)} %copy-done.7), channel_id=1, source_target_pairs={{0,131},{1,0},{2,1},{3,2},{128,3},{129,128},{130,129},{131,130},{4... | collective-permute-start | bytes 393224 | tf_op jit(solution)/shard_map/ppermute | solution.py:739
  17.9 48.5 %collective-permute-start.6 = (f32[2,4,16,256]{3,2,1,0:T(8,128)S(1)}, f32[2,4,16,256]{3,2,1,0:T(8,128)S(1)}, u32[]{:S(2)}, u32[]{:S(2)}) collective-permute-start(f32[2,4,16,256]{3,2,1,0:T(8,128)S(1)} %copy-done.7), channel_id=1, source_target_pairs={{0,2},{1,3},{2,128},{3,129},{128,130},{129,131},{130,0},{131,1},{4... | collective-permute-start | bytes 393224 | tf_op jit(solution)/shard_map/ppermute | solution.py:739
  66.4 7.5 %collective-permute-start.7 = (f32[4,48,256]{2,1,0:T(8,128)S(1)}, f32[4,48,256]{2,1,0:T(8,128)S(1)}, u32[]{:S(2)}, u32[]{:S(2)}) collective-permute-start(f32[4,48,256]{2,1,0:T(8,128)S(1)} %get-tuple-element.43.refs_0_), channel_id=1, source_target_pairs={{0,96},{32,0},{64,32},{96,64},{1,97},{33,1},{65,33},{97,65},{2,98}... | collective-permute-start | bytes 589832 | tf_op jit(solution)/shard_map/ppermute | solution.py:739
  69.0 6.0 %collective-permute-start.8 = (f32[4,48,256]{2,1,0:T(8,128)S(1)}, f32[4,48,256]{2,1,0:T(8,128)S(1)}, u32[]{:S(2)}, u32[]{:S(2)}) collective-permute-start(f32[4,48,256]{2,1,0:T(8,128)S(1)} %get-tuple-element.43.refs_0_), channel_id=1, source_target_pairs={{0,64},{32,96},{64,0},{96,32},{1,65},{33,97},{65,1},{97,33},{2,66}... | collective-permute-start | bytes 589832 | tf_op jit(solution)/shard_map/ppermute | solution.py:739
  73.9 6.9 %collective-permute-start.9 = (f32[4,48,256]{2,1,0:T(8,128)S(1)}, f32[4,48,256]{2,1,0:T(8,128)S(1)}, u32[]{:S(2)}, u32[]{:S(2)}) collective-permute-start(f32[4,48,256]{2,1,0:T(8,128)S(1)} %get-tuple-element.43.refs_0_), channel_id=1, source_target_pairs={{0,32},{32,64},{64,96},{96,0},{1,33},{33,65},{65,97},{97,1},{2,34}... | collective-permute-start | bytes 589832 | tf_op jit(solution)/shard_map/ppermute | solution.py:739
  75.0 8.7 %collective-permute-start.10 = (f32[4,48,256]{2,1,0:T(8,128)S(1)}, f32[4,48,256]{2,1,0:T(8,128)S(1)}, u32[]{:S(2)}, u32[]{:S(2)}) collective-permute-start(f32[4,48,256]{2,1,0:T(8,128)S(1)} %get-tuple-element.44.refs_4_), channel_id=1, source_target_pairs={{0,24},{8,0},{16,8},{24,16},{1,25},{9,1},{17,9},{25,17},{2,26},{10... | collective-permute-start | bytes 589832 | tf_op jit(solution)/shard_map/ppermute | solution.py:739
  80.8 9.2 %collective-permute-start.11 = (f32[4,48,256]{2,1,0:T(8,128)S(1)}, f32[4,48,256]{2,1,0:T(8,128)S(1)}, u32[]{:S(2)}, u32[]{:S(2)}) collective-permute-start(f32[4,48,256]{2,1,0:T(8,128)S(1)} %get-tuple-element.44.refs_4_), channel_id=1, source_target_pairs={{0,16},{8,24},{16,0},{24,8},{1,17},{9,25},{17,1},{25,9},{2,18},{10... | collective-permute-start | bytes 589832 | tf_op jit(solution)/shard_map/ppermute | solution.py:739
  83.7 25.7 %collective-permute-start.17 = (f32[8,128,256]{2,1,0:T(8,128)}, f32[8,128,256]{2,1,0:T(8,128)}, u32[]{:S(2)}, u32[]{:S(2)}) collective-permute-start(f32[8,128,256]{2,1,0:T(8,128)} %get-tuple-element.41.rest_1_), channel_id=1, source_target_pairs={{0,131},{1,0},{2,1},{3,2},{128,3},{129,128},{130,129},{131,130},{4... | collective-permute-start | bytes 3145736 | tf_op jit(solution)/shard_map/ppermute | solution.py:739
  89.9 5.7 %collective-permute-start.12 = (f32[4,48,256]{2,1,0:T(8,128)S(1)}, f32[4,48,256]{2,1,0:T(8,128)S(1)}, u32[]{:S(2)}, u32[]{:S(2)}) collective-permute-start(f32[4,48,256]{2,1,0:T(8,128)S(1)} %get-tuple-element.44.refs_4_), channel_id=1, source_target_pairs={{0,8},{8,16},{16,24},{24,0},{1,9},{9,17},{17,25},{25,1},{2,10},{10... | collective-permute-start | bytes 589832 | tf_op jit(solution)/shard_map/ppermute | solution.py:739
  90.5 18.9 %copy-start.4 = (s32[16]{0:T(128)}, s32[16]{0:T(128)S(1)}, u32[]{:S(2)}) copy-start(s32[16]{0:T(128)S(1)} %select_reduce_fusion) | copy-start | bytes 196
  95.7 7.7 %collective-permute-start.2 = (f32[1]{0:T(128)}, f32[1]{0:T(128)}, u32[]{:S(2)}, u32[]{:S(2)}) collective-permute-start(f32[1]{0:T(128)} %param.8), channel_id=1, source_target_pairs={{0,4},{4,0},{1,5},{5,1},{2,6},{6,2},{3,7},{7,3},{8,12},{12,8},{9,1... | collective-permute-start | bytes 20 | tf_op jit(solution)/shard_map/ppermute | solution.py:787
  103.4 20.6 %collective-permute-start.18 = (f32[16,48,256]{2,1,0:T(8,128)}, f32[16,48,256]{2,1,0:T(8,128)}, u32[]{:S(2)}, u32[]{:S(2)}) collective-permute-start(f32[16,48,256]{2,1,0:T(8,128)} %get-tuple-element.45.rest_2_), channel_id=1, source_target_pairs={{0,8},{8,16},{16,24},{24,0},{1,9},{9,17},{17,25},{25,1},{2,10},{10... | collective-permute-start | bytes 2359304 | tf_op jit(solution)/shard_map/ppermute | solution.py:739
  103.4 20.6 %collective-permute-start.19 = (f32[16,48,256]{2,1,0:T(8,128)}, f32[16,48,256]{2,1,0:T(8,128)}, u32[]{:S(2)}, u32[]{:S(2)}) collective-permute-start(f32[16,48,256]{2,1,0:T(8,128)} %get-tuple-element.45.rest_2_), channel_id=1, source_target_pairs={{0,24},{8,0},{16,8},{24,16},{1,25},{9,1},{17,9},{25,17},{2,26},{10... | collective-permute-start | bytes 2359304 | tf_op jit(solution)/shard_map/ppermute | solution.py:739
  106.1 3.4 %copy-start.6 = (f32[8,128,256]{2,1,0:T(8,128)}, f32[8,128,256]{2,1,0:T(8,128)S(1)}, u32[]{:S(2)}) copy-start(f32[8,128,256]{2,1,0:T(8,128)S(1)} %collective-permute-done.15.rest_1_) | copy-start | bytes 3145732
  106.1 20.1 %collective-permute-start.20 = (f32[16,48,256]{2,1,0:T(8,128)}, f32[16,48,256]{2,1,0:T(8,128)}, u32[]{:S(2)}, u32[]{:S(2)}) collective-permute-start(f32[16,48,256]{2,1,0:T(8,128)} %get-tuple-element.46.rest_3_), channel_id=1, source_target_pairs={{0,32},{32,64},{64,96},{96,0},{1,33},{33,65},{65,97},{97,1},{2,34}... | collective-permute-start | bytes 2359304 | tf_op jit(solution)/shard_map/ppermute | solution.py:739
  108.1 18.6 %collective-permute-start.21 = (f32[16,48,256]{2,1,0:T(8,128)}, f32[16,48,256]{2,1,0:T(8,128)}, u32[]{:S(2)}, u32[]{:S(2)}) collective-permute-start(f32[16,48,256]{2,1,0:T(8,128)} %get-tuple-element.46.rest_3_), channel_id=1, source_target_pairs={{0,96},{32,0},{64,32},{96,64},{1,97},{33,1},{65,33},{97,65},{2,98}... | collective-permute-start | bytes 2359304 | tf_op jit(solution)/shard_map/ppermute | solution.py:739
  109.4 37.1 %collective-permute-start = (s32[17,8,128]{2,1,0:T(8,128)}, s32[17,8,128]{2,1,0:T(8,128)}, u32[]{:S(2)}, u32[]{:S(2)}) collective-permute-start(s32[17,8,128]{2,1,0:T(8,128)} %pad_add_fusion.mine), channel_id=1, source_target_pairs={{0,128},{128,0},{1,129},{129,1},{2,130},{130,2},{3,131},{131,3},{4... | collective-permute-start | bytes 208904 | tf_op jit(solution)/shard_map/ppermute | solution.py:752
  124.0 44.1 %collective-permute-start.25 = (f32[16,48,256]{2,1,0:T(8,128)}, f32[16,48,256]{2,1,0:T(8,128)}, u32[]{:S(2)}, u32[]{:S(2)}) collective-permute-start(f32[16,48,256]{2,1,0:T(8,128)} %get-tuple-element.45.rest_2_), channel_id=1, source_target_pairs={{0,16},{8,24},{16,0},{24,8},{1,17},{9,25},{17,1},{25,9},{2,18},{10... | collective-permute-start | bytes 2359304 | tf_op jit(solution)/shard_map/ppermute | solution.py:739
  124.0 44.6 %collective-permute-start.26 = (f32[16,48,256]{2,1,0:T(8,128)}, f32[16,48,256]{2,1,0:T(8,128)}, u32[]{:S(2)}, u32[]{:S(2)}) collective-permute-start(f32[16,48,256]{2,1,0:T(8,128)} %get-tuple-element.46.rest_3_), channel_id=1, source_target_pairs={{0,64},{32,96},{64,0},{96,32},{1,65},{33,97},{65,1},{97,33},{2,66}... | collective-permute-start | bytes 2359304 | tf_op jit(solution)/shard_map/ppermute | solution.py:739
  126.1 42.5 %collective-permute-start.23 = (f32[8,128,256]{2,1,0:T(8,128)}, f32[8,128,256]{2,1,0:T(8,128)}, u32[]{:S(2)}, u32[]{:S(2)}) collective-permute-start(f32[8,128,256]{2,1,0:T(8,128)} %collective-permute-done.14.rest_0_), channel_id=1, source_target_pairs={{0,1},{1,2},{2,3},{3,128},{128,129},{129,130},{130,131},{131,0},{4... | collective-permute-start | bytes 3145736 | tf_op jit(solution)/shard_map/ppermute | solution.py:739
  126.7 42.0 %collective-permute-start.24 = (f32[8,128,256]{2,1,0:T(8,128)}, f32[8,128,256]{2,1,0:T(8,128)}, u32[]{:S(2)}, u32[]{:S(2)}) collective-permute-start(f32[8,128,256]{2,1,0:T(8,128)} %collective-permute-done.17.rest_3_), channel_id=1, source_target_pairs={{0,131},{1,0},{2,1},{3,2},{128,3},{129,128},{130,129},{131,130},{4... | collective-permute-start | bytes 3145736 | tf_op jit(solution)/shard_map/ppermute | solution.py:739
  146.5 43.1 %collective-permute-start.22 = (f32[2,2,56,8,256]{4,3,2,1,0:T(8,128)}, f32[2,2,56,8,256]{4,3,2,1,0:T(8,128)}, u32[]{:S(2)}, u32[]{:S(2)}) collective-permute-start(f32[2,2,56,8,256]{4,3,2,1,0:T(8,128)} %get-tuple-element.50), channel_id=1, source_target_pairs={{0,4},{4,0},{1,5},{5,1},{2,6},{6,2},{3,7},{7,3},{8,12},{12,8},{9,1... | collective-permute-start | bytes 5505032 | tf_op jit(solution)/shard_map/ppermute | solution.py:796
  151.0 28.7 %all-to-all-start = ((s32[16,72,128]{2,1,0:T(8,128)}), s32[16,72,128]{2,1,0:T(8,128)}, u32[]{:S(2)}, u32[]{:S(2)}) async-start(s32[16,72,128]{2,1,0:T(8,128)} %arrange.1), calls=%async_computation | async-start | bytes 1179648 | tf_op jit(solution)/shard_map/all_to_all | solution.py:785
  168.1 21.5 %collective-permute-start.13 = (f32[2,2,28,8,256]{4,3,2,1,0:T(8,128)}, f32[2,2,28,8,256]{4,3,2,1,0:T(8,128)}, u32[]{:S(2)}, u32[]{:S(2)}) collective-permute-start(f32[2,2,28,8,256]{4,3,2,1,0:T(8,128)} %get-tuple-element.48), channel_id=1, source_target_pairs={{0,4},{4,0},{1,5},{5,1},{2,6},{6,2},{3,7},{7,3},{8,12},{12,8},{9,1... | collective-permute-start | bytes 2752520 | tf_op jit(solution)/shard_map/ppermute | solution.py:796
  179.3 10.3 %collective-permute-start.27 = (f32[2,2,28,8,256]{4,3,2,1,0:T(8,128)}, f32[2,2,28,8,256]{4,3,2,1,0:T(8,128)}, u32[]{:S(2)}, u32[]{:S(2)}) collective-permute-start(f32[2,2,28,8,256]{4,3,2,1,0:T(8,128)} %get-tuple-element.52), channel_id=1, source_target_pairs={{0,4},{4,0},{1,5},{5,1},{2,6},{6,2},{3,7},{7,3},{8,12},{12,8},{9,1... | collective-permute-start | bytes 2752520 | tf_op jit(solution)/shard_map/ppermute | solution.py:796
  179.7 9.9 %collective-permute-start.1 = (s32[16,72,128]{2,1,0:T(8,128)}, s32[16,72,128]{2,1,0:T(8,128)}, u32[]{:S(2)}, u32[]{:S(2)}) collective-permute-start(s32[16,72,128]{2,1,0:T(8,128)} %all-to-all-done.pos_a), channel_id=1, source_target_pairs={{0,4},{4,0},{1,5},{5,1},{2,6},{6,2},{3,7},{7,3},{8,12},{12,8},{9,1... | collective-permute-start | bytes 1769480 | tf_op jit(solution)/shard_map/ppermute | solution.py:786
  187.2 2.3 collective-permute-start.3
  206.4 13.4 %copy-start.1 = (f32[16,2,512]{2,1,0:T(2,128)S(1)}, f32[16,2,512]{2,1,0:T(2,128)}, u32[]{:S(2)}) copy-start(f32[16,2,512]{2,1,0:T(2,128)} %param.13) | copy-start | bytes 196612
  206.4 13.5 %copy-start.3 = (s32[16,1]{0,1:T(1,128)S(1)}, s32[16,1]{0,1:T(1,128)}, u32[]{:S(2)}) copy-start(s32[16,1]{0,1:T(1,128)} %param.11) | copy-start | bytes 196
  206.4 13.5 %copy-start.5 = (s32[16]{0:T(128)S(1)}, s32[16]{0:T(128)}, u32[]{:S(2)}) copy-start(s32[16]{0:T(128)} %copy-done.4) | copy-start | bytes 196
  206.5 2.2 collective-permute-start.28
  210.6 19.6 %all-to-all-start.1 = ((f32[16,64,128]{2,1,0:T(8,128)}), f32[16,64,128]{2,1,0:T(8,128)S(1)}, u32[]{:S(2)}, u32[]{:S(2)}) async-start(f32[16,64,128]{2,1,0:T(8,128)} %bitcast.7), calls=%async_computation.1 | async-start | bytes 1048576 | tf_op jit(solution)/shard_map/all_to_all | solution.py:819
  230.8 12.3 %collective-permute-start.29 = (f32[16,8,128]{2,1,0:T(8,128)S(1)}, f32[16,8,128]{2,1,0:T(8,128)S(1)}, u32[]{:S(2)}, u32[]{:S(2)}) collective-permute-start(f32[16,8,128]{2,1,0:T(8,128)S(1)} %get-tuple-element.56), channel_id=1, source_target_pairs={{0,128},{128,0},{1,129},{129,1},{2,130},{130,2},{3,131},{131,3},{4... | collective-permute-start | bytes 196616 | tf_op jit(solution)/shard_map/ppermute | solution.py:821
